TPU v7x, 32 devices: a whole 2x2x4 slice. The times are simulated.
32 devices in a mesh: dp: 4 (over x, core), fsdp: 8 (over z, y).
Axes of the slice: x: 2, y: 2, z: 4, core: 2. Of those that a mesh axis runs over, the one named last changes fastest.
Arguments:
- tokens: bfloat16 [16384, 768], P(('dp', 'fsdp')), may hold values from -6 to 6
- lengths: int32 [32, 6], P(('dp', 'fsdp')), may hold values from 1 to 128, 256 in all within a row
- norm1_gain: bfloat16 [768], P('fsdp'), may hold values from 0.25 to 1.75
- norm1_bias: bfloat16 [768], P('fsdp'), may hold values from -1.75 to 1.75
- query_weight: bfloat16 [768, 768], P('fsdp'), may hold values from -0.21875 to 0.21875
- key_weight: bfloat16 [768, 768], P('fsdp'), may hold values from -0.21875 to 0.21875
- value_weight: bfloat16 [768, 768], P('fsdp'), may hold values from -0.21875 to 0.21875
- output_weight: bfloat16 [768, 768], P('fsdp'), may hold values from -0.625 to 0.625
- norm2_gain: bfloat16 [768], P('fsdp'), may hold values from 0.25 to 1.75
- norm2_bias: bfloat16 [768], P('fsdp'), may hold values from -1.75 to 1.75
- up_weight: bfloat16 [768, 3072], P('fsdp'), may hold values from -0.21875 to 0.21875
- up_bias: bfloat16 [3072], P('fsdp'), may hold values from -3 to 3
- down_weight: bfloat16 [3072, 768], P('fsdp'), may hold values from -0.109375 to 0.109375
- down_bias: bfloat16 [768], P('fsdp'), may hold values from -1.75 to 1.75
- cotangent: bfloat16 [16384, 768], P(('dp', 'fsdp')), may hold values from -6 to 6
Outputs:
- output: bfloat16 [16384, 768], P(('dp', 'fsdp'))
- input_grad: float32 [16384, 768], P(('dp', 'fsdp'))
- norm1_gain_grad: float32 [768], P('fsdp')
- norm1_bias_grad: float32 [768], P('fsdp')
- query_weight_grad: float32 [768, 768], P('fsdp')
- key_weight_grad: float32 [768, 768], P('fsdp')
- value_weight_grad: float32 [768, 768], P('fsdp')
- output_weight_grad: float32 [768, 768], P('fsdp')
- norm2_gain_grad: float32 [768], P('fsdp')
- norm2_bias_grad: float32 [768], P('fsdp')
- up_weight_grad: float32 [768, 3072], P('fsdp')
- up_bias_grad: float32 [3072], P('fsdp')
- down_weight_grad: float32 [3072, 768], P('fsdp')
- down_bias_grad: float32 [768], P('fsdp')
Inputs may be any that keep to these rules, and one draw needn't show every extreme that they name: Each row of lengths sums to 256, and its largest entry equals 128.
All inputs are finite; a program needn't handle non-finite values.
Results may differ from a plain program's by a relative error of at most 0.012.
Values may be sent and summed in bfloat16 or wider, within the bound.
No kernel may reach another device: no remote copies, remote signals or barrier semaphores. Data moves between devices by JAX's collectives and lax.ppermute only.
A program may use at most 192 MiB of HBM per device.

v0:
```python
from functools import partial
import math

import jax
import jax.numpy as jnp
from jax import lax
from jax.experimental import pallas as pl
from jax.experimental.pallas import tpu as pltpu
from jax.sharding import PartitionSpec as P

H = 12
HD = 64
BLOCK = 16
EPSILON = 1e-05
BASE = 10000.0
NEGATIVE = -1e30
BF = jnp.bfloat16
F32 = jnp.float32
SMALL = 16
SPAN = 4.8e10
VMEM_LIMIT = 56 * 1024 * 1024


def row_layout(length_row, row_count, slot_count):
    doubled = 2 * length_row
    ends_at = jnp.cumsum(doubled, dtype=jnp.int32)
    starts_at = ends_at - doubled
    row_index = jnp.arange(row_count, dtype=jnp.int32)
    member = (row_index[:, None] >= starts_at[None, :]) & (row_index[:, None] < ends_at[None, :])
    slot_ids = jnp.arange(slot_count, dtype=jnp.int32)
    slot_index = jnp.sum(jnp.where(member, slot_ids[None, :], 0), axis=1, dtype=jnp.int32)
    start_row = jnp.sum(jnp.where(member, starts_at[None, :], 0), axis=1, dtype=jnp.int32)
    seq_length = jnp.sum(jnp.where(member, length_row[None, :], 0), axis=1, dtype=jnp.int32)
    local_row = row_index - start_row
    clean_flag = (local_row >= seq_length).astype(jnp.int32)
    position = local_row - clean_flag * seq_length
    return (row_index, slot_index, clean_flag, position)


def allowed_pairs(query_side, key_side, block_size, slot_count):
    query_row, query_slot, query_clean, query_pos = query_side
    key_row, key_slot, key_clean, key_pos = key_side
    query_block = query_pos // block_size
    key_block = key_pos // block_size
    same_seq = query_slot[:, None] == key_slot[None, :]
    key_noisy = key_clean[None, :] == 0
    key_plain = key_clean[None, :] == 1
    noisy_rule = key_noisy & (key_block[None, :] == query_block[:, None]) | key_plain & (
        key_block[None, :] < query_block[:, None]
    )
    clean_rule = key_plain & (key_block[None, :] <= query_block[:, None])
    rule_held = jnp.where(query_clean[:, None] == 1, clean_rule, noisy_rule)
    padded = query_slot == slot_count - 1
    real_pairs = same_seq & rule_held & jnp.logical_not(padded)[:, None]
    self_pairs = padded[:, None] & (query_row[:, None] == key_row[None, :])
    return real_pairs | self_pairs


def rotary_tables(position):
    half = HD // 2
    lane = jnp.arange(2 * HD, dtype=jnp.int32)
    freqs = jnp.exp((lane % half).astype(F32) * (-2.0 * math.log(BASE) / HD))
    angles = position.astype(F32)[:, None] * freqs[None, :]
    sign = jnp.where(lane % HD < half, -1.0, 1.0)
    return jnp.cos(angles), jnp.sin(angles) * sign[None, :]


def swap(values, axis, mask, size):
    return lax.ppermute(values, axis, [(i, i ^ mask) for i in range(size)])


def dot(a, b):
    return jnp.dot(a, b, preferred_element_type=F32)


def dot_nt(a, b):
    return lax.dot_general(a, b, (((1,), (1,)), ((), ())), preferred_element_type=F32)


def dot_tn(a, b):
    return lax.dot_general(a, b, (((0,), (0,)), ((), ())), preferred_element_type=F32)


def params(**more):
    return pltpu.CompilerParams(vmem_limit_bytes=VMEM_LIMIT, **more)


def cost(flops, moved):
    return pl.CostEstimate(flops=int(max(flops, SPAN)), bytes_accessed=int(moved), transcendentals=0)


def norm_parts(values):
    center = values - jnp.mean(values, axis=-1, keepdims=True)
    spread = jnp.mean(center * center, axis=-1, keepdims=True)
    inv = lax.rsqrt(spread + EPSILON)
    return center * inv, inv


def norm_back(grad, unit, inv, gain):
    scaled = grad * gain
    first = jnp.mean(scaled, axis=-1, keepdims=True)
    second = jnp.mean(scaled * unit, axis=-1, keepdims=True)
    return inv * (scaled - first - unit * second)


def turn(values, cosine, sine):
    half = HD // 2
    pair = 2 * HD
    lane = lax.broadcasted_iota(jnp.int32, (1, pair), 1)
    low = (lane % HD) < half
    parts = []
    for at in range(0, values.shape[1], pair):
        part = values[:, at : at + pair]
        other = jnp.where(low, pltpu.roll(part, pair - half, 1), pltpu.roll(part, half, 1))
        parts.append(part * cosine + other * sine)
    return parts[0] if len(parts) == 1 else jnp.concatenate(parts, axis=1)


def bits_of(index, masks):
    total = 0
    for bit, mask in enumerate(masks):
        if (index >> bit) & 1:
            total |= mask
    return total


def piece_map(which, masks):
    count = 1 << len(masks)
    half = count // 2
    kind, r, y = which
    if kind == "a":
        return [((i,), r, bits_of(i, masks), 0) for i in range(count)]
    return [
        ((x * half + i,), r | (2 * x), bits_of(i, masks) | y, 1)
        for x in range(2)
        for i in range(half)
    ]


def fetch(pieces, maps, me_f, h, w_ref, slot_of, sems):
    for ref, entries in zip(pieces, maps):
        for at, r, k, colour in entries:
            slot = slot_of(r)
            pltpu.make_async_copy(
                ref.at[at],
                w_ref.at[slot, me_f ^ k, pl.ds(colour * h, h)],
                sems.at[slot],
            ).start()


def fetched(w_ref, slot, sems):
    pltpu.make_async_copy(w_ref.at[slot], w_ref.at[slot], sems.at[slot]).wait()


def qkv_kernel(
    maps, h, idx_ref, x_ref, small_ref, cos_ref, sin_ref, p0, p1, p2, p3, p4, p5, p6, p7,
    normed_ref, out_ref, w_out, keep, w_ref, sems, out_sems,
):
    g = pl.program_id(0)
    d4, me_f = idx_ref[0], idx_ref[1]
    d = keep.shape[1]

    def send(slot):
        return pltpu.make_async_copy(w_ref.at[slot], w_out.at[slot], out_sems.at[slot])

    @pl.when(g == 0)
    def _():
        fetch((p0, p1, p2, p3, p4, p5, p6, p7), maps, me_f, h, w_ref, lambda r: d4 ^ r, sems)
        unit, _ = norm_parts(x_ref[...].astype(F32))
        normed = (unit * small_ref[0:1, :] + small_ref[1:2, :]).astype(BF)
        keep[...] = normed
        normed_ref[...] = normed

    fetched(w_ref, g, sems)
    send(g).start()

    @pl.when(g == 2)
    def _():
        fetched(w_ref, 3, sems)
        send(3).start()

    product = dot(keep[...], w_ref[g].reshape(d, d))

    @pl.when(g < 2)
    def _():
        out_ref[0] = turn(product, cos_ref[...], sin_ref[...]).astype(BF)

    @pl.when(g == 2)
    def _():
        out_ref[0] = product.astype(BF)
        for slot in range(4):
            send(slot).wait()


def qkv(idx, x, small, cosine, sine, pieces, maps, shards, h):
    n, d = x.shape
    return pl.pallas_call(
        partial(qkv_kernel, maps, h),
        grid=(3,),
        out_shape=(
            jax.ShapeDtypeStruct((n, d), BF),
            jax.ShapeDtypeStruct((3, n, d), BF),
            jax.ShapeDtypeStruct((4, shards, 2 * h, d), BF),
        ),
        in_specs=[
            pl.BlockSpec(memory_space=pltpu.SMEM),
            pl.BlockSpec((n, d), lambda g: (0, 0)),
            pl.BlockSpec(small.shape, lambda g: (0, 0)),
            pl.BlockSpec(cosine.shape, lambda g: (0, 0)),
            pl.BlockSpec(sine.shape, lambda g: (0, 0)),
        ]
        + [pl.BlockSpec(memory_space=pl.ANY)] * 8,
        out_specs=(
            pl.BlockSpec((n, d), lambda g: (0, 0)),
            pl.BlockSpec((1, n, d), lambda g: (g, 0, 0)),
            pl.BlockSpec(memory_space=pl.ANY),
        ),
        scratch_shapes=[
            pltpu.VMEM((n, d), BF),
            pltpu.VMEM((4, shards, 2 * h, d), BF),
            pltpu.SemaphoreType.DMA((4,)),
            pltpu.SemaphoreType.DMA((4,)),
        ],
        compiler_params=params(),
        cost_estimate=cost(6 * n * d * d, 2 * (5 * n * d + 8 * d * d)),
        name="qkv",
    )(idx, x, small, cosine, sine, *pieces)


def head_mask(which):
    lane = lax.broadcasted_iota(jnp.int32, (1, 2 * HD), 1)
    return (lane < HD) if which == 0 else (lane >= HD)


def attend_kernel(q_ref, k_ref, v_ref, bias_ref, mixed_ref, probs_ref):
    q, k, v = q_ref[0], k_ref[0], v_ref[0]
    zero = jnp.zeros((), BF)
    parts = []
    for h in range(2):
        own = jnp.where(head_mask(h), q, zero)
        scores = dot_nt(own, k) * (HD**-0.5) + bias_ref[...]
        top = jnp.max(scores, axis=1, keepdims=True)
        raised = jnp.exp(scores - top)
        total = jnp.sum(raised, axis=1, keepdims=True)
        probs = (raised * (1.0 / total)).astype(BF)
        probs_ref[h] = probs
        parts.append(dot(probs, v))
    mixed_ref[...] = jnp.where(head_mask(0), parts[0], parts[1]).astype(BF)


def attend(three, bias):
    _, n, d = three.shape
    pair = 2 * HD
    return pl.pallas_call(
        attend_kernel,
        grid=(d // pair,),
        out_shape=(
            jax.ShapeDtypeStruct((n, d), BF),
            jax.ShapeDtypeStruct((d // HD, n, n), BF),
        ),
        in_specs=[
            pl.BlockSpec((1, n, pair), lambda p: (0, 0, p)),
            pl.BlockSpec((1, n, pair), lambda p: (1, 0, p)),
            pl.BlockSpec((1, n, pair), lambda p: (2, 0, p)),
            pl.BlockSpec((n, n), lambda p: (0, 0)),
        ],
        out_specs=(
            pl.BlockSpec((n, pair), lambda p: (0, p)),
            pl.BlockSpec((2, n, n), lambda p: (p, 0, 0)),
        ),
        compiler_params=params(),
        cost_estimate=cost(8 * n * n * d, 2 * n * n * (d // HD) + 8 * n * d),
        name="attend",
    )(three, three, three, bias)


def attend_back_kernel(
    q_ref, k_ref, v_ref, probs_ref, grad_ref, mixed_ref, cos_ref, sin_ref, out_ref
):
    q, k, v, grad = q_ref[0], k_ref[0], v_ref[0], grad_ref[...]
    zero = jnp.zeros((), BF)
    product = grad.astype(F32) * mixed_ref[...].astype(F32)
    dq, dk, dv = [], [], []
    for h in range(2):
        mask = head_mask(h)
        inner = jnp.sum(jnp.where(mask, product, 0.0), axis=1, keepdims=True)
        probs = probs_ref[h]
        prob_grad = dot_nt(jnp.where(mask, grad, zero), v)
        score_grad = (probs.astype(F32) * (prob_grad - inner)).astype(BF)
        dq.append(dot(score_grad, k))
        dk.append(dot_tn(score_grad, q))
        dv.append(dot_tn(probs, grad))
    first = head_mask(0)
    scale = HD**-0.5
    cosine, sine = cos_ref[...], sin_ref[...]
    out_ref[0] = turn(jnp.where(first, dq[0], dq[1]) * scale, cosine, -sine).astype(BF)
    out_ref[1] = turn(jnp.where(first, dk[0], dk[1]) * scale, cosine, -sine).astype(BF)
    out_ref[2] = jnp.where(first, dv[0], dv[1]).astype(BF)


def attend_back(three, probs, grad, mixed, cosine, sine):
    _, n, d = three.shape
    pair = 2 * HD
    return pl.pallas_call(
        attend_back_kernel,
        grid=(d // pair,),
        out_shape=jax.ShapeDtypeStruct((3, n, d), BF),
        in_specs=[
            pl.BlockSpec((1, n, pair), lambda p: (0, 0, p)),
            pl.BlockSpec((1, n, pair), lambda p: (1, 0, p)),
            pl.BlockSpec((1, n, pair), lambda p: (2, 0, p)),
            pl.BlockSpec((2, n, n), lambda p: (p, 0, 0)),
            pl.BlockSpec((n, pair), lambda p: (0, p)),
            pl.BlockSpec((n, pair), lambda p: (0, p)),
            pl.BlockSpec(cosine.shape, lambda p: (0, 0)),
            pl.BlockSpec(sine.shape, lambda p: (0, 0)),
        ],
        out_specs=pl.BlockSpec((3, n, pair), lambda p: (0, 0, p)),
        compiler_params=params(),
        cost_estimate=cost(16 * n * n * d, 2 * n * n * (d // HD) + 16 * n * d),
        name="attend_back",
    )(three, three, three, probs, grad, mixed, cosine, sine)


def branch_kernel(x_ref, mixed_ref, w_ref, small_ref, residual_ref, hidden_ref):
    residual = x_ref[...].astype(F32) + dot(mixed_ref[...], w_ref[0])
    residual_ref[...] = residual
    unit, _ = norm_parts(residual)
    hidden_ref[...] = (unit * small_ref[2:3, :] + small_ref[3:4, :]).astype(BF)


def branch(x, mixed, weights, small):
    n, d = x.shape
    rows = n // 2
    return pl.pallas_call(
        branch_kernel,
        grid=(2,),
        out_shape=(jax.ShapeDtypeStruct((n, d), F32), jax.ShapeDtypeStruct((n, d), BF)),
        in_specs=[
            pl.BlockSpec((rows, d), lambda g: (g, 0)),
            pl.BlockSpec((rows, d), lambda g: (g, 0)),
            pl.BlockSpec((1, d, d), lambda g: (3, 0, 0)),
            pl.BlockSpec(small.shape, lambda g: (0, 0)),
        ],
        out_specs=(
            pl.BlockSpec((rows, d), lambda g: (g, 0)),
            pl.BlockSpec((rows, d), lambda g: (g, 0)),
        ),
        compiler_params=params(),
        cost_estimate=cost(2 * n * d * d, 10 * n * d + 2 * d * d),
        name="branch",
    )(x, mixed, weights, small)


def spread(out_ref, keep, product, me_f, masks, h, shards):
    keep[...] = product.astype(BF)
    for i in range(shards):
        j = me_f ^ bits_of(i, masks)
        for colour in range(2):
            start = pl.multiple_of(j * (2 * h) + colour * h, h & -h)
            out_ref[0, colour, i] = keep[pl.ds(start, h), :]


def up_kernel(
    masks, maps, rs, h, shards, idx_ref, hidden_ref, c_ref, small_ref, p0, p1, p2, p3,
    act_ref, slope_ref, grad_ref, w_out, w_ref, keep, sems, out_sems,
):
    g = pl.program_id(0)
    d4, me_f = idx_ref[0], idx_ref[1]
    d = hidden_ref.shape[1]

    def send(slot):
        return pltpu.make_async_copy(w_ref.at[slot], w_out.at[slot], out_sems.at[slot])

    @pl.when(g == 0)
    def _():
        fetch((p0, p1, p2, p3), maps, me_f, h, w_ref, rs.index, sems)

    fetched(w_ref, g, sems)
    send(g).start()
    chunk = d4 ^ jnp.where(g == 0, rs[0], rs[1])
    bias = small_ref[5:6, :]
    for other in range(1, 4):
        bias = jnp.where(chunk == other, small_ref[5 + other : 6 + other, :], bias)
    v = dot(hidden_ref[...], w_ref[g].reshape(d, d)) + bias
    c = math.sqrt(2.0 / math.pi)
    square = v * v
    t = jnp.tanh(v * (c + (c * 0.044715) * square))
    half = 0.5 * (1.0 + t)
    act = (v * half).astype(BF)
    act_ref[0] = act
    slope = half + (0.5 * v) * (1.0 - t * t) * (c + (3.0 * c * 0.044715) * square)
    slope_ref[0] = slope.astype(BF)
    spread(grad_ref, keep, dot_tn(act, c_ref[...]), me_f, masks, h, shards)

    @pl.when(g == 1)
    def _():
        send(0).wait()
        send(1).wait()


def up(idx, hidden, c, small, pieces, maps, rs, masks, shards, h):
    n, d = hidden.shape
    return pl.pallas_call(
        partial(up_kernel, masks, maps, rs, h, shards),
        grid=(2,),
        out_shape=(
            jax.ShapeDtypeStruct((2, n, d), BF),
            jax.ShapeDtypeStruct((2, n, d), BF),
            jax.ShapeDtypeStruct((2, 2, shards, h, d), BF),
            jax.ShapeDtypeStruct((2, shards, 2 * h, d), BF),
        ),
        in_specs=[
            pl.BlockSpec(memory_space=pltpu.SMEM),
            pl.BlockSpec((n, d), lambda g: (0, 0)),
            pl.BlockSpec((n, d), lambda g: (0, 0)),
            pl.BlockSpec(small.shape, lambda g: (0, 0)),
        ]
        + [pl.BlockSpec(memory_space=pl.ANY)] * 4,
        out_specs=(
            pl.BlockSpec((1, n, d), lambda g: (g, 0, 0)),
            pl.BlockSpec((1, n, d), lambda g: (g, 0, 0)),
            pl.BlockSpec((1, 2, shards, h, d), lambda g: (g, 0, 0, 0, 0)),
            pl.BlockSpec(memory_space=pl.ANY),
        ),
        scratch_shapes=[
            pltpu.VMEM((2, shards, 2 * h, d), BF),
            pltpu.VMEM((d, d), BF),
            pltpu.SemaphoreType.DMA((2,)),
            pltpu.SemaphoreType.DMA((2,)),
        ],
        compiler_params=params(),
        cost_estimate=cost(8 * n * d * d, 2 * (6 * n * d + 6 * d * d)),
        name="up",
    )(idx, hidden, c, small, *pieces)


def act_grad_kernel(
    masks, maps, rs, h, shards, first, idx_ref, c_ref, x_ref, up_ref, slope_ref, p0, p1, p2, p3,
    *more,
):
    if first:
        (hidden_ref, sums_ref, grad_ref, w_out, w_ref, keep, sems, out_sems) = more
    else:
        (
            hidden_in, sums_in, hidden_ref, sums_ref, grad_ref, w_out, w_ref, keep, sems, out_sems,
        ) = more
    g = pl.program_id(0)
    d4, me_f = idx_ref[0], idx_ref[1]
    d = x_ref.shape[1]
    c = c_ref[...]

    def send(slot):
        return pltpu.make_async_copy(w_ref.at[slot], w_out.at[slot], out_sems.at[slot])

    @pl.when(g == 0)
    def _():
        fetch((p0, p1, p2, p3), maps, me_f, h, w_ref, rs.index, sems)
        if first:
            hidden_ref[...] = jnp.zeros_like(hidden_ref)
            sums_ref[...] = jnp.zeros_like(sums_ref)
            sums_ref[4:5, :] = jnp.sum(c.astype(F32), axis=0, keepdims=True)
        else:
            hidden_ref[...] = hidden_in[...]
            sums_ref[...] = sums_in[...]

    fetched(w_ref, g, sems)
    send(g).start()
    chunk = d4 ^ jnp.where(g == 0, rs[0], rs[1])
    pre = (dot_nt(c, w_ref[g].reshape(d, d)) * slope_ref[0].astype(F32)).astype(BF)
    sums = jnp.sum(pre.astype(F32), axis=0, keepdims=True)
    row = lax.broadcasted_iota(jnp.int32, (sums_ref.shape[0], 1), 0)
    sums_ref[...] += jnp.where(row == 5 + chunk, sums, 0.0)
    hidden_ref[...] += dot_nt(pre, up_ref[0])
    spread(grad_ref, keep, dot_tn(x_ref[...], pre), me_f, masks, h, shards)

    @pl.when(g == 1)
    def _():
        send(0).wait()
        send(1).wait()


def act_grad(idx, c, hidden, up_half, slope, pieces, maps, rs, masks, shards, h, before=None):
    n, d = c.shape
    whole = pl.BlockSpec((n, d), lambda g: (0, 0))
    sums = pl.BlockSpec((SMALL, d), lambda g: (0, 0))
    return pl.pallas_call(
        partial(act_grad_kernel, masks, maps, rs, h, shards, before is None),
        grid=(2,),
        out_shape=(
            jax.ShapeDtypeStruct((n, d), F32),
            jax.ShapeDtypeStruct((SMALL, d), F32),
            jax.ShapeDtypeStruct((2, 2, shards, h, d), BF),
            jax.ShapeDtypeStruct((2, shards, 2 * h, d), BF),
        ),
        in_specs=[
            pl.BlockSpec(memory_space=pltpu.SMEM),
            whole,
            whole,
            pl.BlockSpec((1, d, d), lambda g: (g, 0, 0)),
            pl.BlockSpec((1, n, d), lambda g: (g, 0, 0)),
        ]
        + [pl.BlockSpec(memory_space=pl.ANY)] * 4
        + ([] if before is None else [whole, sums]),
        out_specs=(
            whole,
            sums,
            pl.BlockSpec((1, 2, shards, h, d), lambda g: (g, 0, 0, 0, 0)),
            pl.BlockSpec(memory_space=pl.ANY),
        ),
        scratch_shapes=[
            pltpu.VMEM((2, shards, 2 * h, d), BF),
            pltpu.VMEM((d, d), BF),
            pltpu.SemaphoreType.DMA((2,)),
            pltpu.SemaphoreType.DMA((2,)),
        ],
        compiler_params=params(),
        cost_estimate=cost(12 * n * d * d, 2 * (8 * n * d + 8 * d * d)),
        name="act_grad",
    )(idx, c, hidden, up_half.reshape(2, d, d), slope, *pieces, *(before or ()))


def first_grad_kernel(
    masks, h, shards, rs, idx_ref, normed_ref, mixed_ref, three_ref, branch_ref, out_ref, keep
):
    g = pl.program_id(0)
    last = (idx_ref[0] ^ jnp.where(g == 0, rs[0], rs[1])) == 3
    x = jnp.where(last, mixed_ref[...], normed_ref[...])
    y = jnp.where(last, branch_ref[...], three_ref[0])
    spread(out_ref, keep, dot_tn(x, y), idx_ref[1], masks, h, shards)


def first_grad(idx, normed, mixed, three_grad, branch_grad, rs, masks, shards, h):
    n, d = normed.shape

    def which(g, idx_ref):
        return jnp.minimum(idx_ref[0] ^ jnp.where(g == 0, rs[0], rs[1]), 2)

    whole = pl.BlockSpec((n, d), lambda g, i: (0, 0))
    return pl.pallas_call(
        partial(first_grad_kernel, masks, h, shards, rs),
        grid_spec=pltpu.PrefetchScalarGridSpec(
            num_scalar_prefetch=1,
            grid=(2,),
            in_specs=[
                whole,
                whole,
                pl.BlockSpec((1, n, d), lambda g, i: (which(g, i), 0, 0)),
                whole,
            ],
            out_specs=pl.BlockSpec((1, 2, shards, h, d), lambda g, i: (g, 0, 0, 0, 0)),
            scratch_shapes=[pltpu.VMEM((d, d), BF)],
        ),
        out_shape=jax.ShapeDtypeStruct((2, 2, shards, h, d), BF),
        compiler_params=params(),
        cost_estimate=cost(4 * n * d * d, 2 * (5 * n * d + 2 * d * d)),
        name="first_grad",
    )(idx, normed, mixed, three_grad, branch_grad)


def middle_kernel(
    c_ref, hidden_ref, residual_ref, small_ref, w_ref, grad_ref, low_ref, mixed_ref, sums_ref
):
    @pl.when(pl.program_id(0) == 0)
    def _():
        sums_ref[...] = jnp.zeros_like(sums_ref)

    grad = hidden_ref[...]
    unit, inv = norm_parts(residual_ref[...])
    sums_ref[2:3, :] += jnp.sum(grad * unit, axis=0, keepdims=True)
    sums_ref[3:4, :] += jnp.sum(grad, axis=0, keepdims=True)
    full = c_ref[...].astype(F32) + norm_back(grad, unit, inv, small_ref[2:3, :])
    grad_ref[...] = full
    low = full.astype(BF)
    low_ref[...] = low
    mixed_ref[...] = dot_nt(low, w_ref[0]).astype(BF)


def middle(c, hidden_grad, residual, small, weights):
    n, d = c.shape
    rows = n // 2
    return pl.pallas_call(
        middle_kernel,
        grid=(2,),
        out_shape=(
            jax.ShapeDtypeStruct((n, d), F32),
            jax.ShapeDtypeStruct((n, d), BF),
            jax.ShapeDtypeStruct((n, d), BF),
            jax.ShapeDtypeStruct((SMALL, d), F32),
        ),
        in_specs=[
            pl.BlockSpec((rows, d), lambda g: (g, 0)),
            pl.BlockSpec((rows, d), lambda g: (g, 0)),
            pl.BlockSpec((rows, d), lambda g: (g, 0)),
            pl.BlockSpec(small.shape, lambda g: (0, 0)),
            pl.BlockSpec((1, d, d), lambda g: (3, 0, 0)),
        ],
        out_specs=(
            pl.BlockSpec((rows, d), lambda g: (g, 0)),
            pl.BlockSpec((rows, d), lambda g: (g, 0)),
            pl.BlockSpec((rows, d), lambda g: (g, 0)),
            pl.BlockSpec((SMALL, d), lambda g: (0, 0)),
        ),
        compiler_params=params(),
        cost_estimate=cost(2 * n * d * d, 18 * n * d + 2 * d * d),
        name="middle",
    )(c, hidden_grad, residual, small, weights)


def input_kernel(x_ref, three_ref, w_ref, small_ref, grad_ref, out_ref, sums_ref, total):
    g = pl.program_id(0)
    part = dot_nt(three_ref[0], w_ref[0])

    @pl.when(g == 0)
    def _():
        total[...] = part

    @pl.when(g > 0)
    def _():
        total[...] += part

    @pl.when(g == 2)
    def _():
        grad = total[...]
        unit, inv = norm_parts(x_ref[...].astype(F32))
        sums_ref[...] = jnp.zeros_like(sums_ref)
        sums_ref[0:1, :] = jnp.sum(grad * unit, axis=0, keepdims=True)
        sums_ref[1:2, :] = jnp.sum(grad, axis=0, keepdims=True)
        out_ref[...] = grad_ref[...] + norm_back(grad, unit, inv, small_ref[0:1, :])


def input_grads(x, three_grad, weights, small, residual_grad):
    n, d = x.shape
    return pl.pallas_call(
        input_kernel,
        grid=(3,),
        out_shape=(jax.ShapeDtypeStruct((n, d), F32), jax.ShapeDtypeStruct((SMALL, d), F32)),
        in_specs=[
            pl.BlockSpec((n, d), lambda g: (0, 0)),
            pl.BlockSpec((1, n, d), lambda g: (g, 0, 0)),
            pl.BlockSpec((1, d, d), lambda g: (g, 0, 0)),
            pl.BlockSpec(small.shape, lambda g: (0, 0)),
            pl.BlockSpec((n, d), lambda g: (0, 0)),
        ],
        out_specs=(
            pl.BlockSpec((n, d), lambda g: (0, 0)),
            pl.BlockSpec((SMALL, d), lambda g: (0, 0)),
        ),
        scratch_shapes=[pltpu.VMEM((n, d), F32)],
        compiler_params=params(),
        cost_estimate=cost(6 * n * d * d, 16 * n * d + 6 * d * d),
        name="input_grads",
    )(x, three_grad, weights, small, residual_grad)


def down_kernel(a0_ref, a1_ref, w0_ref, w1_ref, small_ref, residual_ref, out_ref, total):
    g = pl.program_id(0)
    part = dot(a0_ref[0], w0_ref[0]) + dot(a1_ref[0], w1_ref[0])

    @pl.when(g == 0)
    def _():
        total[...] = residual_ref[...] + small_ref[4:5, :] + part

    @pl.when(g == 1)
    def _():
        out_ref[...] = (total[...] + part).astype(BF)


def down_out(acts, weights, small, residual):
    n, d = residual.shape
    return pl.pallas_call(
        down_kernel,
        grid=(2,),
        out_shape=jax.ShapeDtypeStruct((n, d), BF),
        in_specs=[
            pl.BlockSpec((1, n, d), lambda g: (g, 0, 0)),
            pl.BlockSpec((1, n, d), lambda g: (g, 0, 0)),
            pl.BlockSpec((1, d, d), lambda g: (g, 0, 0)),
            pl.BlockSpec((1, d, d), lambda g: (g, 0, 0)),
            pl.BlockSpec(small.shape, lambda g: (0, 0)),
            pl.BlockSpec((n, d), lambda g: (0, 0)),
        ],
        out_specs=pl.BlockSpec((n, d), lambda g: (0, 0)),
        scratch_shapes=[pltpu.VMEM((n, d), F32)],
        compiler_params=params(),
        cost_estimate=cost(8 * n * d * d, 14 * n * d + 8 * d * d),
        name="down_out",
    )(*acts, *(w.reshape(2, d, d) for w in weights), small, residual)


def last_kernel(shards, idx_ref, p0, p1, p2, p3, up_ref, down_ref, keep):
    _, rows, d = keep.shape
    for r, ref in enumerate((p0, p1, p2, p3)):
        at = idx_ref[0] ^ r
        keep[at] = ref[0].reshape(rows, d).astype(F32)
        down_ref[pl.ds(pl.multiple_of(at * rows, 8), rows), :] = ref[1].reshape(rows, d).astype(F32)
    for i in range(shards):
        part = [keep[chunk, :, i * rows : (i + 1) * rows] for chunk in range(4)]
        up_ref[:, 4 * rows * i : 4 * rows * (i + 1)] = jnp.concatenate(part, axis=1)


def last_out(idx, pieces, shards):
    d = pieces[0].shape[-1]
    rows = d // shards
    vmem = pl.BlockSpec(memory_space=pltpu.VMEM)
    return pl.pallas_call(
        partial(last_kernel, shards),
        out_shape=(
            jax.ShapeDtypeStruct((rows, 4 * d), F32),
            jax.ShapeDtypeStruct((4 * rows, d), F32),
        ),
        in_specs=[pl.BlockSpec(memory_space=pltpu.SMEM)] + [vmem] * 4,
        out_specs=(vmem, vmem),
        scratch_shapes=[pltpu.VMEM((4, rows, d), F32)],
        compiler_params=params(),
        name="last_out",
    )(idx, *pieces)


def local(dp, fsdp, tokens, lengths, *rest):
    (
        norm1_gain,
        norm1_bias,
        query_weight,
        key_weight,
        value_weight,
        output_weight,
        norm2_gain,
        norm2_bias,
        up_weight,
        up_bias,
        down_weight,
        down_bias,
        cotangent,
    ) = rest
    row_count, width = tokens.shape
    slot_count = lengths.shape[1]
    R = width // fsdp
    h = R // 2
    me_dp = lax.axis_index("dp").astype(jnp.int32)
    me_f = lax.axis_index("fsdp").astype(jnp.int32)
    d4 = me_dp % 4
    idx = jnp.stack([d4, me_f])
    masks = []
    mask = fsdp // 2
    while mask >= 1:
        masks.append(mask)
        mask //= 2
    masks = tuple(masks)
    outer = masks[:-1]

    def fswap(v, m):
        return swap(v, "fsdp", m, fsdp)

    def dswap(v, m):
        return swap(v, "dp", m, dp)

    def after(value, *tokens):
        return lax.optimization_barrier((value,) + tokens)[0]

    def after_all(values, *tokens):
        values = tuple(values)
        return list(lax.optimization_barrier(values + tokens)[: len(values)])

    half = fsdp // 2
    maps_own = [
        piece_map(w, masks) for w in (("a", 0, 0), ("a", 2, 0), ("b", 0, 0), ("b", 0, 1))
    ]
    maps_core = [
        piece_map(w, masks) for w in (("a", 1, 0), ("a", 3, 0), ("b", 1, 0), ("b", 1, 1))
    ]

    class Gather:
        def __init__(self, piece):
            self.cur = piece[None]

        def far(self, m):
            self.got = fswap(self.cur, m)

        def join(self):
            self.cur = jnp.concatenate([self.cur, self.got], axis=0)

        def near(self):
            self.got = fswap(self.cur, outer[-1])

        def sides(self):
            a = jnp.concatenate([self.cur[:, :h], self.got[:, :h]], axis=0)
            b = jnp.concatenate([self.cur[:, h:R], self.got[:, h:R]], axis=0)
            self.ab = (a, b)
            self.got_ab = (fswap(a, masks[-1]), dswap(b, 2))

        def cross(self):
            a1 = jnp.concatenate([self.ab[0], self.got_ab[0]], axis=0)
            b1 = jnp.concatenate([self.ab[1], self.got_ab[1]], axis=0)
            self.ab1 = (a1, b1)
            self.got_ab1 = (dswap(a1, 2), fswap(b1, masks[-1]))
            self.core = [dswap(a1, 1), dswap(b1, 1)]

        def finish(self):
            a_x, b_y = self.got_ab1
            a1, b1 = self.ab1
            self.own = [a1, a_x, b1, b_y]
            self.other = [self.core[0], dswap(a_x, 1), self.core[1], dswap(b_y, 1)]

    class Inner:
        def __init__(self, cur):
            self.cur = cur
            self.got = None
            self.left = list(reversed(outer))

        def step(self, *tokens):
            if self.got is not None:
                self.cur = self.cur + after(self.got, *tokens)
                self.got = None
            if self.left:
                count = self.cur.shape[0] // 2
                front = self.cur[count:]
                self.got = fswap(front, self.left.pop(0))
                self.cur = self.cur[:count]
                return front
            return self.cur

        def sums(self):
            while self.got is not None or self.left:
                self.step()
            return self.cur[0]

    class Spread:
        def __init__(self, total):
            m = 4
            while m < dp:
                total = total + dswap(total, m)
                m *= 2
            self.total = total
            self.pair = dswap(total, 2)
            self.core = dswap(total, 1)

        def four(self, *tokens):
            pair = after(self.pair, *tokens)
            return [self.total, self.core, pair, dswap(pair, 1)]

    piece1 = lax.select_n(d4, query_weight, key_weight, value_weight, output_weight)
    g1 = Gather(piece1)
    for m in outer[:-1]:
        g1.far(m)
        g1.join()
    g1_first = g1.cur
    g1.near()
    vectors = after_all(
        (norm1_gain, norm1_bias, norm2_gain, norm2_bias, down_bias, up_bias, up_weight), piece1
    )
    tall = jnp.concatenate(vectors[:6]).reshape(9, R)
    lane = jnp.arange(width, dtype=jnp.int32) // R
    tall = jnp.where((lane == me_f)[None, :], jnp.tile(tall, (1, fsdp)), jnp.zeros((), BF))
    tall = jnp.pad(tall, ((0, SMALL - 9), (0, 0)))
    fronts = []
    for m in reversed(masks):
        if len(fronts) == 1:
            tall = after(tall, g1.got)
        fronts.append(tall)
        tall = tall + fswap(tall, m)
    small = tall.astype(F32)
    piece2 = lax.dynamic_index_in_dim(
        vectors[6].reshape(R, fsdp, 4, R), d4, axis=2, keepdims=False
    ).reshape(R, width)
    g2 = Gather(after(piece2, g1.got, *fronts[2:]))
    for m in outer[:-1]:
        g2.far(m)
        g2.join()
    g1.sides()
    g2.cur, g2.got = after_all((g2.cur, g2.got), *g1.ab)
    g2.near()
    g1.cross()
    early = outer[:-1]
    g3 = Gather(
        lax.dynamic_slice_in_dim(after(down_weight, g2.cur), d4 * R, R, axis=0)
    )
    for m in early[:-1]:
        g3.far(m)
        g3.join()
    g3.far(early[-1])
    g1.finish()
    g2.cur, g2.got = after_all((g2.cur, g2.got), *g1.got_ab1)
    g2.sides()
    g3.join()
    g3.near()

    layout = row_layout(after(lengths, g1_first)[0], row_count, slot_count)
    cosine, sine = rotary_tables(layout[3])
    bias = jnp.where(allowed_pairs(layout, layout, BLOCK, slot_count), 0.0, NEGATIVE)
    normed, three, first4 = qkv(
        idx, after(tokens, *g2.ab, g3.cur, bias), small, cosine, sine, g1.own + g1.other,
        maps_own + maps_core, fsdp, h,
    )
    first4 = first4.reshape(4, width, width)
    g2.got_ab = after_all(g2.got_ab, three)
    g2.cross()
    mixed, probs = attend(after(three, *g2.ab1), bias)
    g2.got_ab1 = after_all(g2.got_ab1, mixed)
    g2.finish()
    g3.cur, g3.got = after_all((g3.cur, g3.got), mixed)
    g3.sides()
    residual, hidden_in = branch(tokens, after(mixed, *g2.got_ab1, *g2.core, *g3.ab), first4, small)
    g3.got_ab = after_all(g3.got_ab, hidden_in)
    g3.cross()
    send_rs, keep_rs = (1, 3), (0, 2)
    act_s, slope_s, send3, up_s = up(
        idx, after(hidden_in, *g3.ab1), cotangent, small, g2.other, maps_core, send_rs, masks,
        fsdp, h,
    )
    act_k, slope_k, keep3, up_k = up(
        idx, after(hidden_in, send3), cotangent, small, g2.own, maps_own, keep_rs, masks, fsdp, h,
    )
    g3.got_ab1 = after_all(g3.got_ab1, keep3)
    g3.finish()

    class Scatter:
        def __init__(self, send):
            self.got = dswap(send, 1)

        def sides(self, keep):
            got = self.got
            a = keep[1, 0] + got[1, 0]
            b = keep[:, 1, half:] + got[:, 1, half:]
            self.keep = (keep[0, 0] + got[0, 0], keep[:, 1, :half] + got[:, 1, :half])
            self.mid = [dswap(a, 2), fswap(b, masks[-1])]
            self.done = (a, b) + self.keep

        def cross(self):
            (a, b), (x, y) = self.keep, self.mid
            self.last = (a[:half] + x[:half], b[0] + y[0])
            out = (a[half:] + x[half:], b[1] + y[1])
            self.got_last = [fswap(out[0], masks[-1]), dswap(out[1], 2)]
            self.done = out + self.last

        def rows(self):
            (a, b), (x, y) = self.last, self.got_last
            return jnp.stack([a + x, b + y], axis=1)

    s3 = Scatter(send3)
    s3.sides(keep3)
    hidden_s, sums_s, send2, down_s = act_grad(
        idx, after(cotangent, *s3.done), hidden_in, up_s, slope_s, g3.other, maps_core, send_rs,
        masks, fsdp, h,
    )
    s2 = Scatter(send2)
    s3.mid = after_all(s3.mid, send2)
    s3.cross()
    hidden_grad, sums_act, keep2, down_k = act_grad(
        idx, after(cotangent, send2, *s3.done), hidden_in, up_k, slope_k, g3.own, maps_own,
        keep_rs, masks, fsdp, h, (hidden_s, sums_s),
    )
    s2.sides(keep2)
    s3.got_last = after_all(s3.got_last, keep2)
    rows3 = Inner(s3.rows())
    front = rows3.step()
    residual_grad, branch_grad, mixed_grad, sums_mid = middle(
        cotangent, after(hidden_grad, *s2.done, front), residual, small, first4
    )
    front = rows3.step(mixed_grad)
    three_grad = attend_back(three, probs, after(mixed_grad, front), mixed, cosine, sine)
    s2.mid = after_all(s2.mid, three_grad)
    s2.cross()
    front = rows3.step(three_grad)
    send1 = first_grad(
        idx, after(normed, *s2.done, front), mixed, three_grad, branch_grad, send_rs, masks, fsdp,
        h,
    )
    s1 = Scatter(send1)
    s2.got_last = after_all(s2.got_last, send1)
    rows2 = Inner(s2.rows())
    front = rows2.step()
    keep1 = first_grad(
        idx, after(normed, front, send1), mixed, three_grad, branch_grad, keep_rs, masks, fsdp, h
    )
    s1.sides(keep1)
    front = rows2.step(*s1.done)
    input_grad, sums_in = input_grads(
        after(tokens, *s1.done, front), three_grad, first4, small, residual_grad
    )
    front = rows2.step(input_grad)
    small_sum = sums_act + sums_mid + sums_in

    def small_step(swapper, m, *tokens):
        low = after(small_sum.astype(BF), *tokens)
        return low, swapper(low, m)

    low, small_got = small_step(dswap, 1)
    output = down_out(
        (act_s, act_k), (down_s, down_k), small, after(residual, front, low)
    )
    s1.mid = after_all(s1.mid, output)
    s1.cross()
    both = Spread(after(jnp.stack([rows2.sums(), rows3.sums()]), *s1.done))
    rest = [(fswap, m) for m in reversed(masks)]
    m = 2
    while m < dp:
        rest.append((dswap, m))
        m *= 2
    small_sum = small_sum + after(small_got, output).astype(F32)
    low, small_got = small_step(*rest.pop(), *s1.done)
    rows1 = Inner(s1.rows())
    small_sum = small_sum + after(small_got, rows1.cur).astype(F32)
    front = rows1.step()
    low, small_got = small_step(*rest.pop(), front)
    both.pair = after(both.pair, rows1.cur)
    front = rows1.step(low)
    small_sum = small_sum + after(small_got, front).astype(F32)
    low, small_got = small_step(*rest.pop(), front)
    four23 = both.four(front)

    up_grad, down_grad = last_out(idx, four23, fsdp)
    if rows1.got is not None:
        rows1.got = after(rows1.got, up_grad)
    one = Spread(rows1.sums())
    small_sum = small_sum + after(small_got, one.total).astype(F32)
    while rest:
        low, small_got = small_step(*rest.pop(), one.total)
        small_sum = small_sum + small_got.astype(F32)
    four1 = jnp.stack(one.four())
    first_grads = [
        lax.dynamic_index_in_dim(four1, d4 ^ d, axis=0, keepdims=False)
        .reshape(R, width)
        .astype(F32)
        for d in range(4)
    ]
    own = lax.dynamic_slice_in_dim(small_sum, me_f * R, R, axis=1)
    return (
        output,
        input_grad,
        own[0],
        own[1],
        first_grads[0],
        first_grads[1],
        first_grads[2],
        first_grads[3],
        own[2],
        own[3],
        up_grad,
        own[5:9].reshape(4 * R),
        down_grad,
        own[4],
    )


def solution(mesh):
    rows = P(("dp", "fsdp"), None)
    flat = P("fsdp")
    tall = P("fsdp", None)
    in_specs = (
        rows, rows, flat, flat, tall, tall, tall, tall, flat, flat, tall, flat, tall, flat, rows,
    )
    out_specs = (
        rows, rows, flat, flat, tall, tall, tall, tall, flat, flat, tall, flat, tall, flat,
    )
    return jax.shard_map(
        partial(local, mesh.shape["dp"], mesh.shape["fsdp"]),
        mesh=mesh,
        in_specs=in_specs,
        out_specs=out_specs,
        check_vma=False,
    )
```

profile of v0, /device:TPU:0, one launch (start us, length us, event | category | flops | bytes accessed | tf_op | source)
XLA Modules:
  0.0 245.5 jit_solution(12157432064804750396)
XLA Ops:
  1.8 4.1 %collective-permute-start = (bf16[1,96,768]{2,1,0:T(8,128)(2,1)S(1)}, bf16[1,96,768]{2,1,0:T(8,128)(2,1)S(1)}, u32[]{:S(2)}, u32[]{:S(2)}) collective-permute-start(bf16[1,96,768]{2,1,0:T(8,128)(2,1)S(1)} %bitcast.156), channel_id=1, source_target_pairs={{0,4},{1,5},{2,6},{3,7},{4,0},{5,1},{6,2},{7,3},{8,12},{9,13},{10,... | collective-permute-start | bytes 442376 | tf_op jit(solution)/shard_map/ppermute | solution.py:69
  5.9 4.1 %concatenate.55 = bf16[864]{0:T(1024)(128)(2,1)S(1)} concatenate(bf16[96]{0:T(256)(128)(2,1)} %param.17, bf16[96]{0:T(256)(128)(2,1)} %param.18, bf16[96]{0:T(256)(128)(2,1)} %param.23, bf16[96]{0:T(256)(128)(2,1)} %param.24, bf16[96]{0:T(256)(128)(2,1)} %param.28, bf16[384]{0:T(512)(128)(2,1)} %param.26), dimensions={0} | concatenate | bytes 3456 | tf_op jit(solution)/shard_map/concatenate | solution.py:852
  10.3 1.6 collective-permute-start.2
  11.9 2.3 reshape.252
  16.2 1.6 collective-permute-start.1
  18.3 6.2 %collective-permute-done.1 = bf16[2,96,768]{2,1,0:T(8,128)(2,1)S(1)} collective-permute-done((bf16[2,96,768]{2,1,0:T(8,128)(2,1)S(1)}, bf16[2,96,768]{2,1,0:T(8,128)(2,1)S(1)}, u32[]{:S(2)}, u32[]{:S(2)}) %collective-permute-start.1) | collective-permute-done | bytes 294944 | tf_op jit(solution)/shard_map/ppermute | solution.py:69
  24.5 1.6 collective-permute-start.3
  26.7 1.6 collective-permute-start.8
  28.3 1.7 fusion.2.bias_ref
  31.1 2.1 collective-permute-done.6
  33.3 1.6 collective-permute-start.7
  35.0 1.6 collective-permute-start.9
  36.5 1.8 fusion.33
  39.4 2.5 %collective-permute-start.10 = (bf16[1,96,768]{2,1,0:T(8,128)(2,1)S(1)}, bf16[1,96,768]{2,1,0:T(8,128)(2,1)S(1)}, u32[]{:S(2)}, u32[]{:S(2)}) collective-permute-start(bf16[1,96,768]{2,1,0:T(8,128)(2,1)S(1)} %dynamic-slice_bitcast_fusion), channel_id=1, source_target_pairs={{0,4},{1,5},{2,6},{3,7},{4,0},{5,1},{6,2},{7,3},{8,12},{9,13},{10,... | collective-permute-start | bytes 442376 | tf_op jit(solution)/shard_map/ppermute | solution.py:69
  41.9 2.3 collective-permute-done.11
  44.8 1.6 collective-permute-done.10
  48.5 1.9 collective-permute-start.22
  53.3 9.4 %qkv.1 = (bf16[512,768]{1,0:T(8,128)(2,1)}, bf16[3,512,768]{2,1,0:T(8,128)(2,1)}, bf16[4,8,96,768]{3,2,1,0:T(8,128)(2,1)}) custom-call(s32[2]{0:T(128)} %pad_add_fusion.idx_ref, bf16[512,768]{1,0:T(8,128)(2,1)} %x_ref.3, f32[16,768]{1,0:T(8,128)} %add_convert_fusion.small_ref, f32[512,128]{1,0:T(8,128)} %get-tuple-element.263.cos_ref, ...), custom_call_target="tpu_custom_call" | custom-call | flops 48000000000 | bytes 13369344 | tf_op jit(solution)/shard_map/qkv/pallas_call | solution.py:197
  62.9 1.6 collective-permute-start.18
  66.0 10.4 %attend.1 = (bf16[512,768]{1,0:T(8,128)(2,1)}, bf16[12,512,512]{2,1,0:T(8,128)(2,1)}) custom-call(bf16[3,512,768]{2,1,0:T(8,128)(2,1)} %get-tuple-element.127.q_ref.k_ref.v_ref, bf16[3,512,768]{2,1,0:T(8,128)(2,1)} %get-tuple-element.127.q_ref.k_ref.v_ref, bf16[3,512,768]{2,1,0:T(8,128)(2,1)} %get-tuple-element.127.q_ref.k_ref.v_ref, f32[512,512]{1,0:T(8,128)} %fusion.2.bias_ref), custom_call_target="tpu_custom_call" | custom-call | flops 48000000000 | bytes 9437184 | tf_op jit(solution)/shard_map/attend/pallas_call | solution.py:254
  80.8 4.0 %branch.1 = (f32[512,768]{1,0:T(8,128)}, bf16[512,768]{1,0:T(8,128)(2,1)}) custom-call(bf16[512,768]{1,0:T(8,128)(2,1)} %x_ref.3, bf16[512,768]{1,0:T(8,128)(2,1)} %get-tuple-element.133.mixed_ref, bf16[4,768,768]{2,1,0:T(8,128)(2,1)} %bitcast.168, f32[16,768]{1,0:T(8,128)} %add_convert_fusion.small_ref), custom_call_target="tpu_custom_call" | custom-call | flops 48000000000 | bytes 5111808 | tf_op jit(solution)/shard_map/branch/pallas_call | solution.py:335
  90.6 9.1 %up.2 = (bf16[2,512,768]{2,1,0:T(8,128)(2,1)}, bf16[2,512,768]{2,1,0:T(8,128)(2,1)}, bf16[2,2,8,48,768]{4,3,2,1,0:T(8,128)(2,1)}, bf16[2,8,96,768]{3,2,1,0:T(8,128)(2,1)}) custom-call(s32[2]{0:T(128)} %pad_add_fusion.idx_ref, bf16[512,768]{1,0:T(8,128)(2,1)} %get-tuple-element.141.hidden_ref.x_ref, bf16[512,768]{1,0:T(8,128)(2,1)} %c_ref.7, ...), custom_call_target="tpu_custom_call" | custom-call | flops 48000000000 | bytes 11796480 | tf_op jit(solution)/shard_map/up/pallas_call | solution.py:404
  99.8 9.1 %up.3 = (bf16[2,512,768]{2,1,0:T(8,128)(2,1)}, bf16[2,512,768]{2,1,0:T(8,128)(2,1)}, bf16[2,2,8,48,768]{4,3,2,1,0:T(8,128)(2,1)}, bf16[2,8,96,768]{3,2,1,0:T(8,128)(2,1)}) custom-call(s32[2]{0:T(128)} %pad_add_fusion.idx_ref, bf16[512,768]{1,0:T(8,128)(2,1)} %get-tuple-element.141.hidden_ref.x_ref, bf16[512,768]{1,0:T(8,128)(2,1)} %c_ref.7, ...), custom_call_target="tpu_custom_call" | custom-call | flops 48000000000 | bytes 11796480 | tf_op jit(solution)/shard_map/up/pallas_call | solution.py:404
  109.5 1.9 slice_add_fusion.9
  115.4 9.8 %act_grad.2 = (f32[512,768]{1,0:T(8,128)}, f32[16,768]{1,0:T(8,128)}, bf16[2,2,8,48,768]{4,3,2,1,0:T(8,128)(2,1)}, bf16[2,8,96,768]{3,2,1,0:T(8,128)(2,1)}) custom-call(s32[2]{0:T(128)} %pad_add_fusion.idx_ref, bf16[512,768]{1,0:T(8,128)(2,1)} %c_ref.7, bf16[512,768]{1,0:T(8,128)(2,1)} %get-tuple-element.141.hidden_ref.x_ref, ...), custom_call_target="tpu_custom_call" | custom-call | flops 48000000000 | bytes 15728640 | tf_op jit(solution)/shard_map/act_grad/pallas_call | solution.py:487
  125.3 1.8 collective-permute-done.34
  130.3 10.3 %act_grad.3 = (f32[512,768]{1,0:T(8,128)}, f32[16,768]{1,0:T(8,128)}, bf16[2,2,8,48,768]{4,3,2,1,0:T(8,128)(2,1)}, bf16[2,8,96,768]{3,2,1,0:T(8,128)(2,1)}) custom-call(s32[2]{0:T(128)} %pad_add_fusion.idx_ref, bf16[512,768]{1,0:T(8,128)(2,1)} %c_ref.7, bf16[512,768]{1,0:T(8,128)(2,1)} %get-tuple-element.141.hidden_ref.x_ref, ...), custom_call_target="tpu_custom_call" | custom-call | flops 48000000000 | bytes 15728640 | tf_op jit(solution)/shard_map/act_grad/pallas_call | solution.py:487
  140.8 2.2 collective-permute-start.41
  145.3 4.9 %middle.1 = (f32[512,768]{1,0:T(8,128)}, bf16[512,768]{1,0:T(8,128)(2,1)}, bf16[512,768]{1,0:T(8,128)(2,1)}, f32[16,768]{1,0:T(8,128)}) custom-call(bf16[512,768]{1,0:T(8,128)(2,1)} %c_ref.7, f32[512,768]{1,0:T(8,128)} %get-tuple-element.165.hidden_ref, f32[512,768]{1,0:T(8,128)} %get-tuple-element.186.residual_ref, f32[16,768]{1,0:T(8,128)} %add_convert_fusion.small_ref, ...), custom_call_target="tpu_custom_call" | custom-call | flops 48000000000 | bytes 8257536 | tf_op jit(solution)/shard_map/middle/pallas_call | solution.py:582
  150.3 1.5 collective-permute-start.44
  151.8 11.6 %attend_back.1.three_ref = bf16[3,512,768]{2,1,0:T(8,128)(2,1)} custom-call(bf16[3,512,768]{2,1,0:T(8,128)(2,1)} %get-tuple-element.127.q_ref.k_ref.v_ref, bf16[3,512,768]{2,1,0:T(8,128)(2,1)} %get-tuple-element.127.q_ref.k_ref.v_ref, bf16[3,512,768]{2,1,0:T(8,128)(2,1)} %get-tuple-element.127.q_ref.k_ref.v_ref, ...), custom_call_target="tpu_custom_call" | custom-call | flops 48000000000 | bytes 12582912 | tf_op jit(solution)/shard_map/attend_back/pallas_call | solution.py:304
  164.9 1.7 collective-permute-start.43
  166.6 5.4 %first_grad.2 = bf16[2,2,8,48,768]{4,3,2,1,0:T(8,128)(2,1)} custom-call(s32[2]{0:T(128)} %pad_add_fusion.idx_ref, bf16[512,768]{1,0:T(8,128)(2,1)} %get-tuple-element.177.normed_ref, bf16[512,768]{1,0:T(8,128)(2,1)} %get-tuple-element.133.mixed_ref, bf16[3,512,768]{2,1,0:T(8,128)(2,1)} %attend_back.1.three_ref, bf16[512,768]{1,0:T(8,128)(2,1)} %get-tuple-element.174.branch_ref), custom_call_target="tpu_custom_call" | custom-call | flops 48000000000 | bytes 6291456 | tf_op jit(solution)/shard_map/first_grad/pallas_call | solution.py:540
  172.2 1.5 collective-permute-start.45
  173.7 5.4 %first_grad.3 = bf16[2,2,8,48,768]{4,3,2,1,0:T(8,128)(2,1)} custom-call(s32[2]{0:T(128)} %pad_add_fusion.idx_ref, bf16[512,768]{1,0:T(8,128)(2,1)} %get-tuple-element.177.normed_ref, bf16[512,768]{1,0:T(8,128)(2,1)} %get-tuple-element.133.mixed_ref, bf16[3,512,768]{2,1,0:T(8,128)(2,1)} %attend_back.1.three_ref, bf16[512,768]{1,0:T(8,128)(2,1)} %get-tuple-element.174.branch_ref), custom_call_target="tpu_custom_call" | custom-call | flops 48000000000 | bytes 6291456 | tf_op jit(solution)/shard_map/first_grad/pallas_call | solution.py:540
  179.1 1.5 slice_add_fusion.1
  181.7 1.6 collective-permute-start.47
  185.0 7.9 %input_grads.1 = (f32[512,768]{1,0:T(8,128)}, f32[16,768]{1,0:T(8,128)}) custom-call(bf16[512,768]{1,0:T(8,128)(2,1)} %x_ref.3, bf16[3,512,768]{2,1,0:T(8,128)(2,1)} %attend_back.1.three_ref, bf16[4,768,768]{2,1,0:T(8,128)(2,1)} %bitcast.170, f32[16,768]{1,0:T(8,128)} %add_convert_fusion.small_ref, f32[512,768]{1,0:T(8,128)} %get-tuple-element.180.grad_ref), custom_call_target="tpu_custom_call" | custom-call | flops 48000000000 | bytes 9830400 | tf_op jit(solution)/shard_map/input_grads/pallas_call | solution.py:634
  193.9 6.9 %down_out.1 = bf16[512,768]{1,0:T(8,128)(2,1)} custom-call(bf16[2,512,768]{2,1,0:T(8,128)(2,1)} %get-tuple-element.139.a0_ref, bf16[2,512,768]{2,1,0:T(8,128)(2,1)} %get-tuple-element.142.a1_ref, bf16[2,768,768]{2,1,0:T(8,128)(2,1)} %bitcast.171, bf16[2,768,768]{2,1,0:T(8,128)(2,1)} %bitcast.172, f32[16,768]{1,0:T(8,128)} %add_convert_fusion.small_ref, ...), custom_call_target="tpu_custom_call" | custom-call | flops 48000000000 | bytes 10223616 | tf_op jit(solution)/shard_map/down_out/pallas_call | solution.py:671
  203.3 7.0 %collective-permute-done.52 = bf16[4,48,768]{2,1,0:T(8,128)(2,1)S(1)} collective-permute-done((bf16[4,48,768]{2,1,0:T(8,128)(2,1)S(1)}, bf16[4,48,768]{2,1,0:T(8,128)(2,1)S(1)}, u32[]{:S(2)}, u32[]{:S(2)}) %collective-permute-start.52) | collective-permute-done | bytes 294944 | tf_op jit(solution)/shard_map/ppermute | solution.py:69
  212.5 1.5 collective-permute-start.55
  215.3 5.3 %collective-permute-done.55 = bf16[2,2,48,768]{3,2,0,1:T(8,128)(2,1)S(1)} collective-permute-done((bf16[2,2,48,768]{3,2,0,1:T(8,128)(2,1)S(1)}, bf16[2,2,48,768]{3,2,0,1:T(8,128)(2,1)S(1)}, u32[]{:S(2)}, u32[]{:S(2)}) %collective-permute-start.55) | collective-permute-done | bytes 294944 | tf_op jit(solution)/shard_map/ppermute | solution.py:69
  220.6 2.9 %collective-permute-done.59.p2 = bf16[2,2,48,768]{3,2,1,0:T(8,128)(2,1)S(1)} collective-permute-done((bf16[2,2,48,768]{3,2,1,0:T(8,128)(2,1)S(1)}, bf16[2,2,48,768]{3,2,1,0:T(8,128)(2,1)S(1)}, u32[]{:S(2)}, u32[]{:S(2)}) %collective-permute-start.59) | collective-permute-done | bytes 294944 | tf_op jit(solution)/shard_map/ppermute | solution.py:69
  225.0 1.5 collective-permute-start.57
  226.5 2.1 collective-permute-done.54
  230.4 3.2 %last_out.1 = (f32[96,3072]{1,0:T(8,128)}, f32[384,768]{1,0:T(8,128)}) custom-call(s32[2]{0:T(128)} %pad_add_fusion.idx_ref, bf16[2,2,48,768]{3,2,1,0:T(8,128)(2,1)} %copy-done.5, bf16[2,2,48,768]{3,2,1,0:T(8,128)(2,1)} %copy-done.13, bf16[2,2,48,768]{3,2,1,0:T(8,128)(2,1)} %copy-done.14, bf16[2,2,48,768]{3,2,1,0:T(8,128)(2,1)} %copy-done.15), custom_call_target="tpu_custom_call" | custom-call | tf_op jit(solution)/shard_map/last_out/pallas_call | solution.py:706
  233.7 1.5 collective-permute-done.57
  236.8 2.8 %collective-permute-done.61 = bf16[16,768]{1,0:T(8,128)(2,1)S(1)} collective-permute-done((bf16[16,768]{1,0:T(8,128)(2,1)S(1)}, bf16[16,768]{1,0:T(8,128)(2,1)S(1)}, u32[]{:S(2)}, u32[]{:S(2)}) %collective-permute-start.61) | collective-permute-done | bytes 24608 | tf_op jit(solution)/shard_map/ppermute | solution.py:69
  (256 shorter events, 56.3 us)
Async XLA Ops:
  1.8 14.4 %collective-permute-start = (bf16[1,96,768]{2,1,0:T(8,128)(2,1)S(1)}, bf16[1,96,768]{2,1,0:T(8,128)(2,1)S(1)}, u32[]{:S(2)}, u32[]{:S(2)}) collective-permute-start(bf16[1,96,768]{2,1,0:T(8,128)(2,1)S(1)} %bitcast.156), channel_id=1, source_target_pairs={{0,4},{1,5},{2,6},{3,7},{4,0},{5,1},{6,2},{7,3},{8,12},{9,13},{10,... | collective-permute-start | bytes 442376 | tf_op jit(solution)/shard_map/ppermute | solution.py:69
  16.2 8.3 %collective-permute-start.1 = (bf16[2,96,768]{2,1,0:T(8,128)(2,1)S(1)}, bf16[2,96,768]{2,1,0:T(8,128)(2,1)S(1)}, u32[]{:S(2)}, u32[]{:S(2)}) collective-permute-start(bf16[2,96,768]{2,1,0:T(8,128)(2,1)S(1)} %pad_maximum_fusion.8), channel_id=1, source_target_pairs={{0,2},{1,3},{2,0},{3,1},{4,6},{5,7},{6,4},{7,5},{8,10},{9,11},{10,... | collective-permute-start | bytes 884744 | tf_op jit(solution)/shard_map/ppermute | solution.py:69
  26.1 7.1 %collective-permute-start.6 = (bf16[4,48,768]{2,1,0:T(8,128)(2,1)S(1)}, bf16[4,48,768]{2,1,0:T(8,128)(2,1)S(1)}, u32[]{:S(2)}, u32[]{:S(2)}) collective-permute-start(bf16[4,48,768]{2,1,0:T(8,128)(2,1)S(1)} %pad_maximum_fusion.12), channel_id=1, source_target_pairs={{0,1},{1,0},{2,3},{3,2},{4,5},{5,4},{6,7},{7,6},{8,9},{9,8},{10,11... | collective-permute-start | bytes 884744 | tf_op jit(solution)/shard_map/ppermute | solution.py:69
  26.7 8.2 %collective-permute-start.8 = (bf16[4,48,768]{2,1,0:T(8,128)(2,1)S(1)}, bf16[4,48,768]{2,1,0:T(8,128)(2,1)S(1)}, u32[]{:S(2)}, u32[]{:S(2)}) collective-permute-start(bf16[4,48,768]{2,1,0:T(8,128)(2,1)S(1)} %pad_maximum_fusion.13), channel_id=1, source_target_pairs={{0,16},{8,24},{16,0},{24,8},{1,17},{9,25},{17,1},{25,9},{2,18},{10... | collective-permute-start | bytes 884744 | tf_op jit(solution)/shard_map/ppermute | solution.py:69
  30.0 8.9 %collective-permute-start.4 = (bf16[1,96,768]{2,1,0:T(8,128)(2,1)S(1)}, bf16[1,96,768]{2,1,0:T(8,128)(2,1)S(1)}, u32[]{:S(2)}, u32[]{:S(2)}) collective-permute-start(bf16[1,96,768]{2,1,0:T(8,128)(2,1)S(1)} %bitcast.161), channel_id=1, source_target_pairs={{0,4},{1,5},{2,6},{3,7},{4,0},{5,1},{6,2},{7,3},{8,12},{9,13},{10,... | collective-permute-start | bytes 442376 | tf_op jit(solution)/shard_map/ppermute | solution.py:69
  33.3 13.1 %collective-permute-start.7 = (bf16[8,48,768]{2,1,0:T(8,128)(2,1)S(1)}, bf16[8,48,768]{2,1,0:T(8,128)(2,1)S(1)}, u32[]{:S(2)}, u32[]{:S(2)}) collective-permute-start(bf16[8,48,768]{2,1,0:T(8,128)(2,1)S(1)} %pad_maximum_fusion.1.p0), channel_id=1, source_target_pairs={{0,16},{8,24},{16,0},{24,8},{1,17},{9,25},{17,1},{25,9},{2,18},{10... | collective-permute-start | bytes 1769480 | tf_op jit(solution)/shard_map/ppermute | solution.py:69
  35.0 12.3 %collective-permute-start.9 = (bf16[8,48,768]{2,1,0:T(8,128)(2,1)S(1)}, bf16[8,48,768]{2,1,0:T(8,128)(2,1)S(1)}, u32[]{:S(2)}, u32[]{:S(2)}) collective-permute-start(bf16[8,48,768]{2,1,0:T(8,128)(2,1)S(1)} %pad_maximum_fusion.2.p2), channel_id=1, source_target_pairs={{0,1},{1,0},{2,3},{3,2},{4,5},{5,4},{6,7},{7,6},{8,9},{9,8},{10,11... | collective-permute-start | bytes 1769480 | tf_op jit(solution)/shard_map/ppermute | solution.py:69
  39.0 9.5 %collective-permute-start.5 = (bf16[2,96,768]{2,1,0:T(8,128)(2,1)S(1)}, bf16[2,96,768]{2,1,0:T(8,128)(2,1)S(1)}, u32[]{:S(2)}, u32[]{:S(2)}) collective-permute-start(bf16[2,96,768]{2,1,0:T(8,128)(2,1)S(1)} %pad_maximum_fusion.11), channel_id=1, source_target_pairs={{0,2},{1,3},{2,0},{3,1},{4,6},{5,7},{6,4},{7,5},{8,10},{9,11},{10,... | collective-permute-start | bytes 884744 | tf_op jit(solution)/shard_map/ppermute | solution.py:69
  39.4 7.1 %collective-permute-start.10 = (bf16[1,96,768]{2,1,0:T(8,128)(2,1)S(1)}, bf16[1,96,768]{2,1,0:T(8,128)(2,1)S(1)}, u32[]{:S(2)}, u32[]{:S(2)}) collective-permute-start(bf16[1,96,768]{2,1,0:T(8,128)(2,1)S(1)} %dynamic-slice_bitcast_fusion), channel_id=1, source_target_pairs={{0,4},{1,5},{2,6},{3,7},{4,0},{5,1},{6,2},{7,3},{8,12},{9,13},{10,... | collective-permute-start | bytes 442376 | tf_op jit(solution)/shard_map/ppermute | solution.py:69
  48.5 27.9 %collective-permute-start.22 = (bf16[2,96,768]{2,1,0:T(8,128)(2,1)S(1)}, bf16[2,96,768]{2,1,0:T(8,128)(2,1)S(1)}, u32[]{:S(2)}, u32[]{:S(2)}) collective-permute-start(bf16[2,96,768]{2,1,0:T(8,128)(2,1)S(1)} %pad_maximum_fusion.16), channel_id=1, source_target_pairs={{0,2},{1,3},{2,0},{3,1},{4,6},{5,7},{6,4},{7,5},{8,10},{9,11},{10,... | collective-permute-start | bytes 884744 | tf_op jit(solution)/shard_map/ppermute | solution.py:69
  50.5 12.1 %collective-permute-start.16 = (bf16[4,48,768]{2,1,0:T(8,128)(2,1)S(1)}, bf16[4,48,768]{2,1,0:T(8,128)(2,1)S(1)}, u32[]{:S(2)}, u32[]{:S(2)}) collective-permute-start(bf16[4,48,768]{2,1,0:T(8,128)(2,1)S(1)} %pad_maximum_fusion.14), channel_id=1, source_target_pairs={{0,1},{1,0},{2,3},{3,2},{4,5},{5,4},{6,7},{7,6},{8,9},{9,8},{10,11... | collective-permute-start | bytes 884744 | tf_op jit(solution)/shard_map/ppermute | solution.py:69
  51.6 11.1 %collective-permute-start.17 = (bf16[4,48,768]{2,1,0:T(8,128)(2,1)S(1)}, bf16[4,48,768]{2,1,0:T(8,128)(2,1)S(1)}, u32[]{:S(2)}, u32[]{:S(2)}) collective-permute-start(bf16[4,48,768]{2,1,0:T(8,128)(2,1)S(1)} %pad_maximum_fusion.15), channel_id=1, source_target_pairs={{0,16},{8,24},{16,0},{24,8},{1,17},{9,25},{17,1},{25,9},{2,18},{10... | collective-permute-start | bytes 884744 | tf_op jit(solution)/shard_map/ppermute | solution.py:69
  62.9 15.9 %collective-permute-start.18 = (bf16[8,48,768]{2,1,0:T(8,128)(2,1)S(1)}, bf16[8,48,768]{2,1,0:T(8,128)(2,1)S(1)}, u32[]{:S(2)}, u32[]{:S(2)}) collective-permute-start(bf16[8,48,768]{2,1,0:T(8,128)(2,1)S(1)} %pad_maximum_fusion.3.p0), channel_id=1, source_target_pairs={{0,16},{8,24},{16,0},{24,8},{1,17},{9,25},{17,1},{25,9},{2,18},{10... | collective-permute-start | bytes 1769480 | tf_op jit(solution)/shard_map/ppermute | solution.py:69
  64.4 15.8 %collective-permute-start.19 = (bf16[8,48,768]{2,1,0:T(8,128)(2,1)S(1)}, bf16[8,48,768]{2,1,0:T(8,128)(2,1)S(1)}, u32[]{:S(2)}, u32[]{:S(2)}) collective-permute-start(bf16[8,48,768]{2,1,0:T(8,128)(2,1)S(1)} %pad_maximum_fusion.4.p2), channel_id=1, source_target_pairs={{0,1},{1,0},{2,3},{3,2},{4,5},{5,4},{6,7},{7,6},{8,9},{9,8},{10,11... | collective-permute-start | bytes 1769480 | tf_op jit(solution)/shard_map/ppermute | solution.py:69
  65.5 14.8 %collective-permute-start.20 = (bf16[8,48,768]{2,1,0:T(8,128)(2,1)S(1)}, bf16[8,48,768]{2,1,0:T(8,128)(2,1)S(1)}, u32[]{:S(2)}, u32[]{:S(2)}) collective-permute-start(bf16[8,48,768]{2,1,0:T(8,128)(2,1)S(1)} %pad_maximum_fusion.3.p0), channel_id=1, source_target_pairs={{0,8},{8,0},{16,24},{24,16},{1,9},{9,1},{17,25},{25,17},{2,10},{10... | collective-permute-start | bytes 1769480 | tf_op jit(solution)/shard_map/ppermute | solution.py:69
  65.5 15.3 %collective-permute-start.21 = (bf16[8,48,768]{2,1,0:T(8,128)(2,1)S(1)}, bf16[8,48,768]{2,1,0:T(8,128)(2,1)S(1)}, u32[]{:S(2)}, u32[]{:S(2)}) collective-permute-start(bf16[8,48,768]{2,1,0:T(8,128)(2,1)S(1)} %pad_maximum_fusion.4.p2), channel_id=1, source_target_pairs={{0,8},{8,0},{16,24},{24,16},{1,9},{9,1},{17,25},{25,17},{2,10},{10... | collective-permute-start | bytes 1769480 | tf_op jit(solution)/shard_map/ppermute | solution.py:69
  76.5 9.5 %collective-permute-start.23 = (bf16[4,48,768]{2,1,0:T(8,128)(2,1)S(1)}, bf16[4,48,768]{2,1,0:T(8,128)(2,1)S(1)}, u32[]{:S(2)}, u32[]{:S(2)}) collective-permute-start(bf16[4,48,768]{2,1,0:T(8,128)(2,1)S(1)} %pad_maximum_fusion.17), channel_id=1, source_target_pairs={{0,1},{1,0},{2,3},{3,2},{4,5},{5,4},{6,7},{7,6},{8,9},{9,8},{10,11... | collective-permute-start | bytes 884744 | tf_op jit(solution)/shard_map/ppermute | solution.py:69
  78.7 8.6 %collective-permute-start.24 = (bf16[4,48,768]{2,1,0:T(8,128)(2,1)S(1)}, bf16[4,48,768]{2,1,0:T(8,128)(2,1)S(1)}, u32[]{:S(2)}, u32[]{:S(2)}) collective-permute-start(bf16[4,48,768]{2,1,0:T(8,128)(2,1)S(1)} %pad_maximum_fusion.18), channel_id=1, source_target_pairs={{0,16},{8,24},{16,0},{24,8},{1,17},{9,25},{17,1},{25,9},{2,18},{10... | collective-permute-start | bytes 884744 | tf_op jit(solution)/shard_map/ppermute | solution.py:69
  80.2 9.5 %collective-permute-start.25 = (bf16[8,48,768]{2,1,0:T(8,128)(2,1)S(1)}, bf16[8,48,768]{2,1,0:T(8,128)(2,1)S(1)}, u32[]{:S(2)}, u32[]{:S(2)}) collective-permute-start(bf16[8,48,768]{2,1,0:T(8,128)(2,1)S(1)} %collective-permute-done.18.p1), channel_id=1, source_target_pairs={{0,8},{8,0},{16,24},{24,16},{1,9},{9,1},{17,25},{25,17},{2,10},{10... | collective-permute-start | bytes 1769480 | tf_op jit(solution)/shard_map/ppermute | solution.py:69
  80.3 9.5 %collective-permute-start.26 = (bf16[8,48,768]{2,1,0:T(8,128)(2,1)S(1)}, bf16[8,48,768]{2,1,0:T(8,128)(2,1)}, u32[]{:S(2)}, u32[]{:S(2)}) collective-permute-start(bf16[8,48,768]{2,1,0:T(8,128)(2,1)S(1)} %collective-permute-done.19.p3), channel_id=1, source_target_pairs={{0,8},{8,0},{16,24},{24,16},{1,9},{9,1},{17,25},{25,17},{2,10},{10... | collective-permute-start | bytes 1769480 | tf_op jit(solution)/shard_map/ppermute | solution.py:69
  87.5 25.6 %collective-permute-start.28 = (bf16[8,48,768]{2,1,0:T(8,128)(2,1)S(1)}, bf16[8,48,768]{2,1,0:T(8,128)(2,1)}, u32[]{:S(2)}, u32[]{:S(2)}) collective-permute-start(bf16[8,48,768]{2,1,0:T(8,128)(2,1)S(1)} %pad_maximum_fusion.5.p0), channel_id=1, source_target_pairs={{0,8},{8,0},{16,24},{24,16},{1,9},{9,1},{17,25},{25,17},{2,10},{10... | collective-permute-start | bytes 1769480 | tf_op jit(solution)/shard_map/ppermute | solution.py:69
  87.5 21.3 %collective-permute-start.29 = (bf16[8,48,768]{2,1,0:T(8,128)(2,1)S(1)}, bf16[8,48,768]{2,1,0:T(8,128)(2,1)S(1)}, u32[]{:S(2)}, u32[]{:S(2)}) collective-permute-start(bf16[8,48,768]{2,1,0:T(8,128)(2,1)S(1)} %pad_maximum_fusion.5.p0), channel_id=1, source_target_pairs={{0,16},{8,24},{16,0},{24,8},{1,17},{9,25},{17,1},{25,9},{2,18},{10... | collective-permute-start | bytes 1769480 | tf_op jit(solution)/shard_map/ppermute | solution.py:69
  88.6 20.2 %collective-permute-start.30 = (bf16[8,48,768]{2,1,0:T(8,128)(2,1)S(1)}, bf16[8,48,768]{2,1,0:T(8,128)(2,1)S(1)}, u32[]{:S(2)}, u32[]{:S(2)}) collective-permute-start(bf16[8,48,768]{2,1,0:T(8,128)(2,1)S(1)} %pad_maximum_fusion.6.p2), channel_id=1, source_target_pairs={{0,1},{1,0},{2,3},{3,2},{4,5},{5,4},{6,7},{7,6},{8,9},{9,8},{10,11... | collective-permute-start | bytes 1769480 | tf_op jit(solution)/shard_map/ppermute | solution.py:69
  89.7 24.0 %collective-permute-start.32 = (bf16[8,48,768]{2,1,0:T(8,128)(2,1)S(1)}, bf16[8,48,768]{2,1,0:T(8,128)(2,1)}, u32[]{:S(2)}, u32[]{:S(2)}) collective-permute-start(bf16[8,48,768]{2,1,0:T(8,128)(2,1)S(1)} %pad_maximum_fusion.6.p2), channel_id=1, source_target_pairs={{0,8},{8,0},{16,24},{24,16},{1,9},{9,1},{17,25},{25,17},{2,10},{10... | collective-permute-start | bytes 1769480 | tf_op jit(solution)/shard_map/ppermute | solution.py:69
  99.7 9.8 %collective-permute-start.27 = (bf16[2,2,8,48,768]{4,3,2,1,0:T(8,128)(2,1)}, bf16[2,2,8,48,768]{4,3,2,1,0:T(8,128)(2,1)S(1)}, u32[]{:S(2)}, u32[]{:S(2)}) collective-permute-start(bf16[2,2,8,48,768]{4,3,2,1,0:T(8,128)(2,1)} %get-tuple-element.140), channel_id=1, source_target_pairs={{0,8},{8,0},{16,24},{24,16},{1,9},{9,1},{17,25},{25,17},{2,10},{10... | collective-permute-start | bytes 7077896 | tf_op jit(solution)/shard_map/ppermute | solution.py:69
  111.3 15.7 %collective-permute-start.34 = (bf16[8,48,768]{2,1,0:T(8,128)(2,1)S(1)}, bf16[8,48,768]{2,1,0:T(8,128)(2,1)S(1)}, u32[]{:S(2)}, u32[]{:S(2)}) collective-permute-start(bf16[8,48,768]{2,1,0:T(8,128)(2,1)S(1)} %get-tuple-element.232), channel_id=1, source_target_pairs={{0,16},{8,24},{16,0},{24,8},{1,17},{9,25},{17,1},{25,9},{2,18},{10... | collective-permute-start | bytes 1769480 | tf_op jit(solution)/shard_map/ppermute | solution.py:69
  113.0 15.5 %collective-permute-start.35 = (bf16[2,4,48,768]{3,2,1,0:T(8,128)(2,1)S(1)}, bf16[2,4,48,768]{3,2,1,0:T(8,128)(2,1)S(1)}, u32[]{:S(2)}, u32[]{:S(2)}) collective-permute-start(bf16[2,4,48,768]{3,2,1,0:T(8,128)(2,1)S(1)} %get-tuple-element.230), channel_id=1, source_target_pairs={{0,1},{1,0},{2,3},{3,2},{4,5},{5,4},{6,7},{7,6},{8,9},{9,8},{10,11... | collective-permute-start | bytes 1769480 | tf_op jit(solution)/shard_map/ppermute | solution.py:69
  125.2 17.8 %collective-permute-start.36 = (bf16[2,2,8,48,768]{4,3,2,1,0:T(8,128)(2,1)}, bf16[2,2,8,48,768]{4,3,2,1,0:T(8,128)(2,1)S(1)}, u32[]{:S(2)}, u32[]{:S(2)}) collective-permute-start(bf16[2,2,8,48,768]{4,3,2,1,0:T(8,128)(2,1)} %get-tuple-element.150), channel_id=1, source_target_pairs={{0,8},{8,0},{16,24},{24,16},{1,9},{9,1},{17,25},{25,17},{2,10},{10... | collective-permute-start | bytes 7077896 | tf_op jit(solution)/shard_map/ppermute | solution.py:69
  128.6 12.1 %collective-permute-start.39 = (bf16[4,48,768]{2,1,0:T(8,128)(2,1)S(1)}, bf16[4,48,768]{2,1,0:T(8,128)(2,1)S(1)}, u32[]{:S(2)}, u32[]{:S(2)}) collective-permute-start(bf16[4,48,768]{2,1,0:T(8,128)(2,1)S(1)} %get-tuple-element.240), channel_id=1, source_target_pairs={{0,1},{1,0},{2,3},{3,2},{4,5},{5,4},{6,7},{7,6},{8,9},{9,8},{10,11... | collective-permute-start | bytes 884744 | tf_op jit(solution)/shard_map/ppermute | solution.py:69
  129.3 11.4 %collective-permute-start.40 = (bf16[4,48,768]{2,1,0:T(8,128)(2,1)S(1)}, bf16[4,48,768]{2,1,0:T(8,128)(2,1)S(1)}, u32[]{:S(2)}, u32[]{:S(2)}) collective-permute-start(bf16[4,48,768]{2,1,0:T(8,128)(2,1)S(1)} %get-tuple-element.238), channel_id=1, source_target_pairs={{0,16},{8,24},{16,0},{24,8},{1,17},{9,25},{17,1},{25,9},{2,18},{10... | collective-permute-start | bytes 884744 | tf_op jit(solution)/shard_map/ppermute | solution.py:69
  140.8 9.4 %collective-permute-start.41 = (bf16[2,2,48,768]{3,2,1,0:T(8,128)(2,1)S(1)}, bf16[2,2,48,768]{3,2,1,0:T(8,128)(2,1)S(1)}, u32[]{:S(2)}, u32[]{:S(2)}) collective-permute-start(bf16[2,2,48,768]{3,2,1,0:T(8,128)(2,1)S(1)} %fusion.11), channel_id=1, source_target_pairs={{0,2},{1,3},{2,0},{3,1},{4,6},{5,7},{6,4},{7,5},{8,10},{9,11},{10,... | collective-permute-start | bytes 884744 | tf_op jit(solution)/shard_map/ppermute | solution.py:69
  143.2 20.8 %collective-permute-start.37 = (bf16[8,48,768]{2,1,0:T(8,128)(2,1)S(1)}, bf16[8,48,768]{2,1,0:T(8,128)(2,1)S(1)}, u32[]{:S(2)}, u32[]{:S(2)}) collective-permute-start(bf16[8,48,768]{2,1,0:T(8,128)(2,1)S(1)} %get-tuple-element.226), channel_id=1, source_target_pairs={{0,16},{8,24},{16,0},{24,8},{1,17},{9,25},{17,1},{25,9},{2,18},{10... | collective-permute-start | bytes 1769480 | tf_op jit(solution)/shard_map/ppermute | solution.py:69
  143.9 20.2 %collective-permute-start.38 = (bf16[2,4,48,768]{3,2,1,0:T(8,128)(2,1)S(1)}, bf16[2,4,48,768]{3,2,1,0:T(8,128)(2,1)S(1)}, u32[]{:S(2)}, u32[]{:S(2)}) collective-permute-start(bf16[2,4,48,768]{3,2,1,0:T(8,128)(2,1)S(1)} %get-tuple-element.227), channel_id=1, source_target_pairs={{0,1},{1,0},{2,3},{3,2},{4,5},{5,4},{6,7},{7,6},{8,9},{9,8},{10,11... | collective-permute-start | bytes 1769480 | tf_op jit(solution)/shard_map/ppermute | solution.py:69
  150.3 13.1 %collective-permute-start.44 = (bf16[1,2,48,768]{3,2,1,0:T(8,128)(2,1)S(1)}, bf16[1,2,48,768]{3,2,1,0:T(8,128)(2,1)S(1)}, u32[]{:S(2)}, u32[]{:S(2)}) collective-permute-start(bf16[1,2,48,768]{3,2,1,0:T(8,128)(2,1)S(1)} %slice.380), channel_id=1, source_target_pairs={{0,4},{1,5},{2,6},{3,7},{4,0},{5,1},{6,2},{7,3},{8,12},{9,13},{10,... | collective-permute-start | bytes 442376 | tf_op jit(solution)/shard_map/ppermute | solution.py:69
  164.1 7.9 %collective-permute-start.42 = (bf16[4,48,768]{2,1,0:T(8,128)(2,1)S(1)}, bf16[4,48,768]{2,1,0:T(8,128)(2,1)S(1)}, u32[]{:S(2)}, u32[]{:S(2)}) collective-permute-start(bf16[4,48,768]{2,1,0:T(8,128)(2,1)S(1)} %get-tuple-element.234), channel_id=1, source_target_pairs={{0,1},{1,0},{2,3},{3,2},{4,5},{5,4},{6,7},{7,6},{8,9},{9,8},{10,11... | collective-permute-start | bytes 884744 | tf_op jit(solution)/shard_map/ppermute | solution.py:69
  164.9 7.1 %collective-permute-start.43 = (bf16[4,48,768]{2,1,0:T(8,128)(2,1)S(1)}, bf16[4,48,768]{2,1,0:T(8,128)(2,1)S(1)}, u32[]{:S(2)}, u32[]{:S(2)}) collective-permute-start(bf16[4,48,768]{2,1,0:T(8,128)(2,1)S(1)} %get-tuple-element.235), channel_id=1, source_target_pairs={{0,16},{8,24},{16,0},{24,8},{1,17},{9,25},{17,1},{25,9},{2,18},{10... | collective-permute-start | bytes 884744 | tf_op jit(solution)/shard_map/ppermute | solution.py:69
  172.0 7.1 %collective-permute-start.46 = (bf16[2,2,8,48,768]{4,3,2,1,0:T(8,128)(2,1)}, bf16[2,2,8,48,768]{4,3,2,1,0:T(8,128)(2,1)S(1)}, u32[]{:S(2)}, u32[]{:S(2)}) collective-permute-start(bf16[2,2,8,48,768]{4,3,2,1,0:T(8,128)(2,1)} %first_grad.2), channel_id=1, source_target_pairs={{0,8},{8,0},{16,24},{24,16},{1,9},{9,1},{17,25},{25,17},{2,10},{10... | collective-permute-start | bytes 7077896 | tf_op jit(solution)/shard_map/ppermute | solution.py:69
  172.2 9.5 %collective-permute-start.45 = (bf16[2,2,48,768]{3,2,1,0:T(8,128)(2,1)S(1)}, bf16[2,2,48,768]{3,2,1,0:T(8,128)(2,1)S(1)}, u32[]{:S(2)}, u32[]{:S(2)}) collective-permute-start(bf16[2,2,48,768]{3,2,1,0:T(8,128)(2,1)S(1)} %pad_maximum_fusion.9), channel_id=1, source_target_pairs={{0,2},{1,3},{2,0},{3,1},{4,6},{5,7},{6,4},{7,5},{8,10},{9,11},{10,... | collective-permute-start | bytes 884744 | tf_op jit(solution)/shard_map/ppermute | solution.py:69
  181.7 12.2 %collective-permute-start.47 = (bf16[1,2,48,768]{3,2,1,0:T(8,128)(2,1)S(1)}, bf16[1,2,48,768]{3,2,1,0:T(8,128)(2,1)S(1)}, u32[]{:S(2)}, u32[]{:S(2)}) collective-permute-start(bf16[1,2,48,768]{3,2,1,0:T(8,128)(2,1)S(1)} %slice.397), channel_id=1, source_target_pairs={{0,4},{1,5},{2,6},{3,7},{4,0},{5,1},{6,2},{7,3},{8,12},{9,13},{10,... | collective-permute-start | bytes 442376 | tf_op jit(solution)/shard_map/ppermute | solution.py:69
  183.3 17.5 %collective-permute-start.49 = (bf16[8,48,768]{2,1,0:T(8,128)(2,1)S(1)}, bf16[8,48,768]{2,1,0:T(8,128)(2,1)S(1)}, u32[]{:S(2)}, u32[]{:S(2)}) collective-permute-start(bf16[8,48,768]{2,1,0:T(8,128)(2,1)S(1)} %get-tuple-element.224), channel_id=1, source_target_pairs={{0,16},{8,24},{16,0},{24,8},{1,17},{9,25},{17,1},{25,9},{2,18},{10... | collective-permute-start | bytes 1769480 | tf_op jit(solution)/shard_map/ppermute | solution.py:69
  184.2 16.6 %collective-permute-start.50 = (bf16[2,4,48,768]{3,2,1,0:T(8,128)(2,1)S(1)}, bf16[2,4,48,768]{3,2,1,0:T(8,128)(2,1)S(1)}, u32[]{:S(2)}, u32[]{:S(2)}) collective-permute-start(bf16[2,4,48,768]{3,2,1,0:T(8,128)(2,1)S(1)} %get-tuple-element.222), channel_id=1, source_target_pairs={{0,1},{1,0},{2,3},{3,2},{4,5},{5,4},{6,7},{7,6},{8,9},{9,8},{10,11... | collective-permute-start | bytes 1769480 | tf_op jit(solution)/shard_map/ppermute | solution.py:69
  200.8 9.5 %collective-permute-start.52 = (bf16[4,48,768]{2,1,0:T(8,128)(2,1)S(1)}, bf16[4,48,768]{2,1,0:T(8,128)(2,1)S(1)}, u32[]{:S(2)}, u32[]{:S(2)}) collective-permute-start(bf16[4,48,768]{2,1,0:T(8,128)(2,1)S(1)} %fusion.19), channel_id=1, source_target_pairs={{0,1},{1,0},{2,3},{3,2},{4,5},{5,4},{6,7},{7,6},{8,9},{9,8},{10,11... | collective-permute-start | bytes 884744 | tf_op jit(solution)/shard_map/ppermute | solution.py:69
  202.1 9.2 %collective-permute-start.53 = (bf16[4,48,768]{2,1,0:T(8,128)(2,1)S(1)}, bf16[4,48,768]{2,1,0:T(8,128)(2,1)S(1)}, u32[]{:S(2)}, u32[]{:S(2)}) collective-permute-start(bf16[4,48,768]{2,1,0:T(8,128)(2,1)S(1)} %fusion.18), channel_id=1, source_target_pairs={{0,16},{8,24},{16,0},{24,8},{1,17},{9,25},{17,1},{25,9},{2,18},{10... | collective-permute-start | bytes 884744 | tf_op jit(solution)/shard_map/ppermute | solution.py:69
  212.5 8.0 %collective-permute-start.55 = (bf16[2,2,48,768]{3,2,0,1:T(8,128)(2,1)S(1)}, bf16[2,2,48,768]{3,2,0,1:T(8,128)(2,1)S(1)}, u32[]{:S(2)}, u32[]{:S(2)}) collective-permute-start(bf16[2,2,48,768]{3,2,0,1:T(8,128)(2,1)S(1)} %fusion.12), channel_id=1, source_target_pairs={{0,2},{1,3},{2,0},{3,1},{4,6},{5,7},{6,4},{7,5},{8,10},{9,11},{10,... | collective-permute-start | bytes 884744 | tf_op jit(solution)/shard_map/ppermute | solution.py:69
  214.1 14.9 %collective-permute-start.58 = (bf16[2,2,48,768]{3,2,1,0:T(8,128)(2,1)S(1)}, bf16[2,2,48,768]{3,2,1,0:T(8,128)(2,1)S(1)}, u32[]{:S(2)}, u32[]{:S(2)}) collective-permute-start(bf16[2,2,48,768]{3,2,1,0:T(8,128)(2,1)S(1)} %pad_maximum_fusion.19.p0), channel_id=1, source_target_pairs={{0,8},{8,0},{16,24},{24,16},{1,9},{9,1},{17,25},{25,17},{2,10},{10... | collective-permute-start | bytes 884744 | tf_op jit(solution)/shard_map/ppermute | solution.py:69
  214.2 9.4 %collective-permute-start.59 = (bf16[2,2,48,768]{3,2,1,0:T(8,128)(2,1)S(1)}, bf16[2,2,48,768]{3,2,1,0:T(8,128)(2,1)S(1)}, u32[]{:S(2)}, u32[]{:S(2)}) collective-permute-start(bf16[2,2,48,768]{3,2,1,0:T(8,128)(2,1)S(1)} %pad_maximum_fusion.19.p0), channel_id=1, source_target_pairs={{0,16},{8,24},{16,0},{24,8},{1,17},{9,25},{17,1},{25,9},{2,18},{10... | collective-permute-start | bytes 884744 | tf_op jit(solution)/shard_map/ppermute | solution.py:69
  225.0 10.1 %collective-permute-start.57 = (bf16[1,2,48,768]{3,2,0,1:T(8,128)(2,1)S(1)}, bf16[1,2,48,768]{3,2,0,1:T(8,128)(2,1)S(1)}, u32[]{:S(2)}, u32[]{:S(2)}) collective-permute-start(bf16[1,2,48,768]{3,2,0,1:T(8,128)(2,1)S(1)} %slice.406), channel_id=1, source_target_pairs={{0,4},{1,5},{2,6},{3,7},{4,0},{5,1},{6,2},{7,3},{8,12},{9,13},{10,... | collective-permute-start | bytes 442376 | tf_op jit(solution)/shard_map/ppermute | solution.py:69
  228.7 7.0 %collective-permute-start.56 = (bf16[16,768]{1,0:T(8,128)(2,1)S(1)}, bf16[16,768]{1,0:T(8,128)(2,1)S(1)}, u32[]{:S(2)}, u32[]{:S(2)}) collective-permute-start(bf16[16,768]{1,0:T(8,128)(2,1)S(1)} %fusion.37), channel_id=1, source_target_pairs={{0,2},{1,3},{2,0},{3,1},{4,6},{5,7},{6,4},{7,5},{8,10},{9,11},{10,... | collective-permute-start | bytes 73736 | tf_op jit(solution)/shard_map/ppermute | solution.py:69
  (51 other events, 340.5 us)
where the time goes:
time: 247 us; the launch traced here: 246 us
  Pallas kernels  107 us (43%)
  starting transfers between devices  58.9 us (24%)
  waiting for transfers between devices  46.3 us (19%)
  other arithmetic  16.4 us (7%)
  local copies, waits for them, and re-layouts  14.9 us (6%)
    ppermute x65, starting transfers between devices, swap(): return lax.ppermute(values, axis, [(i, i ^ mask) for i in range(size)])  58.9 us
    ppermute x65, waiting for transfers between devices, swap(): return lax.ppermute(values, axis, [(i, i ^ mask) for i in range(size)])  46.3 us
    pallas_call x2, Pallas kernels, act_grad(): pl.pallas_call(partial(act_grad_kernel, masks, maps, rs, h, shards, befor...  20.1 us
    pallas_call x2, Pallas kernels, up(): pl.pallas_call(partial(up_kernel, masks, maps, rs, h, shards), grid=(2,),...  18.1 us
    pallas_call x1, Pallas kernels, attend_back(): pl.pallas_call(attend_back_kernel, grid=(d // pair,), out_shape=jax.Shape...  11.6 us
    pallas_call x2, Pallas kernels, first_grad(): pl.pallas_call(partial(first_grad_kernel, masks, h, shards, rs), grid_spe...  10.9 us
    pallas_call x1, Pallas kernels, attend(): pl.pallas_call(attend_kernel, grid=(d // pair,), out_shape=(jax.ShapeDtyp...  10.4 us
    pallas_call x1, Pallas kernels, qkv(): pl.pallas_call(partial(qkv_kernel, maps, h), grid=(3,), out_shape=(jax.Sh...  9.42 us
  transfers between devices with their start and end apart: 65, of which 23 were waited for; matrix products, arithmetic and copies ran while one was open for 9% of the time, Pallas kernels for 44%

commit v1 on v0

--- a/solution.py
+++ b/solution.py
@@ -18,7 +18,7 @@
 F32 = jnp.float32
 SMALL = 16
 SPAN = 4.8e10
-VMEM_LIMIT = 56 * 1024 * 1024
+VMEM_LIMIT = 16 * 1024 * 1024
 
 
 def row_layout(length_row, row_count, slot_count):
@@ -137,90 +137,55 @@
     ]
 
 
-def fetch(pieces, maps, me_f, h, w_ref, slot_of, sems):
+def place(pieces, maps, me_f, h, w_ref, slot_of):
     for ref, entries in zip(pieces, maps):
         for at, r, k, colour in entries:
-            slot = slot_of(r)
-            pltpu.make_async_copy(
-                ref.at[at],
-                w_ref.at[slot, me_f ^ k, pl.ds(colour * h, h)],
-                sems.at[slot],
-            ).start()
-
-
-def fetched(w_ref, slot, sems):
-    pltpu.make_async_copy(w_ref.at[slot], w_ref.at[slot], sems.at[slot]).wait()
+            w_ref[slot_of(r), me_f ^ k, colour * h : (colour + 1) * h, :] = ref[at]
+
+
+def times(count, body):
+    def step(g, carry):
+        body(g)
+        return carry
+
+    lax.fori_loop(0, count, step, 0)
+
+
+def vmem(count):
+    return [pl.BlockSpec(memory_space=pltpu.VMEM)] * count
 
 
 def qkv_kernel(
     maps, h, idx_ref, x_ref, small_ref, cos_ref, sin_ref, p0, p1, p2, p3, p4, p5, p6, p7,
-    normed_ref, out_ref, w_out, keep, w_ref, sems, out_sems,
+    normed_ref, out_ref, w_ref,
 ):
-    g = pl.program_id(0)
     d4, me_f = idx_ref[0], idx_ref[1]
-    d = keep.shape[1]
-
-    def send(slot):
-        return pltpu.make_async_copy(w_ref.at[slot], w_out.at[slot], out_sems.at[slot])
-
-    @pl.when(g == 0)
-    def _():
-        fetch((p0, p1, p2, p3, p4, p5, p6, p7), maps, me_f, h, w_ref, lambda r: d4 ^ r, sems)
-        unit, _ = norm_parts(x_ref[...].astype(F32))
-        normed = (unit * small_ref[0:1, :] + small_ref[1:2, :]).astype(BF)
-        keep[...] = normed
-        normed_ref[...] = normed
-
-    fetched(w_ref, g, sems)
-    send(g).start()
-
-    @pl.when(g == 2)
-    def _():
-        fetched(w_ref, 3, sems)
-        send(3).start()
-
-    product = dot(keep[...], w_ref[g].reshape(d, d))
-
-    @pl.when(g < 2)
-    def _():
-        out_ref[0] = turn(product, cos_ref[...], sin_ref[...]).astype(BF)
-
-    @pl.when(g == 2)
-    def _():
-        out_ref[0] = product.astype(BF)
-        for slot in range(4):
-            send(slot).wait()
+    d = x_ref.shape[1]
+    place((p0, p1, p2, p3, p4, p5, p6, p7), maps, me_f, h, w_ref, lambda r: d4 ^ r)
+    unit, _ = norm_parts(x_ref[...].astype(F32))
+    normed_ref[...] = (unit * small_ref[0:1, :] + small_ref[1:2, :]).astype(BF)
+
+    def product(g):
+        return dot(normed_ref[...], w_ref[g].reshape(d, d))
+
+    def turned(g):
+        out_ref[g] = turn(product(g), cos_ref[...], sin_ref[...]).astype(BF)
+
+    times(2, turned)
+    out_ref[2] = product(2).astype(BF)
 
 
 def qkv(idx, x, small, cosine, sine, pieces, maps, shards, h):
     n, d = x.shape
     return pl.pallas_call(
         partial(qkv_kernel, maps, h),
-        grid=(3,),
         out_shape=(
             jax.ShapeDtypeStruct((n, d), BF),
             jax.ShapeDtypeStruct((3, n, d), BF),
             jax.ShapeDtypeStruct((4, shards, 2 * h, d), BF),
         ),
-        in_specs=[
-            pl.BlockSpec(memory_space=pltpu.SMEM),
-            pl.BlockSpec((n, d), lambda g: (0, 0)),
-            pl.BlockSpec(small.shape, lambda g: (0, 0)),
-            pl.BlockSpec(cosine.shape, lambda g: (0, 0)),
-            pl.BlockSpec(sine.shape, lambda g: (0, 0)),
-        ]
-        + [pl.BlockSpec(memory_space=pl.ANY)] * 8,
-        out_specs=(
-            pl.BlockSpec((n, d), lambda g: (0, 0)),
-            pl.BlockSpec((1, n, d), lambda g: (g, 0, 0)),
-            pl.BlockSpec(memory_space=pl.ANY),
-        ),
-        scratch_shapes=[
-            pltpu.VMEM((n, d), BF),
-            pltpu.VMEM((4, shards, 2 * h, d), BF),
-            pltpu.SemaphoreType.DMA((4,)),
-            pltpu.SemaphoreType.DMA((4,)),
-        ],
+        in_specs=[pl.BlockSpec(memory_space=pltpu.SMEM)] + vmem(12),
+        out_specs=tuple(vmem(3)),
         compiler_params=params(),
         cost_estimate=cost(6 * n * d * d, 2 * (5 * n * d + 8 * d * d)),
         name="qkv",
@@ -352,83 +317,55 @@
     )(x, mixed, weights, small)
 
 
-def spread(out_ref, keep, product, me_f, masks, h, shards):
+def spread(out_ref, g, keep, product, me_f, masks, h, shards):
     keep[...] = product.astype(BF)
     for i in range(shards):
         j = me_f ^ bits_of(i, masks)
         for colour in range(2):
             start = pl.multiple_of(j * (2 * h) + colour * h, h & -h)
-            out_ref[0, colour, i] = keep[pl.ds(start, h), :]
+            out_ref[g, colour, i] = keep[pl.ds(start, h), :]
 
 
 def up_kernel(
     masks, maps, rs, h, shards, idx_ref, hidden_ref, c_ref, small_ref, p0, p1, p2, p3,
-    act_ref, slope_ref, grad_ref, w_out, w_ref, keep, sems, out_sems,
+    act_ref, slope_ref, grad_ref, w_ref, keep,
 ):
-    g = pl.program_id(0)
     d4, me_f = idx_ref[0], idx_ref[1]
     d = hidden_ref.shape[1]
-
-    def send(slot):
-        return pltpu.make_async_copy(w_ref.at[slot], w_out.at[slot], out_sems.at[slot])
-
-    @pl.when(g == 0)
-    def _():
-        fetch((p0, p1, p2, p3), maps, me_f, h, w_ref, rs.index, sems)
-
-    fetched(w_ref, g, sems)
-    send(g).start()
-    chunk = d4 ^ jnp.where(g == 0, rs[0], rs[1])
-    bias = small_ref[5:6, :]
-    for other in range(1, 4):
-        bias = jnp.where(chunk == other, small_ref[5 + other : 6 + other, :], bias)
-    v = dot(hidden_ref[...], w_ref[g].reshape(d, d)) + bias
-    c = math.sqrt(2.0 / math.pi)
-    square = v * v
-    t = jnp.tanh(v * (c + (c * 0.044715) * square))
-    half = 0.5 * (1.0 + t)
-    act = (v * half).astype(BF)
-    act_ref[0] = act
-    slope = half + (0.5 * v) * (1.0 - t * t) * (c + (3.0 * c * 0.044715) * square)
-    slope_ref[0] = slope.astype(BF)
-    spread(grad_ref, keep, dot_tn(act, c_ref[...]), me_f, masks, h, shards)
-
-    @pl.when(g == 1)
-    def _():
-        send(0).wait()
-        send(1).wait()
+    place((p0, p1, p2, p3), maps, me_f, h, w_ref, rs.index)
+
+    def half_step(g):
+        chunk = d4 ^ jnp.where(g == 0, rs[0], rs[1])
+        bias = small_ref[5:6, :]
+        for other in range(1, 4):
+            bias = jnp.where(chunk == other, small_ref[5 + other : 6 + other, :], bias)
+        v = dot(hidden_ref[...], w_ref[g].reshape(d, d)) + bias
+        c = math.sqrt(2.0 / math.pi)
+        square = v * v
+        t = jnp.tanh(v * (c + (c * 0.044715) * square))
+        half = 0.5 * (1.0 + t)
+        act = (v * half).astype(BF)
+        act_ref[g] = act
+        slope = half + (0.5 * v) * (1.0 - t * t) * (c + (3.0 * c * 0.044715) * square)
+        slope_ref[g] = slope.astype(BF)
+        spread(grad_ref, g, keep, dot_tn(act, c_ref[...]), me_f, masks, h, shards)
+
+    times(2, half_step)
 
 
 def up(idx, hidden, c, small, pieces, maps, rs, masks, shards, h):
     n, d = hidden.shape
     return pl.pallas_call(
         partial(up_kernel, masks, maps, rs, h, shards),
-        grid=(2,),
         out_shape=(
             jax.ShapeDtypeStruct((2, n, d), BF),
             jax.ShapeDtypeStruct((2, n, d), BF),
             jax.ShapeDtypeStruct((2, 2, shards, h, d), BF),
             jax.ShapeDtypeStruct((2, shards, 2 * h, d), BF),
         ),
-        in_specs=[
-            pl.BlockSpec(memory_space=pltpu.SMEM),
-            pl.BlockSpec((n, d), lambda g: (0, 0)),
-            pl.BlockSpec((n, d), lambda g: (0, 0)),
-            pl.BlockSpec(small.shape, lambda g: (0, 0)),
-        ]
-        + [pl.BlockSpec(memory_space=pl.ANY)] * 4,
-        out_specs=(
-            pl.BlockSpec((1, n, d), lambda g: (g, 0, 0)),
-            pl.BlockSpec((1, n, d), lambda g: (g, 0, 0)),
-            pl.BlockSpec((1, 2, shards, h, d), lambda g: (g, 0, 0, 0, 0)),
-            pl.BlockSpec(memory_space=pl.ANY),
-        ),
-        scratch_shapes=[
-            pltpu.VMEM((2, shards, 2 * h, d), BF),
-            pltpu.VMEM((d, d), BF),
-            pltpu.SemaphoreType.DMA((2,)),
-            pltpu.SemaphoreType.DMA((2,)),
-        ],
+        in_specs=[pl.BlockSpec(memory_space=pltpu.SMEM)] + vmem(7),
+        out_specs=tuple(vmem(4)),
+        scratch_shapes=[pltpu.VMEM((d, d), BF)],
         compiler_params=params(),
         cost_estimate=cost(8 * n * d * d, 2 * (6 * n * d + 6 * d * d)),
         name="up",
@@ -440,84 +377,51 @@
     *more,
 ):
     if first:
-        (hidden_ref, sums_ref, grad_ref, w_out, w_ref, keep, sems, out_sems) = more
+        hidden_ref, sums_ref, grad_ref, w_ref, keep = more
     else:
-        (
-            hidden_in, sums_in, hidden_ref, sums_ref, grad_ref, w_out, w_ref, keep, sems, out_sems,
-        ) = more
-    g = pl.program_id(0)
+        hidden_in, sums_in, hidden_ref, sums_ref, grad_ref, w_ref, keep = more
     d4, me_f = idx_ref[0], idx_ref[1]
     d = x_ref.shape[1]
-    c = c_ref[...]
-
-    def send(slot):
-        return pltpu.make_async_copy(w_ref.at[slot], w_out.at[slot], out_sems.at[slot])
-
-    @pl.when(g == 0)
-    def _():
-        fetch((p0, p1, p2, p3), maps, me_f, h, w_ref, rs.index, sems)
-        if first:
-            hidden_ref[...] = jnp.zeros_like(hidden_ref)
-            sums_ref[...] = jnp.zeros_like(sums_ref)
-            sums_ref[4:5, :] = jnp.sum(c.astype(F32), axis=0, keepdims=True)
-        else:
-            hidden_ref[...] = hidden_in[...]
-            sums_ref[...] = sums_in[...]
-
-    fetched(w_ref, g, sems)
-    send(g).start()
-    chunk = d4 ^ jnp.where(g == 0, rs[0], rs[1])
-    pre = (dot_nt(c, w_ref[g].reshape(d, d)) * slope_ref[0].astype(F32)).astype(BF)
-    sums = jnp.sum(pre.astype(F32), axis=0, keepdims=True)
-    row = lax.broadcasted_iota(jnp.int32, (sums_ref.shape[0], 1), 0)
-    sums_ref[...] += jnp.where(row == 5 + chunk, sums, 0.0)
-    hidden_ref[...] += dot_nt(pre, up_ref[0])
-    spread(grad_ref, keep, dot_tn(x_ref[...], pre), me_f, masks, h, shards)
-
-    @pl.when(g == 1)
-    def _():
-        send(0).wait()
-        send(1).wait()
+    place((p0, p1, p2, p3), maps, me_f, h, w_ref, rs.index)
+    if first:
+        hidden_ref[...] = jnp.zeros_like(hidden_ref)
+        sums_ref[...] = jnp.zeros_like(sums_ref)
+        sums_ref[4:5, :] = jnp.sum(c_ref[...].astype(F32), axis=0, keepdims=True)
+    else:
+        hidden_ref[...] = hidden_in[...]
+        sums_ref[...] = sums_in[...]
+
+    def half_step(g):
+        chunk = d4 ^ jnp.where(g == 0, rs[0], rs[1])
+        grad = dot_nt(c_ref[...], w_ref[g].reshape(d, d))
+        pre = (grad * slope_ref[g].astype(F32)).astype(BF)
+        sums = jnp.sum(pre.astype(F32), axis=0, keepdims=True)
+        row = lax.broadcasted_iota(jnp.int32, (sums_ref.shape[0], 1), 0)
+        sums_ref[...] += jnp.where(row == 5 + chunk, sums, 0.0)
+        hidden_ref[...] += dot_nt(pre, up_ref[g])
+        spread(grad_ref, g, keep, dot_tn(x_ref[...], pre), me_f, masks, h, shards)
+
+    times(2, half_step)
 
 
 def act_grad(idx, c, hidden, up_half, slope, pieces, maps, rs, masks, shards, h, before=None):
     n, d = c.shape
-    whole = pl.BlockSpec((n, d), lambda g: (0, 0))
-    sums = pl.BlockSpec((SMALL, d), lambda g: (0, 0))
-    return pl.pallas_call(
-        partial(act_grad_kernel, masks, maps, rs, h, shards, before is None),
-        grid=(2,),
+    before = before or ()
+    return pl.pallas_call(
+        partial(act_grad_kernel, masks, maps, rs, h, shards, not before),
         out_shape=(
             jax.ShapeDtypeStruct((n, d), F32),
             jax.ShapeDtypeStruct((SMALL, d), F32),
             jax.ShapeDtypeStruct((2, 2, shards, h, d), BF),
             jax.ShapeDtypeStruct((2, shards, 2 * h, d), BF),
         ),
-        in_specs=[
-            pl.BlockSpec(memory_space=pltpu.SMEM),
-            whole,
-            whole,
-            pl.BlockSpec((1, d, d), lambda g: (g, 0, 0)),
-            pl.BlockSpec((1, n, d), lambda g: (g, 0, 0)),
-        ]
-        + [pl.BlockSpec(memory_space=pl.ANY)] * 4
-        + ([] if before is None else [whole, sums]),
-        out_specs=(
-            whole,
-            sums,
-            pl.BlockSpec((1, 2, shards, h, d), lambda g: (g, 0, 0, 0, 0)),
-            pl.BlockSpec(memory_space=pl.ANY),
-        ),
-        scratch_shapes=[
-            pltpu.VMEM((2, shards, 2 * h, d), BF),
-            pltpu.VMEM((d, d), BF),
-            pltpu.SemaphoreType.DMA((2,)),
-            pltpu.SemaphoreType.DMA((2,)),
-        ],
+        in_specs=[pl.BlockSpec(memory_space=pltpu.SMEM)] + vmem(8 + len(before)),
+        out_specs=tuple(vmem(4)),
+        scratch_shapes=[pltpu.VMEM((d, d), BF)],
         compiler_params=params(),
         cost_estimate=cost(12 * n * d * d, 2 * (8 * n * d + 8 * d * d)),
         name="act_grad",
-    )(idx, c, hidden, up_half.reshape(2, d, d), slope, *pieces, *(before or ()))
+    )(idx, c, hidden, up_half.reshape(2, d, d), slope, *pieces, *before)
 
 
 def first_grad_kernel(
@@ -527,7 +431,7 @@
     last = (idx_ref[0] ^ jnp.where(g == 0, rs[0], rs[1])) == 3
     x = jnp.where(last, mixed_ref[...], normed_ref[...])
     y = jnp.where(last, branch_ref[...], three_ref[0])
-    spread(out_ref, keep, dot_tn(x, y), idx_ref[1], masks, h, shards)
+    spread(out_ref, 0, keep, dot_tn(x, y), idx_ref[1], masks, h, shards)
 
 
 def first_grad(idx, normed, mixed, three_grad, branch_grad, rs, masks, shards, h):

time: 247 us -> 216 us (0.87)
  Pallas kernels: 107 us -> 64.8 us
  waiting for transfers between devices: 46.3 us -> 71.3 us
  other arithmetic: 16.4 us -> 9.4 us
  local copies, waits for them, and re-layouts: 14.9 us -> 9.49 us
    ppermute x65, waiting for transfers between devices: 46.3 us -> 71.3 us  [swap(): return lax.ppermute(values, axis, [(i, i ^ mask) for i in range(size)])]
    pallas_call x5, Pallas kernels: 47.7 us -> 26 us  [the longest x2 10.8 us: act_grad(): pl.pallas_call(partial(act_grad_kernel, masks, maps, rs, h, shards, not b...]
    pallas_call x2, Pallas kernels: 10.9 us -> 4.94 us  [first_grad(): pl.pallas_call(partial(first_grad_kernel, masks, h, shards, rs), grid_spe...]
    unnamed x68 -> x30, local copies, waits for them, and re-layouts: 5.48 us -> 0.08 us
    add x5, other arithmetic: 3.91 us -> 0.66 us  [sides(): self.keep = (keep[0, 0] + got[0, 0], keep[:, 1, :half] + got[:, 1, :half])]
    pallas_call x1, Pallas kernels: 6.87 us -> 4 us  [down_out(): pl.pallas_call(down_kernel, grid=(2,), out_shape=jax.ShapeDtypeStruct((n,...]
    pallas_call x1, Pallas kernels: 4.91 us -> 2.06 us  [middle(): pl.pallas_call(middle_kernel, grid=(2,), out_shape=(jax.ShapeDtypeStruct(...]
    pallas_call x1, Pallas kernels: 7.91 us -> 5.15 us  [input_grads(): pl.pallas_call(input_kernel, grid=(3,), out_shape=(jax.ShapeDtypeStruct((...]
  transfers between devices with their start and end apart: 65 -> 65, of which waited for: 23 -> 28; matrix products, arithmetic and copies ran while one was open for 9% -> 7% of each run, Pallas kernels for 44% -> 30%
where the time goes in v1:
time: 216 us; the launch traced here: 215 us
  waiting for transfers between devices  71.3 us (33%)
  Pallas kernels  64.8 us (30%)
  starting transfers between devices  59 us (27%)
  local copies, waits for them, and re-layouts  9.49 us (4%)
  other arithmetic  9.4 us (4%)
    ppermute x65, waiting for transfers between devices, swap(): return lax.ppermute(values, axis, [(i, i ^ mask) for i in range(size)])  71.3 us
    ppermute x65, starting transfers between devices, swap(): return lax.ppermute(values, axis, [(i, i ^ mask) for i in range(size)])  59 us
    pallas_call x2, Pallas kernels, act_grad(): pl.pallas_call(partial(act_grad_kernel, masks, maps, rs, h, shards, not b...  10.8 us
    pallas_call x2, Pallas kernels, up(): pl.pallas_call(partial(up_kernel, masks, maps, rs, h, shards), out_shape=...  10.4 us
    pallas_call x1, Pallas kernels, attend_back(): pl.pallas_call(attend_back_kernel, grid=(d // pair,), out_shape=jax.Shape...  9.73 us
    pallas_call x1, Pallas kernels, attend(): pl.pallas_call(attend_kernel, grid=(d // pair,), out_shape=(jax.ShapeDtyp...  8.77 us
    pallas_call x1, Pallas kernels, input_grads(): pl.pallas_call(input_kernel, grid=(3,), out_shape=(jax.ShapeDtypeStruct((...  5.15 us
    pallas_call x2, Pallas kernels, first_grad(): pl.pallas_call(partial(first_grad_kernel, masks, h, shards, rs), grid_spe...  4.94 us
  transfers between devices with their start and end apart: 65, of which 28 were waited for; matrix products, arithmetic and copies ran while one was open for 7% of the time, Pallas kernels for 30%

profile of v1, /device:TPU:0, one launch (start us, length us, event | category | flops | bytes accessed | tf_op | source)
XLA Modules:
  0.0 215.4 jit_solution(9594367947296176439)
XLA Ops:
  1.8 4.1 %collective-permute-start = (bf16[1,96,768]{2,1,0:T(8,128)(2,1)S(1)}, bf16[1,96,768]{2,1,0:T(8,128)(2,1)S(1)}, u32[]{:S(2)}, u32[]{:S(2)}) collective-permute-start(bf16[1,96,768]{2,1,0:T(8,128)(2,1)S(1)} %bitcast.163), channel_id=1, source_target_pairs={{0,4},{1,5},{2,6},{3,7},{4,0},{5,1},{6,2},{7,3},{8,12},{9,13},{10,... | collective-permute-start | bytes 442376 | tf_op jit(solution)/shard_map/ppermute | solution.py:69
  5.9 4.1 %concatenate.55 = bf16[864]{0:T(1024)(128)(2,1)S(1)} concatenate(bf16[96]{0:T(256)(128)(2,1)} %param.17, bf16[96]{0:T(256)(128)(2,1)} %param.18, bf16[96]{0:T(256)(128)(2,1)} %param.23, bf16[96]{0:T(256)(128)(2,1)} %param.24, bf16[96]{0:T(256)(128)(2,1)} %param.28, bf16[384]{0:T(512)(128)(2,1)} %param.26), dimensions={0} | concatenate | bytes 3456 | tf_op jit(solution)/shard_map/concatenate | solution.py:756
  10.3 1.6 collective-permute-start.2
  11.9 2.3 %reshape.252 = bf16[96,8,4,96]{3,2,1,0:T(4,128)(2,1)S(1)} reshape(bf16[96,3072]{1,0:T(8,128)(2,1)} %param.25) | data formatting | bytes 1179648 | tf_op jit(solution)/shard_map/reshape | solution.py:768
  15.7 1.6 collective-permute-start.1
  17.8 6.2 %collective-permute-done.1 = bf16[2,96,768]{2,1,0:T(8,128)(2,1)S(1)} collective-permute-done((bf16[2,96,768]{2,1,0:T(8,128)(2,1)S(1)}, bf16[2,96,768]{2,1,0:T(8,128)(2,1)S(1)}, u32[]{:S(2)}, u32[]{:S(2)}) %collective-permute-start.1) | collective-permute-done | bytes 294944 | tf_op jit(solution)/shard_map/ppermute | solution.py:69
  24.0 1.6 collective-permute-start.3
  26.2 1.6 collective-permute-start.8
  28.5 1.6 collective-permute-start.4
  30.1 2.7 %collective-permute-done.6 = bf16[4,48,768]{2,1,0:T(8,128)(2,1)S(1)} collective-permute-done((bf16[4,48,768]{2,1,0:T(8,128)(2,1)S(1)}, bf16[4,48,768]{2,1,0:T(8,128)(2,1)S(1)}, u32[]{:S(2)}, u32[]{:S(2)}) %collective-permute-start.6) | collective-permute-done | bytes 294944 | tf_op jit(solution)/shard_map/ppermute | solution.py:69
  32.8 1.6 collective-permute-start.7
  34.4 1.6 collective-permute-start.9
  39.0 1.7 collective-permute-start.10
  40.7 2.9 %collective-permute-done.11 = bf16[16,768]{1,0:T(8,128)(2,1)S(1)} collective-permute-done((bf16[16,768]{1,0:T(8,128)(2,1)S(1)}, bf16[16,768]{1,0:T(8,128)(2,1)S(1)}, u32[]{:S(2)}, u32[]{:S(2)}) %collective-permute-start.11) | collective-permute-done | bytes 24608 | tf_op jit(solution)/shard_map/ppermute | solution.py:69
  43.7 2.6 %collective-permute-done.10 = bf16[1,96,768]{2,1,0:T(8,128)(2,1)S(1)} collective-permute-done((bf16[1,96,768]{2,1,0:T(8,128)(2,1)S(1)}, bf16[1,96,768]{2,1,0:T(8,128)(2,1)S(1)}, u32[]{:S(2)}, u32[]{:S(2)}) %collective-permute-start.10) | collective-permute-done | bytes 147488 | tf_op jit(solution)/shard_map/ppermute | solution.py:69
  51.3 4.7 %qkv.1 = (bf16[512,768]{1,0:T(8,128)(2,1)S(1)}, bf16[3,512,768]{2,1,0:T(8,128)(2,1)S(1)}, bf16[4,8,96,768]{3,2,1,0:T(8,128)(2,1)S(1)}) custom-call(s32[2]{0:T(128)S(1)} %pad_add_fusion.idx_ref, bf16[512,768]{1,0:T(8,128)(2,1)S(1)} %copy-done.7, f32[16,768]{1,0:T(8,128)S(1)} %add_convert_fusion.small_ref, f32[512,128]{1,0:T(8,128)S(1)} %get-tuple-element.263.cos_ref, ...), custom_call_target="tpu_custom_call" | custom-call | flops 48000000000 | bytes 13369344 | tf_op jit(solution)/shard_map/qkv/pallas_call | solution.py:180
  56.1 2.5 %collective-permute-done.16 = bf16[4,48,768]{2,1,0:T(8,128)(2,1)S(1)} collective-permute-done((bf16[4,48,768]{2,1,0:T(8,128)(2,1)S(1)}, bf16[4,48,768]{2,1,0:T(8,128)(2,1)S(1)}, u32[]{:S(2)}, u32[]{:S(2)}) %collective-permute-start.16) | collective-permute-done | bytes 294944 | tf_op jit(solution)/shard_map/ppermute | solution.py:69
  60.3 1.6 collective-permute-start.19
  62.4 8.8 %attend.1 = (bf16[512,768]{1,0:T(8,128)(2,1)S(1)}, bf16[12,512,512]{2,1,0:T(8,128)(2,1)S(1)}) custom-call(bf16[3,512,768]{2,1,0:T(8,128)(2,1)S(1)} %get-tuple-element.127.q_ref.k_ref.v_ref, bf16[3,512,768]{2,1,0:T(8,128)(2,1)S(1)} %get-tuple-element.127.q_ref.k_ref.v_ref, bf16[3,512,768]{2,1,0:T(8,128)(2,1)S(1)} %get-tuple-element.127.q_ref.k_ref.v_ref, ...), custom_call_target="tpu_custom_call" | custom-call | flops 48000000000 | bytes 9437184 | tf_op jit(solution)/shard_map/attend/pallas_call | solution.py:219
  71.8 1.8 collective-permute-done.18.p1
  75.4 1.6 branch.1
  77.0 3.7 %collective-permute-done.23 = bf16[4,48,768]{2,1,0:T(8,128)(2,1)S(1)} collective-permute-done((bf16[4,48,768]{2,1,0:T(8,128)(2,1)S(1)}, bf16[4,48,768]{2,1,0:T(8,128)(2,1)S(1)}, u32[]{:S(2)}, u32[]{:S(2)}) %collective-permute-start.23) | collective-permute-done | bytes 294944 | tf_op jit(solution)/shard_map/ppermute | solution.py:69
  83.6 5.2 %up.2 = (bf16[2,512,768]{2,1,0:T(8,128)(2,1)S(1)}, bf16[2,512,768]{2,1,0:T(8,128)(2,1)S(1)}, bf16[2,2,8,48,768]{4,3,2,1,0:T(8,128)(2,1)S(1)}, bf16[2,8,96,768]{3,2,1,0:T(8,128)(2,1)S(1)}) custom-call(s32[2]{0:T(128)S(1)} %pad_add_fusion.idx_ref, bf16[512,768]{1,0:T(8,128)(2,1)S(1)} %get-tuple-element.141.hidden_ref.x_ref, bf16[512,768]{1,0:T(8,128)(2,1)S(1)} %copy-done.6, ...), custom_call_target="tpu_custom_call" | custom-call | flops 48000000000 | bytes 11796480 | tf_op jit(solution)/shard_map/up/pallas_call | solution.py:358
  89.3 5.2 %up.3 = (bf16[2,512,768]{2,1,0:T(8,128)(2,1)S(1)}, bf16[2,512,768]{2,1,0:T(8,128)(2,1)S(1)}, bf16[2,2,8,48,768]{4,3,2,1,0:T(8,128)(2,1)S(1)}, bf16[2,8,96,768]{3,2,1,0:T(8,128)(2,1)S(1)}) custom-call(s32[2]{0:T(128)S(1)} %pad_add_fusion.idx_ref, bf16[512,768]{1,0:T(8,128)(2,1)S(1)} %get-tuple-element.141.hidden_ref.x_ref, bf16[512,768]{1,0:T(8,128)(2,1)S(1)} %copy-done.6, ...), custom_call_target="tpu_custom_call" | custom-call | flops 48000000000 | bytes 11796480 | tf_op jit(solution)/shard_map/up/pallas_call | solution.py:358
  94.6 2.0 collective-permute-done.29.p1
  99.3 1.5 collective-permute-start.35
  100.8 5.5 %act_grad.2 = (f32[512,768]{1,0:T(8,128)S(1)}, f32[16,768]{1,0:T(8,128)S(1)}, bf16[2,2,8,48,768]{4,3,2,1,0:T(8,128)(2,1)S(1)}, bf16[2,8,96,768]{3,2,1,0:T(8,128)(2,1)S(1)}) custom-call(s32[2]{0:T(128)S(1)} %pad_add_fusion.idx_ref, bf16[512,768]{1,0:T(8,128)(2,1)S(1)} %copy-done.6, bf16[512,768]{1,0:T(8,128)(2,1)S(1)} %get-tuple-element.141.hidden_ref.x_ref, ...), custom_call_target="tpu_custom_call" | custom-call | flops 48000000000 | bytes 15728640 | tf_op jit(solution)/shard_map/act_grad/pallas_call | solution.py:410
  106.4 7.1 %collective-permute-done.34 = bf16[8,48,768]{2,1,0:T(8,128)(2,1)S(1)} collective-permute-done((bf16[8,48,768]{2,1,0:T(8,128)(2,1)S(1)}, bf16[8,48,768]{2,1,0:T(8,128)(2,1)S(1)}, u32[]{:S(2)}, u32[]{:S(2)}) %collective-permute-start.34) | collective-permute-done | bytes 589856 | tf_op jit(solution)/shard_map/ppermute | solution.py:69
  114.4 1.5 collective-permute-start.39
  117.1 5.3 %act_grad.3 = (f32[512,768]{1,0:T(8,128)S(1)}, f32[16,768]{1,0:T(8,128)S(1)}, bf16[2,2,8,48,768]{4,3,2,1,0:T(8,128)(2,1)S(1)}, bf16[2,8,96,768]{3,2,1,0:T(8,128)(2,1)S(1)}) custom-call(s32[2]{0:T(128)S(1)} %pad_add_fusion.idx_ref, bf16[512,768]{1,0:T(8,128)(2,1)S(1)} %copy-done.6, bf16[512,768]{1,0:T(8,128)(2,1)S(1)} %get-tuple-element.141.hidden_ref.x_ref, ...), custom_call_target="tpu_custom_call" | custom-call | flops 48000000000 | bytes 15728640 | tf_op jit(solution)/shard_map/act_grad/pallas_call | solution.py:410
  127.0 2.1 middle.1
  130.5 2.4 %collective-permute-start.44 = (bf16[1,2,48,768]{3,2,1,0:T(8,128)(2,1)S(1)}, bf16[1,2,48,768]{3,2,1,0:T(8,128)(2,1)S(1)}, u32[]{:S(2)}, u32[]{:S(2)}) collective-permute-start(bf16[1,2,48,768]{3,2,1,0:T(8,128)(2,1)S(1)} %slice.380), channel_id=1, source_target_pairs={{0,4},{1,5},{2,6},{3,7},{4,0},{5,1},{6,2},{7,3},{8,12},{9,13},{10,... | collective-permute-start | bytes 442376 | tf_op jit(solution)/shard_map/ppermute | solution.py:69
  133.0 9.7 %attend_back.1.three_ref = bf16[3,512,768]{2,1,0:T(8,128)(2,1)S(1)} custom-call(bf16[3,512,768]{2,1,0:T(8,128)(2,1)S(1)} %copy-done.10, bf16[3,512,768]{2,1,0:T(8,128)(2,1)S(1)} %copy-done.10, bf16[3,512,768]{2,1,0:T(8,128)(2,1)S(1)} %copy-done.10, bf16[12,512,512]{2,1,0:T(8,128)(2,1)S(1)} %get-tuple-element.161.probs_ref, ...), custom_call_target="tpu_custom_call" | custom-call | flops 48000000000 | bytes 12582912 | tf_op jit(solution)/shard_map/attend_back/pallas_call | solution.py:269
  144.9 2.5 %first_grad.2 = bf16[2,2,8,48,768]{4,3,2,1,0:T(8,128)(2,1)S(1)} custom-call(s32[2]{0:T(128)S(1)} %pad_add_fusion.idx_ref, bf16[512,768]{1,0:T(8,128)(2,1)S(1)} %get-tuple-element.177.normed_ref, bf16[512,768]{1,0:T(8,128)(2,1)S(1)} %copy-done.12, bf16[3,512,768]{2,1,0:T(8,128)(2,1)S(1)} %attend_back.1.three_ref, ...), custom_call_target="tpu_custom_call" | custom-call | flops 48000000000 | bytes 6291456 | tf_op jit(solution)/shard_map/first_grad/pallas_call | solution.py:444
  147.4 2.9 %collective-permute-done.42 = bf16[4,48,768]{2,1,0:T(8,128)(2,1)S(1)} collective-permute-done((bf16[4,48,768]{2,1,0:T(8,128)(2,1)S(1)}, bf16[4,48,768]{2,1,0:T(8,128)(2,1)S(1)}, u32[]{:S(2)}, u32[]{:S(2)}) %collective-permute-start.42) | collective-permute-done | bytes 294944 | tf_op jit(solution)/shard_map/ppermute | solution.py:69
  151.7 2.5 %first_grad.3 = bf16[2,2,8,48,768]{4,3,2,1,0:T(8,128)(2,1)S(1)} custom-call(s32[2]{0:T(128)S(1)} %pad_add_fusion.idx_ref, bf16[512,768]{1,0:T(8,128)(2,1)S(1)} %get-tuple-element.177.normed_ref, bf16[512,768]{1,0:T(8,128)(2,1)S(1)} %copy-done.12, bf16[3,512,768]{2,1,0:T(8,128)(2,1)S(1)} %attend_back.1.three_ref, ...), custom_call_target="tpu_custom_call" | custom-call | flops 48000000000 | bytes 6291456 | tf_op jit(solution)/shard_map/first_grad/pallas_call | solution.py:444
  154.5 4.5 %collective-permute-done.45 = bf16[2,2,48,768]{3,2,1,0:T(8,128)(2,1)S(1)} collective-permute-done((bf16[2,2,48,768]{3,2,1,0:T(8,128)(2,1)S(1)}, bf16[2,2,48,768]{3,2,1,0:T(8,128)(2,1)S(1)}, u32[]{:S(2)}, u32[]{:S(2)}) %collective-permute-start.45) | collective-permute-done | bytes 294944 | tf_op jit(solution)/shard_map/ppermute | solution.py:69
  161.4 5.2 %input_grads.1 = (f32[512,768]{1,0:T(8,128)}, f32[16,768]{1,0:T(8,128)S(1)}) custom-call(bf16[512,768]{1,0:T(8,128)(2,1)S(1)} %copy-done.8, bf16[3,512,768]{2,1,0:T(8,128)(2,1)S(1)} %attend_back.1.three_ref, bf16[4,768,768]{2,1,0:T(8,128)(2,1)S(1)} %bitcast.158, f32[16,768]{1,0:T(8,128)S(1)} %add_convert_fusion.small_ref, ...), custom_call_target="tpu_custom_call" | custom-call | flops 48000000000 | bytes 9830400 | tf_op jit(solution)/shard_map/input_grads/pallas_call | solution.py:538
  166.7 4.0 %down_out.1 = bf16[512,768]{1,0:T(8,128)(2,1)} custom-call(bf16[2,512,768]{2,1,0:T(8,128)(2,1)S(1)} %get-tuple-element.139.a0_ref, bf16[2,512,768]{2,1,0:T(8,128)(2,1)S(1)} %get-tuple-element.142.a1_ref, bf16[2,768,768]{2,1,0:T(8,128)(2,1)S(1)} %bitcast.159, bf16[2,768,768]{2,1,0:T(8,128)(2,1)S(1)} %bitcast.160, f32[16,768]{1,0:T(8,128)S(1)} %add_convert_fusion.small_ref, ...), custom_call_target="tpu_custom_call" | custom-call | flops 48000000000 | bytes 10223616 | tf_op jit(solution)/shard_map/down_out/pallas_call | solution.py:575
  173.2 7.1 %collective-permute-done.52 = bf16[4,48,768]{2,1,0:T(8,128)(2,1)S(1)} collective-permute-done((bf16[4,48,768]{2,1,0:T(8,128)(2,1)S(1)}, bf16[4,48,768]{2,1,0:T(8,128)(2,1)S(1)}, u32[]{:S(2)}, u32[]{:S(2)}) %collective-permute-start.52) | collective-permute-done | bytes 294944 | tf_op jit(solution)/shard_map/ppermute | solution.py:69
  182.0 1.8 collective-permute-start.55
  184.0 1.8 collective-permute-start.59
  185.8 4.3 %collective-permute-done.55 = bf16[2,2,48,768]{3,2,0,1:T(8,128)(2,1)S(1)} collective-permute-done((bf16[2,2,48,768]{3,2,0,1:T(8,128)(2,1)S(1)}, bf16[2,2,48,768]{3,2,0,1:T(8,128)(2,1)S(1)}, u32[]{:S(2)}, u32[]{:S(2)}) %collective-permute-start.55) | collective-permute-done | bytes 294944 | tf_op jit(solution)/shard_map/ppermute | solution.py:69
  190.2 3.2 %collective-permute-done.59.p2 = bf16[2,2,48,768]{3,2,1,0:T(8,128)(2,1)S(1)} collective-permute-done((bf16[2,2,48,768]{3,2,1,0:T(8,128)(2,1)S(1)}, bf16[2,2,48,768]{3,2,1,0:T(8,128)(2,1)S(1)}, u32[]{:S(2)}, u32[]{:S(2)}) %collective-permute-start.59) | collective-permute-done | bytes 294944 | tf_op jit(solution)/shard_map/ppermute | solution.py:69
  196.3 2.1 collective-permute-done.54
  198.5 2.6 %last_out.1 = (f32[96,3072]{1,0:T(8,128)}, f32[384,768]{1,0:T(8,128)}) custom-call(s32[2]{0:T(128)S(1)} %pad_add_fusion.idx_ref, bf16[2,2,48,768]{3,2,1,0:T(8,128)(2,1)S(1)} %pad_maximum_fusion.19.p0, bf16[2,2,48,768]{3,2,1,0:T(8,128)(2,1)S(1)} %collective-permute-done.58.p1, bf16[2,2,48,768]{3,2,1,0:T(8,128)(2,1)S(1)} %collective-permute-done.59.p2, ...), custom_call_target="tpu_custom_call" | custom-call | tf_op jit(solution)/shard_map/last_out/pallas_call | solution.py:610
  201.1 3.8 %collective-permute-done.57 = bf16[1,2,48,768]{3,2,0,1:T(8,128)(2,1)S(1)} collective-permute-done((bf16[1,2,48,768]{3,2,0,1:T(8,128)(2,1)S(1)}, bf16[1,2,48,768]{3,2,0,1:T(8,128)(2,1)S(1)}, u32[]{:S(2)}, u32[]{:S(2)}) %collective-permute-start.57) | collective-permute-done | bytes 147488 | tf_op jit(solution)/shard_map/ppermute | solution.py:69
  207.5 2.6 %collective-permute-done.61 = bf16[16,768]{1,0:T(8,128)(2,1)S(1)} collective-permute-done((bf16[16,768]{1,0:T(8,128)(2,1)S(1)}, bf16[16,768]{1,0:T(8,128)(2,1)S(1)}, u32[]{:S(2)}, u32[]{:S(2)}) %collective-permute-start.61) | collective-permute-done | bytes 24608 | tf_op jit(solution)/shard_map/ppermute | solution.py:69
  (218 shorter events, 53.3 us)
Async XLA Ops:
  1.8 13.9 %collective-permute-start = (bf16[1,96,768]{2,1,0:T(8,128)(2,1)S(1)}, bf16[1,96,768]{2,1,0:T(8,128)(2,1)S(1)}, u32[]{:S(2)}, u32[]{:S(2)}) collective-permute-start(bf16[1,96,768]{2,1,0:T(8,128)(2,1)S(1)} %bitcast.163), channel_id=1, source_target_pairs={{0,4},{1,5},{2,6},{3,7},{4,0},{5,1},{6,2},{7,3},{8,12},{9,13},{10,... | collective-permute-start | bytes 442376 | tf_op jit(solution)/shard_map/ppermute | solution.py:69
  15.7 8.3 %collective-permute-start.1 = (bf16[2,96,768]{2,1,0:T(8,128)(2,1)S(1)}, bf16[2,96,768]{2,1,0:T(8,128)(2,1)S(1)}, u32[]{:S(2)}, u32[]{:S(2)}) collective-permute-start(bf16[2,96,768]{2,1,0:T(8,128)(2,1)S(1)} %pad_maximum_fusion.8), channel_id=1, source_target_pairs={{0,2},{1,3},{2,0},{3,1},{4,6},{5,7},{6,4},{7,5},{8,10},{9,11},{10,... | collective-permute-start | bytes 884744 | tf_op jit(solution)/shard_map/ppermute | solution.py:69
  25.6 7.1 %collective-permute-start.6 = (bf16[4,48,768]{2,1,0:T(8,128)(2,1)S(1)}, bf16[4,48,768]{2,1,0:T(8,128)(2,1)S(1)}, u32[]{:S(2)}, u32[]{:S(2)}) collective-permute-start(bf16[4,48,768]{2,1,0:T(8,128)(2,1)S(1)} %pad_maximum_fusion.12), channel_id=1, source_target_pairs={{0,1},{1,0},{2,3},{3,2},{4,5},{5,4},{6,7},{7,6},{8,9},{9,8},{10,11... | collective-permute-start | bytes 884744 | tf_op jit(solution)/shard_map/ppermute | solution.py:69
  26.2 8.1 %collective-permute-start.8 = (bf16[4,48,768]{2,1,0:T(8,128)(2,1)S(1)}, bf16[4,48,768]{2,1,0:T(8,128)(2,1)S(1)}, u32[]{:S(2)}, u32[]{:S(2)}) collective-permute-start(bf16[4,48,768]{2,1,0:T(8,128)(2,1)S(1)} %pad_maximum_fusion.13), channel_id=1, source_target_pairs={{0,16},{8,24},{16,0},{24,8},{1,17},{9,25},{17,1},{25,9},{2,18},{10... | collective-permute-start | bytes 884744 | tf_op jit(solution)/shard_map/ppermute | solution.py:69
  28.5 9.8 %collective-permute-start.4 = (bf16[1,96,768]{2,1,0:T(8,128)(2,1)S(1)}, bf16[1,96,768]{2,1,0:T(8,128)(2,1)S(1)}, u32[]{:S(2)}, u32[]{:S(2)}) collective-permute-start(bf16[1,96,768]{2,1,0:T(8,128)(2,1)S(1)} %bitcast.168), channel_id=1, source_target_pairs={{0,4},{1,5},{2,6},{3,7},{4,0},{5,1},{6,2},{7,3},{8,12},{9,13},{10,... | collective-permute-start | bytes 442376 | tf_op jit(solution)/shard_map/ppermute | solution.py:69
  32.8 13.5 %collective-permute-start.7 = (bf16[8,48,768]{2,1,0:T(8,128)(2,1)S(1)}, bf16[8,48,768]{2,1,0:T(8,128)(2,1)S(1)}, u32[]{:S(2)}, u32[]{:S(2)}) collective-permute-start(bf16[8,48,768]{2,1,0:T(8,128)(2,1)S(1)} %pad_maximum_fusion.1.p0), channel_id=1, source_target_pairs={{0,16},{8,24},{16,0},{24,8},{1,17},{9,25},{17,1},{25,9},{2,18},{10... | collective-permute-start | bytes 1769480 | tf_op jit(solution)/shard_map/ppermute | solution.py:69
  34.4 12.3 %collective-permute-start.9 = (bf16[8,48,768]{2,1,0:T(8,128)(2,1)S(1)}, bf16[8,48,768]{2,1,0:T(8,128)(2,1)S(1)}, u32[]{:S(2)}, u32[]{:S(2)}) collective-permute-start(bf16[8,48,768]{2,1,0:T(8,128)(2,1)S(1)} %pad_maximum_fusion.2.p2), channel_id=1, source_target_pairs={{0,1},{1,0},{2,3},{3,2},{4,5},{5,4},{6,7},{7,6},{8,9},{9,8},{10,11... | collective-permute-start | bytes 1769480 | tf_op jit(solution)/shard_map/ppermute | solution.py:69
  38.4 9.6 %collective-permute-start.5 = (bf16[2,96,768]{2,1,0:T(8,128)(2,1)S(1)}, bf16[2,96,768]{2,1,0:T(8,128)(2,1)S(1)}, u32[]{:S(2)}, u32[]{:S(2)}) collective-permute-start(bf16[2,96,768]{2,1,0:T(8,128)(2,1)S(1)} %pad_maximum_fusion.11), channel_id=1, source_target_pairs={{0,2},{1,3},{2,0},{3,1},{4,6},{5,7},{6,4},{7,5},{8,10},{9,11},{10,... | collective-permute-start | bytes 884744 | tf_op jit(solution)/shard_map/ppermute | solution.py:69
  39.0 7.3 %collective-permute-start.10 = (bf16[1,96,768]{2,1,0:T(8,128)(2,1)S(1)}, bf16[1,96,768]{2,1,0:T(8,128)(2,1)S(1)}, u32[]{:S(2)}, u32[]{:S(2)}) collective-permute-start(bf16[1,96,768]{2,1,0:T(8,128)(2,1)S(1)} %dynamic-slice_bitcast_fusion), channel_id=1, source_target_pairs={{0,4},{1,5},{2,6},{3,7},{4,0},{5,1},{6,2},{7,3},{8,12},{9,13},{10,... | collective-permute-start | bytes 442376 | tf_op jit(solution)/shard_map/ppermute | solution.py:69
  48.0 23.2 %collective-permute-start.22 = (bf16[2,96,768]{2,1,0:T(8,128)(2,1)S(1)}, bf16[2,96,768]{2,1,0:T(8,128)(2,1)S(1)}, u32[]{:S(2)}, u32[]{:S(2)}) collective-permute-start(bf16[2,96,768]{2,1,0:T(8,128)(2,1)S(1)} %pad_maximum_fusion.16), channel_id=1, source_target_pairs={{0,2},{1,3},{2,0},{3,1},{4,6},{5,7},{6,4},{7,5},{8,10},{9,11},{10,... | collective-permute-start | bytes 884744 | tf_op jit(solution)/shard_map/ppermute | solution.py:69
  49.4 9.1 %collective-permute-start.16 = (bf16[4,48,768]{2,1,0:T(8,128)(2,1)S(1)}, bf16[4,48,768]{2,1,0:T(8,128)(2,1)S(1)}, u32[]{:S(2)}, u32[]{:S(2)}) collective-permute-start(bf16[4,48,768]{2,1,0:T(8,128)(2,1)S(1)} %pad_maximum_fusion.14), channel_id=1, source_target_pairs={{0,1},{1,0},{2,3},{3,2},{4,5},{5,4},{6,7},{7,6},{8,9},{9,8},{10,11... | collective-permute-start | bytes 884744 | tf_op jit(solution)/shard_map/ppermute | solution.py:69
  50.3 8.8 %collective-permute-start.17 = (bf16[4,48,768]{2,1,0:T(8,128)(2,1)S(1)}, bf16[4,48,768]{2,1,0:T(8,128)(2,1)S(1)}, u32[]{:S(2)}, u32[]{:S(2)}) collective-permute-start(bf16[4,48,768]{2,1,0:T(8,128)(2,1)S(1)} %pad_maximum_fusion.15), channel_id=1, source_target_pairs={{0,16},{8,24},{16,0},{24,8},{1,17},{9,25},{17,1},{25,9},{2,18},{10... | collective-permute-start | bytes 884744 | tf_op jit(solution)/shard_map/ppermute | solution.py:69
  59.2 14.3 %collective-permute-start.18 = (bf16[8,48,768]{2,1,0:T(8,128)(2,1)S(1)}, bf16[8,48,768]{2,1,0:T(8,128)(2,1)S(1)}, u32[]{:S(2)}, u32[]{:S(2)}) collective-permute-start(bf16[8,48,768]{2,1,0:T(8,128)(2,1)S(1)} %pad_maximum_fusion.3.p0), channel_id=1, source_target_pairs={{0,16},{8,24},{16,0},{24,8},{1,17},{9,25},{17,1},{25,9},{2,18},{10... | collective-permute-start | bytes 1769480 | tf_op jit(solution)/shard_map/ppermute | solution.py:69
  60.3 14.6 %collective-permute-start.19 = (bf16[8,48,768]{2,1,0:T(8,128)(2,1)S(1)}, bf16[8,48,768]{2,1,0:T(8,128)(2,1)S(1)}, u32[]{:S(2)}, u32[]{:S(2)}) collective-permute-start(bf16[8,48,768]{2,1,0:T(8,128)(2,1)S(1)} %pad_maximum_fusion.4.p2), channel_id=1, source_target_pairs={{0,1},{1,0},{2,3},{3,2},{4,5},{5,4},{6,7},{7,6},{8,9},{9,8},{10,11... | collective-permute-start | bytes 1769480 | tf_op jit(solution)/shard_map/ppermute | solution.py:69
  61.9 13.0 %collective-permute-start.20 = (bf16[8,48,768]{2,1,0:T(8,128)(2,1)S(1)}, bf16[8,48,768]{2,1,0:T(8,128)(2,1)S(1)}, u32[]{:S(2)}, u32[]{:S(2)}) collective-permute-start(bf16[8,48,768]{2,1,0:T(8,128)(2,1)S(1)} %pad_maximum_fusion.3.p0), channel_id=1, source_target_pairs={{0,8},{8,0},{16,24},{24,16},{1,9},{9,1},{17,25},{25,17},{2,10},{10... | collective-permute-start | bytes 1769480 | tf_op jit(solution)/shard_map/ppermute | solution.py:69
  61.9 13.5 %collective-permute-start.21 = (bf16[8,48,768]{2,1,0:T(8,128)(2,1)S(1)}, bf16[8,48,768]{2,1,0:T(8,128)(2,1)S(1)}, u32[]{:S(2)}, u32[]{:S(2)}) collective-permute-start(bf16[8,48,768]{2,1,0:T(8,128)(2,1)S(1)} %pad_maximum_fusion.4.p2), channel_id=1, source_target_pairs={{0,8},{8,0},{16,24},{24,16},{1,9},{9,1},{17,25},{25,17},{2,10},{10... | collective-permute-start | bytes 1769480 | tf_op jit(solution)/shard_map/ppermute | solution.py:69
  71.3 9.4 %collective-permute-start.23 = (bf16[4,48,768]{2,1,0:T(8,128)(2,1)S(1)}, bf16[4,48,768]{2,1,0:T(8,128)(2,1)S(1)}, u32[]{:S(2)}, u32[]{:S(2)}) collective-permute-start(bf16[4,48,768]{2,1,0:T(8,128)(2,1)S(1)} %pad_maximum_fusion.17), channel_id=1, source_target_pairs={{0,1},{1,0},{2,3},{3,2},{4,5},{5,4},{6,7},{7,6},{8,9},{9,8},{10,11... | collective-permute-start | bytes 884744 | tf_op jit(solution)/shard_map/ppermute | solution.py:69
  73.6 7.1 %collective-permute-start.24 = (bf16[4,48,768]{2,1,0:T(8,128)(2,1)S(1)}, bf16[4,48,768]{2,1,0:T(8,128)(2,1)S(1)}, u32[]{:S(2)}, u32[]{:S(2)}) collective-permute-start(bf16[4,48,768]{2,1,0:T(8,128)(2,1)S(1)} %pad_maximum_fusion.18), channel_id=1, source_target_pairs={{0,16},{8,24},{16,0},{24,8},{1,17},{9,25},{17,1},{25,9},{2,18},{10... | collective-permute-start | bytes 884744 | tf_op jit(solution)/shard_map/ppermute | solution.py:69
  74.8 8.7 %collective-permute-start.25 = (bf16[8,48,768]{2,1,0:T(8,128)(2,1)S(1)}, bf16[8,48,768]{2,1,0:T(8,128)(2,1)S(1)}, u32[]{:S(2)}, u32[]{:S(2)}) collective-permute-start(bf16[8,48,768]{2,1,0:T(8,128)(2,1)S(1)} %collective-permute-done.18.p1), channel_id=1, source_target_pairs={{0,8},{8,0},{16,24},{24,16},{1,9},{9,1},{17,25},{25,17},{2,10},{10... | collective-permute-start | bytes 1769480 | tf_op jit(solution)/shard_map/ppermute | solution.py:69
  74.9 8.7 %collective-permute-start.26 = (bf16[8,48,768]{2,1,0:T(8,128)(2,1)S(1)}, bf16[8,48,768]{2,1,0:T(8,128)(2,1)S(1)}, u32[]{:S(2)}, u32[]{:S(2)}) collective-permute-start(bf16[8,48,768]{2,1,0:T(8,128)(2,1)S(1)} %collective-permute-done.19.p3), channel_id=1, source_target_pairs={{0,8},{8,0},{16,24},{24,16},{1,9},{9,1},{17,25},{25,17},{2,10},{10... | collective-permute-start | bytes 1769480 | tf_op jit(solution)/shard_map/ppermute | solution.py:69
  80.8 18.5 %collective-permute-start.28 = (bf16[8,48,768]{2,1,0:T(8,128)(2,1)S(1)}, bf16[8,48,768]{2,1,0:T(8,128)(2,1)S(1)}, u32[]{:S(2)}, u32[]{:S(2)}) collective-permute-start(bf16[8,48,768]{2,1,0:T(8,128)(2,1)S(1)} %pad_maximum_fusion.5.p0), channel_id=1, source_target_pairs={{0,8},{8,0},{16,24},{24,16},{1,9},{9,1},{17,25},{25,17},{2,10},{10... | collective-permute-start | bytes 1769480 | tf_op jit(solution)/shard_map/ppermute | solution.py:69
  80.9 15.7 %collective-permute-start.29 = (bf16[8,48,768]{2,1,0:T(8,128)(2,1)S(1)}, bf16[8,48,768]{2,1,0:T(8,128)(2,1)S(1)}, u32[]{:S(2)}, u32[]{:S(2)}) collective-permute-start(bf16[8,48,768]{2,1,0:T(8,128)(2,1)S(1)} %pad_maximum_fusion.5.p0), channel_id=1, source_target_pairs={{0,16},{8,24},{16,0},{24,8},{1,17},{9,25},{17,1},{25,9},{2,18},{10... | collective-permute-start | bytes 1769480 | tf_op jit(solution)/shard_map/ppermute | solution.py:69
  82.1 15.4 %collective-permute-start.30 = (bf16[8,48,768]{2,1,0:T(8,128)(2,1)S(1)}, bf16[8,48,768]{2,1,0:T(8,128)(2,1)S(1)}, u32[]{:S(2)}, u32[]{:S(2)}) collective-permute-start(bf16[8,48,768]{2,1,0:T(8,128)(2,1)S(1)} %pad_maximum_fusion.6.p2), channel_id=1, source_target_pairs={{0,1},{1,0},{2,3},{3,2},{4,5},{5,4},{6,7},{7,6},{8,9},{9,8},{10,11... | collective-permute-start | bytes 1769480 | tf_op jit(solution)/shard_map/ppermute | solution.py:69
  83.6 17.3 %collective-permute-start.32 = (bf16[8,48,768]{2,1,0:T(8,128)(2,1)S(1)}, bf16[8,48,768]{2,1,0:T(8,128)(2,1)S(1)}, u32[]{:S(2)}, u32[]{:S(2)}) collective-permute-start(bf16[8,48,768]{2,1,0:T(8,128)(2,1)S(1)} %pad_maximum_fusion.6.p2), channel_id=1, source_target_pairs={{0,8},{8,0},{16,24},{24,16},{1,9},{9,1},{17,25},{25,17},{2,10},{10... | collective-permute-start | bytes 1769480 | tf_op jit(solution)/shard_map/ppermute | solution.py:69
  88.8 9.3 %collective-permute-start.27 = (bf16[2,2,8,48,768]{4,3,2,1,0:T(8,128)(2,1)S(1)}, bf16[2,2,8,48,768]{4,3,2,1,0:T(8,128)(2,1)S(1)}, u32[]{:S(2)}, u32[]{:S(2)}) collective-permute-start(bf16[2,2,8,48,768]{4,3,2,1,0:T(8,128)(2,1)S(1)} %get-tuple-element.140), channel_id=1, source_target_pairs={{0,8},{8,0},{16,24},{24,16},{1,9},{9,1},{17,25},{25,17},{2,10},{10... | collective-permute-start | bytes 7077896 | tf_op jit(solution)/shard_map/ppermute | solution.py:69
  98.2 15.3 %collective-permute-start.34 = (bf16[8,48,768]{2,1,0:T(8,128)(2,1)S(1)}, bf16[8,48,768]{2,1,0:T(8,128)(2,1)S(1)}, u32[]{:S(2)}, u32[]{:S(2)}) collective-permute-start(bf16[8,48,768]{2,1,0:T(8,128)(2,1)S(1)} %get-tuple-element.232), channel_id=1, source_target_pairs={{0,16},{8,24},{16,0},{24,8},{1,17},{9,25},{17,1},{25,9},{2,18},{10... | collective-permute-start | bytes 1769480 | tf_op jit(solution)/shard_map/ppermute | solution.py:69
  99.3 15.0 %collective-permute-start.35 = (bf16[2,4,48,768]{3,2,1,0:T(8,128)(2,1)S(1)}, bf16[2,4,48,768]{3,2,1,0:T(8,128)(2,1)S(1)}, u32[]{:S(2)}, u32[]{:S(2)}) collective-permute-start(bf16[2,4,48,768]{3,2,1,0:T(8,128)(2,1)S(1)} %get-tuple-element.230), channel_id=1, source_target_pairs={{0,1},{1,0},{2,3},{3,2},{4,5},{5,4},{6,7},{7,6},{8,9},{9,8},{10,11... | collective-permute-start | bytes 1769480 | tf_op jit(solution)/shard_map/ppermute | solution.py:69
  106.3 18.0 %collective-permute-start.36 = (bf16[2,2,8,48,768]{4,3,2,1,0:T(8,128)(2,1)S(1)}, bf16[2,2,8,48,768]{4,3,2,1,0:T(8,128)(2,1)S(1)}, u32[]{:S(2)}, u32[]{:S(2)}) collective-permute-start(bf16[2,2,8,48,768]{4,3,2,1,0:T(8,128)(2,1)S(1)} %get-tuple-element.150), channel_id=1, source_target_pairs={{0,8},{8,0},{16,24},{24,16},{1,9},{9,1},{17,25},{25,17},{2,10},{10... | collective-permute-start | bytes 7077896 | tf_op jit(solution)/shard_map/ppermute | solution.py:69
  114.4 8.1 %collective-permute-start.39 = (bf16[4,48,768]{2,1,0:T(8,128)(2,1)S(1)}, bf16[4,48,768]{2,1,0:T(8,128)(2,1)S(1)}, u32[]{:S(2)}, u32[]{:S(2)}) collective-permute-start(bf16[4,48,768]{2,1,0:T(8,128)(2,1)S(1)} %get-tuple-element.240), channel_id=1, source_target_pairs={{0,1},{1,0},{2,3},{3,2},{4,5},{5,4},{6,7},{7,6},{8,9},{9,8},{10,11... | collective-permute-start | bytes 884744 | tf_op jit(solution)/shard_map/ppermute | solution.py:69
  116.0 7.6 %collective-permute-start.40 = (bf16[4,48,768]{2,1,0:T(8,128)(2,1)S(1)}, bf16[4,48,768]{2,1,0:T(8,128)(2,1)S(1)}, u32[]{:S(2)}, u32[]{:S(2)}) collective-permute-start(bf16[4,48,768]{2,1,0:T(8,128)(2,1)S(1)} %get-tuple-element.238), channel_id=1, source_target_pairs={{0,16},{8,24},{16,0},{24,8},{1,17},{9,25},{17,1},{25,9},{2,18},{10... | collective-permute-start | bytes 884744 | tf_op jit(solution)/shard_map/ppermute | solution.py:69
  123.7 6.8 %collective-permute-start.41 = (bf16[2,2,48,768]{3,2,1,0:T(8,128)(2,1)S(1)}, bf16[2,2,48,768]{3,2,1,0:T(8,128)(2,1)S(1)}, u32[]{:S(2)}, u32[]{:S(2)}) collective-permute-start(bf16[2,2,48,768]{3,2,1,0:T(8,128)(2,1)S(1)} %fusion.11), channel_id=1, source_target_pairs={{0,2},{1,3},{2,0},{3,1},{4,6},{5,7},{6,4},{7,5},{8,10},{9,11},{10,... | collective-permute-start | bytes 884744 | tf_op jit(solution)/shard_map/ppermute | solution.py:69
  124.4 19.0 %collective-permute-start.37 = (bf16[8,48,768]{2,1,0:T(8,128)(2,1)S(1)}, bf16[8,48,768]{2,1,0:T(8,128)(2,1)S(1)}, u32[]{:S(2)}, u32[]{:S(2)}) collective-permute-start(bf16[8,48,768]{2,1,0:T(8,128)(2,1)S(1)} %get-tuple-element.226), channel_id=1, source_target_pairs={{0,16},{8,24},{16,0},{24,8},{1,17},{9,25},{17,1},{25,9},{2,18},{10... | collective-permute-start | bytes 1769480 | tf_op jit(solution)/shard_map/ppermute | solution.py:69
  125.9 17.5 %collective-permute-start.38 = (bf16[2,4,48,768]{3,2,1,0:T(8,128)(2,1)S(1)}, bf16[2,4,48,768]{3,2,1,0:T(8,128)(2,1)S(1)}, u32[]{:S(2)}, u32[]{:S(2)}) collective-permute-start(bf16[2,4,48,768]{3,2,1,0:T(8,128)(2,1)S(1)} %get-tuple-element.227), channel_id=1, source_target_pairs={{0,1},{1,0},{2,3},{3,2},{4,5},{5,4},{6,7},{7,6},{8,9},{9,8},{10,11... | collective-permute-start | bytes 1769480 | tf_op jit(solution)/shard_map/ppermute | solution.py:69
  130.5 12.2 %collective-permute-start.44 = (bf16[1,2,48,768]{3,2,1,0:T(8,128)(2,1)S(1)}, bf16[1,2,48,768]{3,2,1,0:T(8,128)(2,1)S(1)}, u32[]{:S(2)}, u32[]{:S(2)}) collective-permute-start(bf16[1,2,48,768]{3,2,1,0:T(8,128)(2,1)S(1)} %slice.380), channel_id=1, source_target_pairs={{0,4},{1,5},{2,6},{3,7},{4,0},{5,1},{6,2},{7,3},{8,12},{9,13},{10,... | collective-permute-start | bytes 442376 | tf_op jit(solution)/shard_map/ppermute | solution.py:69
  143.5 6.8 %collective-permute-start.42 = (bf16[4,48,768]{2,1,0:T(8,128)(2,1)S(1)}, bf16[4,48,768]{2,1,0:T(8,128)(2,1)S(1)}, u32[]{:S(2)}, u32[]{:S(2)}) collective-permute-start(bf16[4,48,768]{2,1,0:T(8,128)(2,1)S(1)} %get-tuple-element.234), channel_id=1, source_target_pairs={{0,1},{1,0},{2,3},{3,2},{4,5},{5,4},{6,7},{7,6},{8,9},{9,8},{10,11... | collective-permute-start | bytes 884744 | tf_op jit(solution)/shard_map/ppermute | solution.py:69
  144.6 6.8 %collective-permute-start.43 = (bf16[4,48,768]{2,1,0:T(8,128)(2,1)S(1)}, bf16[4,48,768]{2,1,0:T(8,128)(2,1)S(1)}, u32[]{:S(2)}, u32[]{:S(2)}) collective-permute-start(bf16[4,48,768]{2,1,0:T(8,128)(2,1)S(1)} %get-tuple-element.235), channel_id=1, source_target_pairs={{0,16},{8,24},{16,0},{24,8},{1,17},{9,25},{17,1},{25,9},{2,18},{10... | collective-permute-start | bytes 884744 | tf_op jit(solution)/shard_map/ppermute | solution.py:69
  147.3 6.9 %collective-permute-start.46 = (bf16[2,2,8,48,768]{4,3,2,1,0:T(8,128)(2,1)S(1)}, bf16[2,2,8,48,768]{4,3,2,1,0:T(8,128)(2,1)S(1)}, u32[]{:S(2)}, u32[]{:S(2)}) collective-permute-start(bf16[2,2,8,48,768]{4,3,2,1,0:T(8,128)(2,1)S(1)} %first_grad.2), channel_id=1, source_target_pairs={{0,8},{8,0},{16,24},{24,16},{1,9},{9,1},{17,25},{25,17},{2,10},{10... | collective-permute-start | bytes 7077896 | tf_op jit(solution)/shard_map/ppermute | solution.py:69
  151.5 7.5 %collective-permute-start.45 = (bf16[2,2,48,768]{3,2,1,0:T(8,128)(2,1)S(1)}, bf16[2,2,48,768]{3,2,1,0:T(8,128)(2,1)S(1)}, u32[]{:S(2)}, u32[]{:S(2)}) collective-permute-start(bf16[2,2,48,768]{3,2,1,0:T(8,128)(2,1)S(1)} %pad_maximum_fusion.9), channel_id=1, source_target_pairs={{0,2},{1,3},{2,0},{3,1},{4,6},{5,7},{6,4},{7,5},{8,10},{9,11},{10,... | collective-permute-start | bytes 884744 | tf_op jit(solution)/shard_map/ppermute | solution.py:69
  159.1 7.6 %collective-permute-start.47 = (bf16[1,2,48,768]{3,2,1,0:T(8,128)(2,1)S(1)}, bf16[1,2,48,768]{3,2,1,0:T(8,128)(2,1)S(1)}, u32[]{:S(2)}, u32[]{:S(2)}) collective-permute-start(bf16[1,2,48,768]{3,2,1,0:T(8,128)(2,1)S(1)} %slice.397), channel_id=1, source_target_pairs={{0,4},{1,5},{2,6},{3,7},{4,0},{5,1},{6,2},{7,3},{8,12},{9,13},{10,... | collective-permute-start | bytes 442376 | tf_op jit(solution)/shard_map/ppermute | solution.py:69
  159.1 11.6 %collective-permute-start.49 = (bf16[8,48,768]{2,1,0:T(8,128)(2,1)S(1)}, bf16[8,48,768]{2,1,0:T(8,128)(2,1)S(1)}, u32[]{:S(2)}, u32[]{:S(2)}) collective-permute-start(bf16[8,48,768]{2,1,0:T(8,128)(2,1)S(1)} %get-tuple-element.224), channel_id=1, source_target_pairs={{0,16},{8,24},{16,0},{24,8},{1,17},{9,25},{17,1},{25,9},{2,18},{10... | collective-permute-start | bytes 1769480 | tf_op jit(solution)/shard_map/ppermute | solution.py:69
  160.2 11.1 %collective-permute-start.50 = (bf16[2,4,48,768]{3,2,1,0:T(8,128)(2,1)S(1)}, bf16[2,4,48,768]{3,2,1,0:T(8,128)(2,1)S(1)}, u32[]{:S(2)}, u32[]{:S(2)}) collective-permute-start(bf16[2,4,48,768]{3,2,1,0:T(8,128)(2,1)S(1)} %get-tuple-element.222), channel_id=1, source_target_pairs={{0,1},{1,0},{2,3},{3,2},{4,5},{5,4},{6,7},{7,6},{8,9},{9,8},{10,11... | collective-permute-start | bytes 1769480 | tf_op jit(solution)/shard_map/ppermute | solution.py:69
  171.4 8.8 %collective-permute-start.52 = (bf16[4,48,768]{2,1,0:T(8,128)(2,1)S(1)}, bf16[4,48,768]{2,1,0:T(8,128)(2,1)S(1)}, u32[]{:S(2)}, u32[]{:S(2)}) collective-permute-start(bf16[4,48,768]{2,1,0:T(8,128)(2,1)S(1)} %fusion.19), channel_id=1, source_target_pairs={{0,1},{1,0},{2,3},{3,2},{4,5},{5,4},{6,7},{7,6},{8,9},{9,8},{10,11... | collective-permute-start | bytes 884744 | tf_op jit(solution)/shard_map/ppermute | solution.py:69
  172.6 8.3 %collective-permute-start.53 = (bf16[4,48,768]{2,1,0:T(8,128)(2,1)S(1)}, bf16[4,48,768]{2,1,0:T(8,128)(2,1)S(1)}, u32[]{:S(2)}, u32[]{:S(2)}) collective-permute-start(bf16[4,48,768]{2,1,0:T(8,128)(2,1)S(1)} %fusion.18), channel_id=1, source_target_pairs={{0,16},{8,24},{16,0},{24,8},{1,17},{9,25},{17,1},{25,9},{2,18},{10... | collective-permute-start | bytes 884744 | tf_op jit(solution)/shard_map/ppermute | solution.py:69
  182.0 8.1 %collective-permute-start.55 = (bf16[2,2,48,768]{3,2,0,1:T(8,128)(2,1)S(1)}, bf16[2,2,48,768]{3,2,0,1:T(8,128)(2,1)S(1)}, u32[]{:S(2)}, u32[]{:S(2)}) collective-permute-start(bf16[2,2,48,768]{3,2,0,1:T(8,128)(2,1)S(1)} %fusion.12), channel_id=1, source_target_pairs={{0,2},{1,3},{2,0},{3,1},{4,6},{5,7},{6,4},{7,5},{8,10},{9,11},{10,... | collective-permute-start | bytes 884744 | tf_op jit(solution)/shard_map/ppermute | solution.py:69
  183.9 14.6 %collective-permute-start.58 = (bf16[2,2,48,768]{3,2,1,0:T(8,128)(2,1)S(1)}, bf16[2,2,48,768]{3,2,1,0:T(8,128)(2,1)S(1)}, u32[]{:S(2)}, u32[]{:S(2)}) collective-permute-start(bf16[2,2,48,768]{3,2,1,0:T(8,128)(2,1)S(1)} %pad_maximum_fusion.19.p0), channel_id=1, source_target_pairs={{0,8},{8,0},{16,24},{24,16},{1,9},{9,1},{17,25},{25,17},{2,10},{10... | collective-permute-start | bytes 884744 | tf_op jit(solution)/shard_map/ppermute | solution.py:69
  184.0 9.4 %collective-permute-start.59 = (bf16[2,2,48,768]{3,2,1,0:T(8,128)(2,1)S(1)}, bf16[2,2,48,768]{3,2,1,0:T(8,128)(2,1)S(1)}, u32[]{:S(2)}, u32[]{:S(2)}) collective-permute-start(bf16[2,2,48,768]{3,2,1,0:T(8,128)(2,1)S(1)} %pad_maximum_fusion.19.p0), channel_id=1, source_target_pairs={{0,16},{8,24},{16,0},{24,8},{1,17},{9,25},{17,1},{25,9},{2,18},{10... | collective-permute-start | bytes 884744 | tf_op jit(solution)/shard_map/ppermute | solution.py:69
  194.9 10.0 %collective-permute-start.57 = (bf16[1,2,48,768]{3,2,0,1:T(8,128)(2,1)S(1)}, bf16[1,2,48,768]{3,2,0,1:T(8,128)(2,1)S(1)}, u32[]{:S(2)}, u32[]{:S(2)}) collective-permute-start(bf16[1,2,48,768]{3,2,0,1:T(8,128)(2,1)S(1)} %slice.406), channel_id=1, source_target_pairs={{0,4},{1,5},{2,6},{3,7},{4,0},{5,1},{6,2},{7,3},{8,12},{9,13},{10,... | collective-permute-start | bytes 442376 | tf_op jit(solution)/shard_map/ppermute | solution.py:69
  198.4 7.9 %collective-permute-start.56 = (bf16[16,768]{1,0:T(8,128)(2,1)S(1)}, bf16[16,768]{1,0:T(8,128)(2,1)S(1)}, u32[]{:S(2)}, u32[]{:S(2)}) collective-permute-start(bf16[16,768]{1,0:T(8,128)(2,1)S(1)} %fusion.37), channel_id=1, source_target_pairs={{0,2},{1,3},{2,0},{3,1},{4,6},{5,7},{6,4},{7,5},{8,10},{9,11},{10,... | collective-permute-start | bytes 73736 | tf_op jit(solution)/shard_map/ppermute | solution.py:69
  (32 other events, 268.2 us)

commit v2 on v1

--- a/solution.py
+++ b/solution.py
@@ -871,14 +871,13 @@
         h,
     )
     s1 = Scatter(send1)
-    s2.got_last = after_all(s2.got_last, send1)
+    keep1 = first_grad(
+        idx, after(normed, send1), mixed, three_grad, branch_grad, keep_rs, masks, fsdp, h
+    )
+    s2.got_last = after_all(s2.got_last, keep1)
     rows2 = Inner(s2.rows())
     front = rows2.step()
-    keep1 = first_grad(
-        idx, after(normed, front, send1), mixed, three_grad, branch_grad, keep_rs, masks, fsdp, h
-    )
     s1.sides(keep1)
-    front = rows2.step(*s1.done)
     input_grad, sums_in = input_grads(
         after(tokens, *s1.done, front), three_grad, first4, small, residual_grad
     )
@@ -895,7 +894,6 @@
     )
     s1.mid = after_all(s1.mid, output)
     s1.cross()
-    both = Spread(after(jnp.stack([rows2.sums(), rows3.sums()]), *s1.done))
     rest = [(fswap, m) for m in reversed(masks)]
     m = 2
     while m < dp:
@@ -904,6 +902,8 @@
     small_sum = small_sum + after(small_got, output).astype(F32)
     low, small_got = small_step(*rest.pop(), *s1.done)
     rows1 = Inner(s1.rows())
+    rows2.got = after(rows2.got, rows1.cur)
+    both = Spread(jnp.stack([rows2.sums(), rows3.sums()]))
     small_sum = small_sum + after(small_got, rows1.cur).astype(F32)
     front = rows1.step()
     low, small_got = small_step(*rest.pop(), front)

time: 216 us -> 211 us (0.977)
  waiting for transfers between devices: 71.3 us -> 67.1 us
    ppermute x65, waiting for transfers between devices: 71.3 us -> 67.1 us  [swap(): return lax.ppermute(values, axis, [(i, i ^ mask) for i in range(size)])]
  transfers between devices with their start and end apart: 65 -> 65, of which waited for: 28 -> 30; matrix products, arithmetic and copies ran while one was open for 7% -> 7% of each run, Pallas kernels for 30% -> 31%
where the time goes in v2:
time: 211 us
  waiting for transfers between devices  67.1 us (32%)
  Pallas kernels  64.8 us (31%)
  starting transfers between devices  59 us (28%)
  local copies, waits for them, and re-layouts  9.5 us (5%)
  other arithmetic  9.41 us (4%)
    ppermute x65, waiting for transfers between devices, swap(): return lax.ppermute(values, axis, [(i, i ^ mask) for i in range(size)])  67.1 us
    ppermute x65, starting transfers between devices, swap(): return lax.ppermute(values, axis, [(i, i ^ mask) for i in range(size)])  59 us
    pallas_call x2, Pallas kernels, act_grad(): pl.pallas_call(partial(act_grad_kernel, masks, maps, rs, h, shards, not b...  10.8 us
    pallas_call x2, Pallas kernels, up(): pl.pallas_call(partial(up_kernel, masks, maps, rs, h, shards), out_shape=...  10.4 us
    pallas_call x1, Pallas kernels, attend_back(): pl.pallas_call(attend_back_kernel, grid=(d // pair,), out_shape=jax.Shape...  9.73 us
    pallas_call x1, Pallas kernels, attend(): pl.pallas_call(attend_kernel, grid=(d // pair,), out_shape=(jax.ShapeDtyp...  8.77 us
    pallas_call x1, Pallas kernels, input_grads(): pl.pallas_call(input_kernel, grid=(3,), out_shape=(jax.ShapeDtypeStruct((...  5.15 us
    pallas_call x2, Pallas kernels, first_grad(): pl.pallas_call(partial(first_grad_kernel, masks, h, shards, rs), grid_spe...  4.94 us
  transfers between devices with their start and end apart: 65, of which 30 were waited for; matrix products, arithmetic and copies ran while one was open for 7% of the time, Pallas kernels for 31%

profile of v2, /device:TPU:0, one launch (start us, length us, event | category | flops | bytes accessed | tf_op | source)
XLA Modules:
  0.0 211.2 jit_solution(10123514771138924217)
XLA Ops:
  1.8 4.1 %collective-permute-start = (bf16[1,96,768]{2,1,0:T(8,128)(2,1)S(1)}, bf16[1,96,768]{2,1,0:T(8,128)(2,1)S(1)}, u32[]{:S(2)}, u32[]{:S(2)}) collective-permute-start(bf16[1,96,768]{2,1,0:T(8,128)(2,1)S(1)} %bitcast.161), channel_id=1, source_target_pairs={{0,4},{1,5},{2,6},{3,7},{4,0},{5,1},{6,2},{7,3},{8,12},{9,13},{10,... | collective-permute-start | bytes 442376 | tf_op jit(solution)/shard_map/ppermute | solution.py:69
  5.9 4.1 %concatenate.55 = bf16[864]{0:T(1024)(128)(2,1)S(1)} concatenate(bf16[96]{0:T(256)(128)(2,1)} %param.17, bf16[96]{0:T(256)(128)(2,1)} %param.18, bf16[96]{0:T(256)(128)(2,1)} %param.23, bf16[96]{0:T(256)(128)(2,1)} %param.24, bf16[96]{0:T(256)(128)(2,1)} %param.28, bf16[384]{0:T(512)(128)(2,1)} %param.26), dimensions={0} | concatenate | bytes 3456 | tf_op jit(solution)/shard_map/concatenate | solution.py:756
  10.3 1.6 collective-permute-start.2
  11.9 2.3 %reshape.252 = bf16[96,8,4,96]{3,2,1,0:T(4,128)(2,1)S(1)} reshape(bf16[96,3072]{1,0:T(8,128)(2,1)} %param.25) | data formatting | bytes 1179648 | tf_op jit(solution)/shard_map/reshape | solution.py:768
  15.7 1.6 collective-permute-start.1
  17.8 6.2 %collective-permute-done.1 = bf16[2,96,768]{2,1,0:T(8,128)(2,1)S(1)} collective-permute-done((bf16[2,96,768]{2,1,0:T(8,128)(2,1)S(1)}, bf16[2,96,768]{2,1,0:T(8,128)(2,1)S(1)}, u32[]{:S(2)}, u32[]{:S(2)}) %collective-permute-start.1) | collective-permute-done | bytes 294944 | tf_op jit(solution)/shard_map/ppermute | solution.py:69
  24.0 1.6 collective-permute-start.3
  26.2 1.6 collective-permute-start.8
  28.5 1.6 collective-permute-start.4
  30.1 2.7 %collective-permute-done.6 = bf16[4,48,768]{2,1,0:T(8,128)(2,1)S(1)} collective-permute-done((bf16[4,48,768]{2,1,0:T(8,128)(2,1)S(1)}, bf16[4,48,768]{2,1,0:T(8,128)(2,1)S(1)}, u32[]{:S(2)}, u32[]{:S(2)}) %collective-permute-start.6) | collective-permute-done | bytes 294944 | tf_op jit(solution)/shard_map/ppermute | solution.py:69
  32.8 1.6 collective-permute-start.7
  34.4 1.6 collective-permute-start.9
  39.0 1.7 collective-permute-start.10
  40.7 2.9 %collective-permute-done.11 = bf16[16,768]{1,0:T(8,128)(2,1)S(1)} collective-permute-done((bf16[16,768]{1,0:T(8,128)(2,1)S(1)}, bf16[16,768]{1,0:T(8,128)(2,1)S(1)}, u32[]{:S(2)}, u32[]{:S(2)}) %collective-permute-start.11) | collective-permute-done | bytes 24608 | tf_op jit(solution)/shard_map/ppermute | solution.py:69
  43.7 2.6 %collective-permute-done.10 = bf16[1,96,768]{2,1,0:T(8,128)(2,1)S(1)} collective-permute-done((bf16[1,96,768]{2,1,0:T(8,128)(2,1)S(1)}, bf16[1,96,768]{2,1,0:T(8,128)(2,1)S(1)}, u32[]{:S(2)}, u32[]{:S(2)}) %collective-permute-start.10) | collective-permute-done | bytes 147488 | tf_op jit(solution)/shard_map/ppermute | solution.py:69
  51.3 4.7 %qkv.1 = (bf16[512,768]{1,0:T(8,128)(2,1)S(1)}, bf16[3,512,768]{2,1,0:T(8,128)(2,1)S(1)}, bf16[4,8,96,768]{3,2,1,0:T(8,128)(2,1)S(1)}) custom-call(s32[2]{0:T(128)S(1)} %pad_add_fusion.idx_ref, bf16[512,768]{1,0:T(8,128)(2,1)S(1)} %copy-done.7, f32[16,768]{1,0:T(8,128)S(1)} %add_convert_fusion.small_ref, f32[512,128]{1,0:T(8,128)S(1)} %get-tuple-element.261.cos_ref, ...), custom_call_target="tpu_custom_call" | custom-call | flops 48000000000 | bytes 13369344 | tf_op jit(solution)/shard_map/qkv/pallas_call | solution.py:180
  56.1 2.5 %collective-permute-done.16 = bf16[4,48,768]{2,1,0:T(8,128)(2,1)S(1)} collective-permute-done((bf16[4,48,768]{2,1,0:T(8,128)(2,1)S(1)}, bf16[4,48,768]{2,1,0:T(8,128)(2,1)S(1)}, u32[]{:S(2)}, u32[]{:S(2)}) %collective-permute-start.16) | collective-permute-done | bytes 294944 | tf_op jit(solution)/shard_map/ppermute | solution.py:69
  60.3 1.6 collective-permute-start.19
  62.4 8.8 %attend.1 = (bf16[512,768]{1,0:T(8,128)(2,1)S(1)}, bf16[12,512,512]{2,1,0:T(8,128)(2,1)S(1)}) custom-call(bf16[3,512,768]{2,1,0:T(8,128)(2,1)S(1)} %get-tuple-element.126.q_ref.k_ref.v_ref, bf16[3,512,768]{2,1,0:T(8,128)(2,1)S(1)} %get-tuple-element.126.q_ref.k_ref.v_ref, bf16[3,512,768]{2,1,0:T(8,128)(2,1)S(1)} %get-tuple-element.126.q_ref.k_ref.v_ref, ...), custom_call_target="tpu_custom_call" | custom-call | flops 48000000000 | bytes 9437184 | tf_op jit(solution)/shard_map/attend/pallas_call | solution.py:219
  71.8 1.8 collective-permute-done.18.p1
  75.4 1.6 branch.1
  77.0 3.7 %collective-permute-done.23 = bf16[4,48,768]{2,1,0:T(8,128)(2,1)S(1)} collective-permute-done((bf16[4,48,768]{2,1,0:T(8,128)(2,1)S(1)}, bf16[4,48,768]{2,1,0:T(8,128)(2,1)S(1)}, u32[]{:S(2)}, u32[]{:S(2)}) %collective-permute-start.23) | collective-permute-done | bytes 294944 | tf_op jit(solution)/shard_map/ppermute | solution.py:69
  83.6 5.2 %up.2 = (bf16[2,512,768]{2,1,0:T(8,128)(2,1)S(1)}, bf16[2,512,768]{2,1,0:T(8,128)(2,1)S(1)}, bf16[2,2,8,48,768]{4,3,2,1,0:T(8,128)(2,1)S(1)}, bf16[2,8,96,768]{3,2,1,0:T(8,128)(2,1)S(1)}) custom-call(s32[2]{0:T(128)S(1)} %pad_add_fusion.idx_ref, bf16[512,768]{1,0:T(8,128)(2,1)S(1)} %get-tuple-element.140.hidden_ref.x_ref, bf16[512,768]{1,0:T(8,128)(2,1)S(1)} %copy-done.6, ...), custom_call_target="tpu_custom_call" | custom-call | flops 48000000000 | bytes 11796480 | tf_op jit(solution)/shard_map/up/pallas_call | solution.py:358
  89.3 5.2 %up.3 = (bf16[2,512,768]{2,1,0:T(8,128)(2,1)S(1)}, bf16[2,512,768]{2,1,0:T(8,128)(2,1)S(1)}, bf16[2,2,8,48,768]{4,3,2,1,0:T(8,128)(2,1)S(1)}, bf16[2,8,96,768]{3,2,1,0:T(8,128)(2,1)S(1)}) custom-call(s32[2]{0:T(128)S(1)} %pad_add_fusion.idx_ref, bf16[512,768]{1,0:T(8,128)(2,1)S(1)} %get-tuple-element.140.hidden_ref.x_ref, bf16[512,768]{1,0:T(8,128)(2,1)S(1)} %copy-done.6, ...), custom_call_target="tpu_custom_call" | custom-call | flops 48000000000 | bytes 11796480 | tf_op jit(solution)/shard_map/up/pallas_call | solution.py:358
  94.6 2.0 collective-permute-done.29.p1
  100.8 5.5 %act_grad.2 = (f32[512,768]{1,0:T(8,128)S(1)}, f32[16,768]{1,0:T(8,128)S(1)}, bf16[2,2,8,48,768]{4,3,2,1,0:T(8,128)(2,1)S(1)}, bf16[2,8,96,768]{3,2,1,0:T(8,128)(2,1)S(1)}) custom-call(s32[2]{0:T(128)S(1)} %pad_add_fusion.idx_ref, bf16[512,768]{1,0:T(8,128)(2,1)S(1)} %copy-done.6, bf16[512,768]{1,0:T(8,128)(2,1)S(1)} %get-tuple-element.140.hidden_ref.x_ref, ...), custom_call_target="tpu_custom_call" | custom-call | flops 48000000000 | bytes 15728640 | tf_op jit(solution)/shard_map/act_grad/pallas_call | solution.py:410
  106.4 7.1 %collective-permute-done.34 = bf16[8,48,768]{2,1,0:T(8,128)(2,1)S(1)} collective-permute-done((bf16[8,48,768]{2,1,0:T(8,128)(2,1)S(1)}, bf16[8,48,768]{2,1,0:T(8,128)(2,1)S(1)}, u32[]{:S(2)}, u32[]{:S(2)}) %collective-permute-start.34) | collective-permute-done | bytes 589856 | tf_op jit(solution)/shard_map/ppermute | solution.py:69
  117.1 5.3 %act_grad.3 = (f32[512,768]{1,0:T(8,128)S(1)}, f32[16,768]{1,0:T(8,128)S(1)}, bf16[2,2,8,48,768]{4,3,2,1,0:T(8,128)(2,1)S(1)}, bf16[2,8,96,768]{3,2,1,0:T(8,128)(2,1)S(1)}) custom-call(s32[2]{0:T(128)S(1)} %pad_add_fusion.idx_ref, bf16[512,768]{1,0:T(8,128)(2,1)S(1)} %copy-done.6, bf16[512,768]{1,0:T(8,128)(2,1)S(1)} %get-tuple-element.140.hidden_ref.x_ref, ...), custom_call_target="tpu_custom_call" | custom-call | flops 48000000000 | bytes 15728640 | tf_op jit(solution)/shard_map/act_grad/pallas_call | solution.py:410
  127.0 2.1 middle.1
  130.5 2.4 %collective-permute-start.44 = (bf16[1,2,48,768]{3,2,1,0:T(8,128)(2,1)S(1)}, bf16[1,2,48,768]{3,2,1,0:T(8,128)(2,1)S(1)}, u32[]{:S(2)}, u32[]{:S(2)}) collective-permute-start(bf16[1,2,48,768]{3,2,1,0:T(8,128)(2,1)S(1)} %slice.380), channel_id=1, source_target_pairs={{0,4},{1,5},{2,6},{3,7},{4,0},{5,1},{6,2},{7,3},{8,12},{9,13},{10,... | collective-permute-start | bytes 442376 | tf_op jit(solution)/shard_map/ppermute | solution.py:69
  133.0 9.7 %attend_back.1.three_ref = bf16[3,512,768]{2,1,0:T(8,128)(2,1)S(1)} custom-call(bf16[3,512,768]{2,1,0:T(8,128)(2,1)S(1)} %copy-done.10, bf16[3,512,768]{2,1,0:T(8,128)(2,1)S(1)} %copy-done.10, bf16[3,512,768]{2,1,0:T(8,128)(2,1)S(1)} %copy-done.10, bf16[12,512,512]{2,1,0:T(8,128)(2,1)S(1)} %get-tuple-element.160.probs_ref, ...), custom_call_target="tpu_custom_call" | custom-call | flops 48000000000 | bytes 12582912 | tf_op jit(solution)/shard_map/attend_back/pallas_call | solution.py:269
  144.9 2.5 %first_grad.2 = bf16[2,2,8,48,768]{4,3,2,1,0:T(8,128)(2,1)S(1)} custom-call(s32[2]{0:T(128)S(1)} %pad_add_fusion.idx_ref, bf16[512,768]{1,0:T(8,128)(2,1)S(1)} %get-tuple-element.174.normed_ref, bf16[512,768]{1,0:T(8,128)(2,1)S(1)} %copy-done.12, bf16[3,512,768]{2,1,0:T(8,128)(2,1)S(1)} %attend_back.1.three_ref, ...), custom_call_target="tpu_custom_call" | custom-call | flops 48000000000 | bytes 6291456 | tf_op jit(solution)/shard_map/first_grad/pallas_call | solution.py:444
  147.4 2.5 %first_grad.3 = bf16[2,2,8,48,768]{4,3,2,1,0:T(8,128)(2,1)S(1)} custom-call(s32[2]{0:T(128)S(1)} %pad_add_fusion.idx_ref, bf16[512,768]{1,0:T(8,128)(2,1)S(1)} %get-tuple-element.174.normed_ref, bf16[512,768]{1,0:T(8,128)(2,1)S(1)} %copy-done.12, bf16[3,512,768]{2,1,0:T(8,128)(2,1)S(1)} %attend_back.1.three_ref, ...), custom_call_target="tpu_custom_call" | custom-call | flops 48000000000 | bytes 6291456 | tf_op jit(solution)/shard_map/first_grad/pallas_call | solution.py:444
  152.1 1.9 collective-permute-start.48
  155.3 5.2 %input_grads.1 = (f32[512,768]{1,0:T(8,128)}, f32[16,768]{1,0:T(8,128)S(1)}) custom-call(bf16[512,768]{1,0:T(8,128)(2,1)S(1)} %copy-done.8, bf16[3,512,768]{2,1,0:T(8,128)(2,1)S(1)} %attend_back.1.three_ref, bf16[4,768,768]{2,1,0:T(8,128)(2,1)S(1)} %bitcast.156, f32[16,768]{1,0:T(8,128)S(1)} %add_convert_fusion.small_ref, ...), custom_call_target="tpu_custom_call" | custom-call | flops 48000000000 | bytes 9830400 | tf_op jit(solution)/shard_map/input_grads/pallas_call | solution.py:538
  161.2 4.0 %down_out.1 = bf16[512,768]{1,0:T(8,128)(2,1)} custom-call(bf16[2,512,768]{2,1,0:T(8,128)(2,1)S(1)} %get-tuple-element.138.a0_ref, bf16[2,512,768]{2,1,0:T(8,128)(2,1)S(1)} %get-tuple-element.141.a1_ref, bf16[2,768,768]{2,1,0:T(8,128)(2,1)S(1)} %bitcast.157, bf16[2,768,768]{2,1,0:T(8,128)(2,1)S(1)} %bitcast.158, f32[16,768]{1,0:T(8,128)S(1)} %add_convert_fusion.small_ref, ...), custom_call_target="tpu_custom_call" | custom-call | flops 48000000000 | bytes 10223616 | tf_op jit(solution)/shard_map/down_out/pallas_call | solution.py:575
  165.2 2.5 %collective-permute-done.48 = bf16[8,48,768]{2,1,0:T(8,128)(2,1)S(1)} collective-permute-done((bf16[8,48,768]{2,1,0:T(8,128)(2,1)S(1)}, bf16[8,48,768]{2,1,0:T(8,128)(2,1)S(1)}, u32[]{:S(2)}, u32[]{:S(2)}) %collective-permute-start.48) | collective-permute-done | bytes 589856 | tf_op jit(solution)/shard_map/ppermute | solution.py:69
  167.7 1.7 collective-permute-done.49
  170.9 6.5 %collective-permute-done.51 = bf16[4,48,768]{2,1,0:T(8,128)(2,1)S(1)} collective-permute-done((bf16[4,48,768]{2,1,0:T(8,128)(2,1)S(1)}, bf16[4,48,768]{2,1,0:T(8,128)(2,1)S(1)}, u32[]{:S(2)}, u32[]{:S(2)}) %collective-permute-start.51) | collective-permute-done | bytes 294944 | tf_op jit(solution)/shard_map/ppermute | solution.py:69
  179.5 1.6 collective-permute-start.59
  182.2 3.4 %collective-permute-done.54 = bf16[2,2,48,768]{3,2,0,1:T(8,128)(2,1)S(1)} collective-permute-done((bf16[2,2,48,768]{3,2,0,1:T(8,128)(2,1)S(1)}, bf16[2,2,48,768]{3,2,0,1:T(8,128)(2,1)S(1)}, u32[]{:S(2)}, u32[]{:S(2)}) %collective-permute-start.54) | collective-permute-done | bytes 294944 | tf_op jit(solution)/shard_map/ppermute | solution.py:69
  185.6 3.3 %collective-permute-done.59.p2 = bf16[2,2,48,768]{3,2,1,0:T(8,128)(2,1)S(1)} collective-permute-done((bf16[2,2,48,768]{3,2,1,0:T(8,128)(2,1)S(1)}, bf16[2,2,48,768]{3,2,1,0:T(8,128)(2,1)S(1)}, u32[]{:S(2)}, u32[]{:S(2)}) %collective-permute-start.59) | collective-permute-done | bytes 294944 | tf_op jit(solution)/shard_map/ppermute | solution.py:69
  188.9 1.9 collective-permute-start.53
  191.8 1.8 collective-permute-done.53
  193.6 1.6 collective-permute-start.55
  195.2 2.6 %last_out.1 = (f32[96,3072]{1,0:T(8,128)}, f32[384,768]{1,0:T(8,128)}) custom-call(s32[2]{0:T(128)S(1)} %pad_add_fusion.idx_ref, bf16[2,2,48,768]{3,2,1,0:T(8,128)(2,1)S(1)} %pad_maximum_fusion.19.p0, bf16[2,2,48,768]{3,2,1,0:T(8,128)(2,1)S(1)} %collective-permute-done.58.p1, bf16[2,2,48,768]{3,2,1,0:T(8,128)(2,1)S(1)} %collective-permute-done.59.p2, ...), custom_call_target="tpu_custom_call" | custom-call | tf_op jit(solution)/shard_map/last_out/pallas_call | solution.py:610
  197.8 3.1 %collective-permute-done.56 = bf16[1,2,48,768]{3,2,0,1:T(8,128)(2,1)S(1)} collective-permute-done((bf16[1,2,48,768]{3,2,0,1:T(8,128)(2,1)S(1)}, bf16[1,2,48,768]{3,2,0,1:T(8,128)(2,1)S(1)}, u32[]{:S(2)}, u32[]{:S(2)}) %collective-permute-start.56) | collective-permute-done | bytes 147488 | tf_op jit(solution)/shard_map/ppermute | solution.py:69
  203.1 2.8 %collective-permute-done.61 = bf16[16,768]{1,0:T(8,128)(2,1)S(1)} collective-permute-done((bf16[16,768]{1,0:T(8,128)(2,1)S(1)}, bf16[16,768]{1,0:T(8,128)(2,1)S(1)}, u32[]{:S(2)}, u32[]{:S(2)}) %collective-permute-start.61) | collective-permute-done | bytes 24608 | tf_op jit(solution)/shard_map/ppermute | solution.py:69
  (218 shorter events, 54.2 us)
Async XLA Ops:
  1.8 13.9 %collective-permute-start = (bf16[1,96,768]{2,1,0:T(8,128)(2,1)S(1)}, bf16[1,96,768]{2,1,0:T(8,128)(2,1)S(1)}, u32[]{:S(2)}, u32[]{:S(2)}) collective-permute-start(bf16[1,96,768]{2,1,0:T(8,128)(2,1)S(1)} %bitcast.161), channel_id=1, source_target_pairs={{0,4},{1,5},{2,6},{3,7},{4,0},{5,1},{6,2},{7,3},{8,12},{9,13},{10,... | collective-permute-start | bytes 442376 | tf_op jit(solution)/shard_map/ppermute | solution.py:69
  15.7 8.3 %collective-permute-start.1 = (bf16[2,96,768]{2,1,0:T(8,128)(2,1)S(1)}, bf16[2,96,768]{2,1,0:T(8,128)(2,1)S(1)}, u32[]{:S(2)}, u32[]{:S(2)}) collective-permute-start(bf16[2,96,768]{2,1,0:T(8,128)(2,1)S(1)} %pad_maximum_fusion.8), channel_id=1, source_target_pairs={{0,2},{1,3},{2,0},{3,1},{4,6},{5,7},{6,4},{7,5},{8,10},{9,11},{10,... | collective-permute-start | bytes 884744 | tf_op jit(solution)/shard_map/ppermute | solution.py:69
  25.6 7.1 %collective-permute-start.6 = (bf16[4,48,768]{2,1,0:T(8,128)(2,1)S(1)}, bf16[4,48,768]{2,1,0:T(8,128)(2,1)S(1)}, u32[]{:S(2)}, u32[]{:S(2)}) collective-permute-start(bf16[4,48,768]{2,1,0:T(8,128)(2,1)S(1)} %pad_maximum_fusion.12), channel_id=1, source_target_pairs={{0,1},{1,0},{2,3},{3,2},{4,5},{5,4},{6,7},{7,6},{8,9},{9,8},{10,11... | collective-permute-start | bytes 884744 | tf_op jit(solution)/shard_map/ppermute | solution.py:69
  26.2 8.1 %collective-permute-start.8 = (bf16[4,48,768]{2,1,0:T(8,128)(2,1)S(1)}, bf16[4,48,768]{2,1,0:T(8,128)(2,1)S(1)}, u32[]{:S(2)}, u32[]{:S(2)}) collective-permute-start(bf16[4,48,768]{2,1,0:T(8,128)(2,1)S(1)} %pad_maximum_fusion.13), channel_id=1, source_target_pairs={{0,16},{8,24},{16,0},{24,8},{1,17},{9,25},{17,1},{25,9},{2,18},{10... | collective-permute-start | bytes 884744 | tf_op jit(solution)/shard_map/ppermute | solution.py:69
  28.5 9.8 %collective-permute-start.4 = (bf16[1,96,768]{2,1,0:T(8,128)(2,1)S(1)}, bf16[1,96,768]{2,1,0:T(8,128)(2,1)S(1)}, u32[]{:S(2)}, u32[]{:S(2)}) collective-permute-start(bf16[1,96,768]{2,1,0:T(8,128)(2,1)S(1)} %bitcast.166), channel_id=1, source_target_pairs={{0,4},{1,5},{2,6},{3,7},{4,0},{5,1},{6,2},{7,3},{8,12},{9,13},{10,... | collective-permute-start | bytes 442376 | tf_op jit(solution)/shard_map/ppermute | solution.py:69
  32.8 13.5 %collective-permute-start.7 = (bf16[8,48,768]{2,1,0:T(8,128)(2,1)S(1)}, bf16[8,48,768]{2,1,0:T(8,128)(2,1)S(1)}, u32[]{:S(2)}, u32[]{:S(2)}) collective-permute-start(bf16[8,48,768]{2,1,0:T(8,128)(2,1)S(1)} %pad_maximum_fusion.1.p0), channel_id=1, source_target_pairs={{0,16},{8,24},{16,0},{24,8},{1,17},{9,25},{17,1},{25,9},{2,18},{10... | collective-permute-start | bytes 1769480 | tf_op jit(solution)/shard_map/ppermute | solution.py:69
  34.4 12.3 %collective-permute-start.9 = (bf16[8,48,768]{2,1,0:T(8,128)(2,1)S(1)}, bf16[8,48,768]{2,1,0:T(8,128)(2,1)S(1)}, u32[]{:S(2)}, u32[]{:S(2)}) collective-permute-start(bf16[8,48,768]{2,1,0:T(8,128)(2,1)S(1)} %pad_maximum_fusion.2.p2), channel_id=1, source_target_pairs={{0,1},{1,0},{2,3},{3,2},{4,5},{5,4},{6,7},{7,6},{8,9},{9,8},{10,11... | collective-permute-start | bytes 1769480 | tf_op jit(solution)/shard_map/ppermute | solution.py:69
  37.1 6.5 %collective-permute-start.11 = (bf16[16,768]{1,0:T(8,128)(2,1)S(1)}, bf16[16,768]{1,0:T(8,128)(2,1)S(1)}, u32[]{:S(2)}, u32[]{:S(2)}) collective-permute-start(bf16[16,768]{1,0:T(8,128)(2,1)S(1)} %add.242), channel_id=1, source_target_pairs={{0,4},{1,5},{2,6},{3,7},{4,0},{5,1},{6,2},{7,3},{8,12},{9,13},{10,... | collective-permute-start | bytes 73736 | tf_op jit(solution)/shard_map/ppermute | solution.py:69
  38.4 9.6 %collective-permute-start.5 = (bf16[2,96,768]{2,1,0:T(8,128)(2,1)S(1)}, bf16[2,96,768]{2,1,0:T(8,128)(2,1)S(1)}, u32[]{:S(2)}, u32[]{:S(2)}) collective-permute-start(bf16[2,96,768]{2,1,0:T(8,128)(2,1)S(1)} %pad_maximum_fusion.11), channel_id=1, source_target_pairs={{0,2},{1,3},{2,0},{3,1},{4,6},{5,7},{6,4},{7,5},{8,10},{9,11},{10,... | collective-permute-start | bytes 884744 | tf_op jit(solution)/shard_map/ppermute | solution.py:69
  39.0 7.3 %collective-permute-start.10 = (bf16[1,96,768]{2,1,0:T(8,128)(2,1)S(1)}, bf16[1,96,768]{2,1,0:T(8,128)(2,1)S(1)}, u32[]{:S(2)}, u32[]{:S(2)}) collective-permute-start(bf16[1,96,768]{2,1,0:T(8,128)(2,1)S(1)} %dynamic-slice_bitcast_fusion), channel_id=1, source_target_pairs={{0,4},{1,5},{2,6},{3,7},{4,0},{5,1},{6,2},{7,3},{8,12},{9,13},{10,... | collective-permute-start | bytes 442376 | tf_op jit(solution)/shard_map/ppermute | solution.py:69
  48.0 23.2 %collective-permute-start.22 = (bf16[2,96,768]{2,1,0:T(8,128)(2,1)S(1)}, bf16[2,96,768]{2,1,0:T(8,128)(2,1)S(1)}, u32[]{:S(2)}, u32[]{:S(2)}) collective-permute-start(bf16[2,96,768]{2,1,0:T(8,128)(2,1)S(1)} %pad_maximum_fusion.16), channel_id=1, source_target_pairs={{0,2},{1,3},{2,0},{3,1},{4,6},{5,7},{6,4},{7,5},{8,10},{9,11},{10,... | collective-permute-start | bytes 884744 | tf_op jit(solution)/shard_map/ppermute | solution.py:69
  49.4 9.1 %collective-permute-start.16 = (bf16[4,48,768]{2,1,0:T(8,128)(2,1)S(1)}, bf16[4,48,768]{2,1,0:T(8,128)(2,1)S(1)}, u32[]{:S(2)}, u32[]{:S(2)}) collective-permute-start(bf16[4,48,768]{2,1,0:T(8,128)(2,1)S(1)} %pad_maximum_fusion.14), channel_id=1, source_target_pairs={{0,1},{1,0},{2,3},{3,2},{4,5},{5,4},{6,7},{7,6},{8,9},{9,8},{10,11... | collective-permute-start | bytes 884744 | tf_op jit(solution)/shard_map/ppermute | solution.py:69
  50.3 8.8 %collective-permute-start.17 = (bf16[4,48,768]{2,1,0:T(8,128)(2,1)S(1)}, bf16[4,48,768]{2,1,0:T(8,128)(2,1)S(1)}, u32[]{:S(2)}, u32[]{:S(2)}) collective-permute-start(bf16[4,48,768]{2,1,0:T(8,128)(2,1)S(1)} %pad_maximum_fusion.15), channel_id=1, source_target_pairs={{0,16},{8,24},{16,0},{24,8},{1,17},{9,25},{17,1},{25,9},{2,18},{10... | collective-permute-start | bytes 884744 | tf_op jit(solution)/shard_map/ppermute | solution.py:69
  59.2 14.3 %collective-permute-start.18 = (bf16[8,48,768]{2,1,0:T(8,128)(2,1)S(1)}, bf16[8,48,768]{2,1,0:T(8,128)(2,1)S(1)}, u32[]{:S(2)}, u32[]{:S(2)}) collective-permute-start(bf16[8,48,768]{2,1,0:T(8,128)(2,1)S(1)} %pad_maximum_fusion.3.p0), channel_id=1, source_target_pairs={{0,16},{8,24},{16,0},{24,8},{1,17},{9,25},{17,1},{25,9},{2,18},{10... | collective-permute-start | bytes 1769480 | tf_op jit(solution)/shard_map/ppermute | solution.py:69
  60.3 14.6 %collective-permute-start.19 = (bf16[8,48,768]{2,1,0:T(8,128)(2,1)S(1)}, bf16[8,48,768]{2,1,0:T(8,128)(2,1)S(1)}, u32[]{:S(2)}, u32[]{:S(2)}) collective-permute-start(bf16[8,48,768]{2,1,0:T(8,128)(2,1)S(1)} %pad_maximum_fusion.4.p2), channel_id=1, source_target_pairs={{0,1},{1,0},{2,3},{3,2},{4,5},{5,4},{6,7},{7,6},{8,9},{9,8},{10,11... | collective-permute-start | bytes 1769480 | tf_op jit(solution)/shard_map/ppermute | solution.py:69
  61.9 13.0 %collective-permute-start.20 = (bf16[8,48,768]{2,1,0:T(8,128)(2,1)S(1)}, bf16[8,48,768]{2,1,0:T(8,128)(2,1)S(1)}, u32[]{:S(2)}, u32[]{:S(2)}) collective-permute-start(bf16[8,48,768]{2,1,0:T(8,128)(2,1)S(1)} %pad_maximum_fusion.3.p0), channel_id=1, source_target_pairs={{0,8},{8,0},{16,24},{24,16},{1,9},{9,1},{17,25},{25,17},{2,10},{10... | collective-permute-start | bytes 1769480 | tf_op jit(solution)/shard_map/ppermute | solution.py:69
  61.9 13.5 %collective-permute-start.21 = (bf16[8,48,768]{2,1,0:T(8,128)(2,1)S(1)}, bf16[8,48,768]{2,1,0:T(8,128)(2,1)S(1)}, u32[]{:S(2)}, u32[]{:S(2)}) collective-permute-start(bf16[8,48,768]{2,1,0:T(8,128)(2,1)S(1)} %pad_maximum_fusion.4.p2), channel_id=1, source_target_pairs={{0,8},{8,0},{16,24},{24,16},{1,9},{9,1},{17,25},{25,17},{2,10},{10... | collective-permute-start | bytes 1769480 | tf_op jit(solution)/shard_map/ppermute | solution.py:69
  71.3 9.4 %collective-permute-start.23 = (bf16[4,48,768]{2,1,0:T(8,128)(2,1)S(1)}, bf16[4,48,768]{2,1,0:T(8,128)(2,1)S(1)}, u32[]{:S(2)}, u32[]{:S(2)}) collective-permute-start(bf16[4,48,768]{2,1,0:T(8,128)(2,1)S(1)} %pad_maximum_fusion.17), channel_id=1, source_target_pairs={{0,1},{1,0},{2,3},{3,2},{4,5},{5,4},{6,7},{7,6},{8,9},{9,8},{10,11... | collective-permute-start | bytes 884744 | tf_op jit(solution)/shard_map/ppermute | solution.py:69
  73.6 7.1 %collective-permute-start.24 = (bf16[4,48,768]{2,1,0:T(8,128)(2,1)S(1)}, bf16[4,48,768]{2,1,0:T(8,128)(2,1)S(1)}, u32[]{:S(2)}, u32[]{:S(2)}) collective-permute-start(bf16[4,48,768]{2,1,0:T(8,128)(2,1)S(1)} %pad_maximum_fusion.18), channel_id=1, source_target_pairs={{0,16},{8,24},{16,0},{24,8},{1,17},{9,25},{17,1},{25,9},{2,18},{10... | collective-permute-start | bytes 884744 | tf_op jit(solution)/shard_map/ppermute | solution.py:69
  74.8 8.7 %collective-permute-start.25 = (bf16[8,48,768]{2,1,0:T(8,128)(2,1)S(1)}, bf16[8,48,768]{2,1,0:T(8,128)(2,1)S(1)}, u32[]{:S(2)}, u32[]{:S(2)}) collective-permute-start(bf16[8,48,768]{2,1,0:T(8,128)(2,1)S(1)} %collective-permute-done.18.p1), channel_id=1, source_target_pairs={{0,8},{8,0},{16,24},{24,16},{1,9},{9,1},{17,25},{25,17},{2,10},{10... | collective-permute-start | bytes 1769480 | tf_op jit(solution)/shard_map/ppermute | solution.py:69
  74.9 8.7 %collective-permute-start.26 = (bf16[8,48,768]{2,1,0:T(8,128)(2,1)S(1)}, bf16[8,48,768]{2,1,0:T(8,128)(2,1)S(1)}, u32[]{:S(2)}, u32[]{:S(2)}) collective-permute-start(bf16[8,48,768]{2,1,0:T(8,128)(2,1)S(1)} %collective-permute-done.19.p3), channel_id=1, source_target_pairs={{0,8},{8,0},{16,24},{24,16},{1,9},{9,1},{17,25},{25,17},{2,10},{10... | collective-permute-start | bytes 1769480 | tf_op jit(solution)/shard_map/ppermute | solution.py:69
  80.8 18.5 %collective-permute-start.28 = (bf16[8,48,768]{2,1,0:T(8,128)(2,1)S(1)}, bf16[8,48,768]{2,1,0:T(8,128)(2,1)S(1)}, u32[]{:S(2)}, u32[]{:S(2)}) collective-permute-start(bf16[8,48,768]{2,1,0:T(8,128)(2,1)S(1)} %pad_maximum_fusion.5.p0), channel_id=1, source_target_pairs={{0,8},{8,0},{16,24},{24,16},{1,9},{9,1},{17,25},{25,17},{2,10},{10... | collective-permute-start | bytes 1769480 | tf_op jit(solution)/shard_map/ppermute | solution.py:69
  80.9 15.7 %collective-permute-start.29 = (bf16[8,48,768]{2,1,0:T(8,128)(2,1)S(1)}, bf16[8,48,768]{2,1,0:T(8,128)(2,1)S(1)}, u32[]{:S(2)}, u32[]{:S(2)}) collective-permute-start(bf16[8,48,768]{2,1,0:T(8,128)(2,1)S(1)} %pad_maximum_fusion.5.p0), channel_id=1, source_target_pairs={{0,16},{8,24},{16,0},{24,8},{1,17},{9,25},{17,1},{25,9},{2,18},{10... | collective-permute-start | bytes 1769480 | tf_op jit(solution)/shard_map/ppermute | solution.py:69
  82.1 15.4 %collective-permute-start.30 = (bf16[8,48,768]{2,1,0:T(8,128)(2,1)S(1)}, bf16[8,48,768]{2,1,0:T(8,128)(2,1)S(1)}, u32[]{:S(2)}, u32[]{:S(2)}) collective-permute-start(bf16[8,48,768]{2,1,0:T(8,128)(2,1)S(1)} %pad_maximum_fusion.6.p2), channel_id=1, source_target_pairs={{0,1},{1,0},{2,3},{3,2},{4,5},{5,4},{6,7},{7,6},{8,9},{9,8},{10,11... | collective-permute-start | bytes 1769480 | tf_op jit(solution)/shard_map/ppermute | solution.py:69
  83.6 17.3 %collective-permute-start.32 = (bf16[8,48,768]{2,1,0:T(8,128)(2,1)S(1)}, bf16[8,48,768]{2,1,0:T(8,128)(2,1)S(1)}, u32[]{:S(2)}, u32[]{:S(2)}) collective-permute-start(bf16[8,48,768]{2,1,0:T(8,128)(2,1)S(1)} %pad_maximum_fusion.6.p2), channel_id=1, source_target_pairs={{0,8},{8,0},{16,24},{24,16},{1,9},{9,1},{17,25},{25,17},{2,10},{10... | collective-permute-start | bytes 1769480 | tf_op jit(solution)/shard_map/ppermute | solution.py:69
  88.8 9.3 %collective-permute-start.27 = (bf16[2,2,8,48,768]{4,3,2,1,0:T(8,128)(2,1)S(1)}, bf16[2,2,8,48,768]{4,3,2,1,0:T(8,128)(2,1)S(1)}, u32[]{:S(2)}, u32[]{:S(2)}) collective-permute-start(bf16[2,2,8,48,768]{4,3,2,1,0:T(8,128)(2,1)S(1)} %get-tuple-element.139), channel_id=1, source_target_pairs={{0,8},{8,0},{16,24},{24,16},{1,9},{9,1},{17,25},{25,17},{2,10},{10... | collective-permute-start | bytes 7077896 | tf_op jit(solution)/shard_map/ppermute | solution.py:69
  98.2 15.3 %collective-permute-start.34 = (bf16[8,48,768]{2,1,0:T(8,128)(2,1)S(1)}, bf16[8,48,768]{2,1,0:T(8,128)(2,1)S(1)}, u32[]{:S(2)}, u32[]{:S(2)}) collective-permute-start(bf16[8,48,768]{2,1,0:T(8,128)(2,1)S(1)} %get-tuple-element.230), channel_id=1, source_target_pairs={{0,16},{8,24},{16,0},{24,8},{1,17},{9,25},{17,1},{25,9},{2,18},{10... | collective-permute-start | bytes 1769480 | tf_op jit(solution)/shard_map/ppermute | solution.py:69
  99.3 15.0 %collective-permute-start.35 = (bf16[2,4,48,768]{3,2,1,0:T(8,128)(2,1)S(1)}, bf16[2,4,48,768]{3,2,1,0:T(8,128)(2,1)S(1)}, u32[]{:S(2)}, u32[]{:S(2)}) collective-permute-start(bf16[2,4,48,768]{3,2,1,0:T(8,128)(2,1)S(1)} %get-tuple-element.228), channel_id=1, source_target_pairs={{0,1},{1,0},{2,3},{3,2},{4,5},{5,4},{6,7},{7,6},{8,9},{9,8},{10,11... | collective-permute-start | bytes 1769480 | tf_op jit(solution)/shard_map/ppermute | solution.py:69
  106.3 18.0 %collective-permute-start.36 = (bf16[2,2,8,48,768]{4,3,2,1,0:T(8,128)(2,1)S(1)}, bf16[2,2,8,48,768]{4,3,2,1,0:T(8,128)(2,1)S(1)}, u32[]{:S(2)}, u32[]{:S(2)}) collective-permute-start(bf16[2,2,8,48,768]{4,3,2,1,0:T(8,128)(2,1)S(1)} %get-tuple-element.149), channel_id=1, source_target_pairs={{0,8},{8,0},{16,24},{24,16},{1,9},{9,1},{17,25},{25,17},{2,10},{10... | collective-permute-start | bytes 7077896 | tf_op jit(solution)/shard_map/ppermute | solution.py:69
  114.4 8.1 %collective-permute-start.39 = (bf16[4,48,768]{2,1,0:T(8,128)(2,1)S(1)}, bf16[4,48,768]{2,1,0:T(8,128)(2,1)S(1)}, u32[]{:S(2)}, u32[]{:S(2)}) collective-permute-start(bf16[4,48,768]{2,1,0:T(8,128)(2,1)S(1)} %get-tuple-element.238), channel_id=1, source_target_pairs={{0,1},{1,0},{2,3},{3,2},{4,5},{5,4},{6,7},{7,6},{8,9},{9,8},{10,11... | collective-permute-start | bytes 884744 | tf_op jit(solution)/shard_map/ppermute | solution.py:69
  116.0 7.6 %collective-permute-start.40 = (bf16[4,48,768]{2,1,0:T(8,128)(2,1)S(1)}, bf16[4,48,768]{2,1,0:T(8,128)(2,1)S(1)}, u32[]{:S(2)}, u32[]{:S(2)}) collective-permute-start(bf16[4,48,768]{2,1,0:T(8,128)(2,1)S(1)} %get-tuple-element.236), channel_id=1, source_target_pairs={{0,16},{8,24},{16,0},{24,8},{1,17},{9,25},{17,1},{25,9},{2,18},{10... | collective-permute-start | bytes 884744 | tf_op jit(solution)/shard_map/ppermute | solution.py:69
  123.7 6.8 %collective-permute-start.41 = (bf16[2,2,48,768]{3,2,1,0:T(8,128)(2,1)S(1)}, bf16[2,2,48,768]{3,2,1,0:T(8,128)(2,1)S(1)}, u32[]{:S(2)}, u32[]{:S(2)}) collective-permute-start(bf16[2,2,48,768]{3,2,1,0:T(8,128)(2,1)S(1)} %fusion.11), channel_id=1, source_target_pairs={{0,2},{1,3},{2,0},{3,1},{4,6},{5,7},{6,4},{7,5},{8,10},{9,11},{10,... | collective-permute-start | bytes 884744 | tf_op jit(solution)/shard_map/ppermute | solution.py:69
  124.4 19.0 %collective-permute-start.37 = (bf16[8,48,768]{2,1,0:T(8,128)(2,1)S(1)}, bf16[8,48,768]{2,1,0:T(8,128)(2,1)S(1)}, u32[]{:S(2)}, u32[]{:S(2)}) collective-permute-start(bf16[8,48,768]{2,1,0:T(8,128)(2,1)S(1)} %get-tuple-element.224), channel_id=1, source_target_pairs={{0,16},{8,24},{16,0},{24,8},{1,17},{9,25},{17,1},{25,9},{2,18},{10... | collective-permute-start | bytes 1769480 | tf_op jit(solution)/shard_map/ppermute | solution.py:69
  125.9 17.5 %collective-permute-start.38 = (bf16[2,4,48,768]{3,2,1,0:T(8,128)(2,1)S(1)}, bf16[2,4,48,768]{3,2,1,0:T(8,128)(2,1)S(1)}, u32[]{:S(2)}, u32[]{:S(2)}) collective-permute-start(bf16[2,4,48,768]{3,2,1,0:T(8,128)(2,1)S(1)} %get-tuple-element.225), channel_id=1, source_target_pairs={{0,1},{1,0},{2,3},{3,2},{4,5},{5,4},{6,7},{7,6},{8,9},{9,8},{10,11... | collective-permute-start | bytes 1769480 | tf_op jit(solution)/shard_map/ppermute | solution.py:69
  130.5 12.2 %collective-permute-start.44 = (bf16[1,2,48,768]{3,2,1,0:T(8,128)(2,1)S(1)}, bf16[1,2,48,768]{3,2,1,0:T(8,128)(2,1)S(1)}, u32[]{:S(2)}, u32[]{:S(2)}) collective-permute-start(bf16[1,2,48,768]{3,2,1,0:T(8,128)(2,1)S(1)} %slice.380), channel_id=1, source_target_pairs={{0,4},{1,5},{2,6},{3,7},{4,0},{5,1},{6,2},{7,3},{8,12},{9,13},{10,... | collective-permute-start | bytes 442376 | tf_op jit(solution)/shard_map/ppermute | solution.py:69
  143.5 6.8 %collective-permute-start.42 = (bf16[4,48,768]{2,1,0:T(8,128)(2,1)S(1)}, bf16[4,48,768]{2,1,0:T(8,128)(2,1)S(1)}, u32[]{:S(2)}, u32[]{:S(2)}) collective-permute-start(bf16[4,48,768]{2,1,0:T(8,128)(2,1)S(1)} %get-tuple-element.232), channel_id=1, source_target_pairs={{0,1},{1,0},{2,3},{3,2},{4,5},{5,4},{6,7},{7,6},{8,9},{9,8},{10,11... | collective-permute-start | bytes 884744 | tf_op jit(solution)/shard_map/ppermute | solution.py:69
  144.6 6.8 %collective-permute-start.43 = (bf16[4,48,768]{2,1,0:T(8,128)(2,1)S(1)}, bf16[4,48,768]{2,1,0:T(8,128)(2,1)S(1)}, u32[]{:S(2)}, u32[]{:S(2)}) collective-permute-start(bf16[4,48,768]{2,1,0:T(8,128)(2,1)S(1)} %get-tuple-element.233), channel_id=1, source_target_pairs={{0,16},{8,24},{16,0},{24,8},{1,17},{9,25},{17,1},{25,9},{2,18},{10... | collective-permute-start | bytes 884744 | tf_op jit(solution)/shard_map/ppermute | solution.py:69
  151.5 8.9 %collective-permute-start.45 = (bf16[2,2,48,768]{3,2,1,0:T(8,128)(2,1)S(1)}, bf16[2,2,48,768]{3,2,1,0:T(8,128)(2,1)S(1)}, u32[]{:S(2)}, u32[]{:S(2)}) collective-permute-start(bf16[2,2,48,768]{3,2,1,0:T(8,128)(2,1)S(1)} %pad_maximum_fusion.9), channel_id=1, source_target_pairs={{0,2},{1,3},{2,0},{3,1},{4,6},{5,7},{6,4},{7,5},{8,10},{9,11},{10,... | collective-permute-start | bytes 884744 | tf_op jit(solution)/shard_map/ppermute | solution.py:69
  152.1 15.6 %collective-permute-start.48 = (bf16[8,48,768]{2,1,0:T(8,128)(2,1)S(1)}, bf16[8,48,768]{2,1,0:T(8,128)(2,1)S(1)}, u32[]{:S(2)}, u32[]{:S(2)}) collective-permute-start(bf16[8,48,768]{2,1,0:T(8,128)(2,1)S(1)} %get-tuple-element.222), channel_id=1, source_target_pairs={{0,16},{8,24},{16,0},{24,8},{1,17},{9,25},{17,1},{25,9},{2,18},{10... | collective-permute-start | bytes 1769480 | tf_op jit(solution)/shard_map/ppermute | solution.py:69
  154.2 15.2 %collective-permute-start.49 = (bf16[2,4,48,768]{3,2,1,0:T(8,128)(2,1)S(1)}, bf16[2,4,48,768]{3,2,1,0:T(8,128)(2,1)S(1)}, u32[]{:S(2)}, u32[]{:S(2)}) collective-permute-start(bf16[2,4,48,768]{3,2,1,0:T(8,128)(2,1)S(1)} %get-tuple-element.220), channel_id=1, source_target_pairs={{0,1},{1,0},{2,3},{3,2},{4,5},{5,4},{6,7},{7,6},{8,9},{9,8},{10,11... | collective-permute-start | bytes 1769480 | tf_op jit(solution)/shard_map/ppermute | solution.py:69
  160.6 18.7 %collective-permute-start.57 = (bf16[1,2,48,768]{3,2,1,0:T(8,128)(2,1)S(1)}, bf16[1,2,48,768]{3,2,1,0:T(8,128)(2,1)S(1)}, u32[]{:S(2)}, u32[]{:S(2)}) collective-permute-start(bf16[1,2,48,768]{3,2,1,0:T(8,128)(2,1)S(1)} %slice.392), channel_id=1, source_target_pairs={{0,4},{1,5},{2,6},{3,7},{4,0},{5,1},{6,2},{7,3},{8,12},{9,13},{10,... | collective-permute-start | bytes 442376 | tf_op jit(solution)/shard_map/ppermute | solution.py:69
  169.4 8.0 %collective-permute-start.51 = (bf16[4,48,768]{2,1,0:T(8,128)(2,1)S(1)}, bf16[4,48,768]{2,1,0:T(8,128)(2,1)S(1)}, u32[]{:S(2)}, u32[]{:S(2)}) collective-permute-start(bf16[4,48,768]{2,1,0:T(8,128)(2,1)S(1)} %fusion.19), channel_id=1, source_target_pairs={{0,1},{1,0},{2,3},{3,2},{4,5},{5,4},{6,7},{7,6},{8,9},{9,8},{10,11... | collective-permute-start | bytes 884744 | tf_op jit(solution)/shard_map/ppermute | solution.py:69
  170.5 7.7 %collective-permute-start.52 = (bf16[4,48,768]{2,1,0:T(8,128)(2,1)S(1)}, bf16[4,48,768]{2,1,0:T(8,128)(2,1)S(1)}, u32[]{:S(2)}, u32[]{:S(2)}) collective-permute-start(bf16[4,48,768]{2,1,0:T(8,128)(2,1)S(1)} %fusion.18), channel_id=1, source_target_pairs={{0,16},{8,24},{16,0},{24,8},{1,17},{9,25},{17,1},{25,9},{2,18},{10... | collective-permute-start | bytes 884744 | tf_op jit(solution)/shard_map/ppermute | solution.py:69
  178.7 6.8 %collective-permute-start.54 = (bf16[2,2,48,768]{3,2,0,1:T(8,128)(2,1)S(1)}, bf16[2,2,48,768]{3,2,0,1:T(8,128)(2,1)S(1)}, u32[]{:S(2)}, u32[]{:S(2)}) collective-permute-start(bf16[2,2,48,768]{3,2,0,1:T(8,128)(2,1)S(1)} %fusion.12), channel_id=1, source_target_pairs={{0,2},{1,3},{2,0},{3,1},{4,6},{5,7},{6,4},{7,5},{8,10},{9,11},{10,... | collective-permute-start | bytes 884744 | tf_op jit(solution)/shard_map/ppermute | solution.py:69
  179.4 15.8 %collective-permute-start.58 = (bf16[2,2,48,768]{3,2,1,0:T(8,128)(2,1)S(1)}, bf16[2,2,48,768]{3,2,1,0:T(8,128)(2,1)S(1)}, u32[]{:S(2)}, u32[]{:S(2)}) collective-permute-start(bf16[2,2,48,768]{3,2,1,0:T(8,128)(2,1)S(1)} %pad_maximum_fusion.19.p0), channel_id=1, source_target_pairs={{0,8},{8,0},{16,24},{24,16},{1,9},{9,1},{17,25},{25,17},{2,10},{10... | collective-permute-start | bytes 884744 | tf_op jit(solution)/shard_map/ppermute | solution.py:69
  179.5 9.4 %collective-permute-start.59 = (bf16[2,2,48,768]{3,2,1,0:T(8,128)(2,1)S(1)}, bf16[2,2,48,768]{3,2,1,0:T(8,128)(2,1)S(1)}, u32[]{:S(2)}, u32[]{:S(2)}) collective-permute-start(bf16[2,2,48,768]{3,2,1,0:T(8,128)(2,1)S(1)} %pad_maximum_fusion.19.p0), channel_id=1, source_target_pairs={{0,16},{8,24},{16,0},{24,8},{1,17},{9,25},{17,1},{25,9},{2,18},{10... | collective-permute-start | bytes 884744 | tf_op jit(solution)/shard_map/ppermute | solution.py:69
  190.7 10.1 %collective-permute-start.56 = (bf16[1,2,48,768]{3,2,0,1:T(8,128)(2,1)S(1)}, bf16[1,2,48,768]{3,2,0,1:T(8,128)(2,1)S(1)}, u32[]{:S(2)}, u32[]{:S(2)}) collective-permute-start(bf16[1,2,48,768]{3,2,0,1:T(8,128)(2,1)S(1)} %slice.405), channel_id=1, source_target_pairs={{0,4},{1,5},{2,6},{3,7},{4,0},{5,1},{6,2},{7,3},{8,12},{9,13},{10,... | collective-permute-start | bytes 442376 | tf_op jit(solution)/shard_map/ppermute | solution.py:69
  193.6 8.4 %collective-permute-start.55 = (bf16[16,768]{1,0:T(8,128)(2,1)S(1)}, bf16[16,768]{1,0:T(8,128)(2,1)S(1)}, u32[]{:S(2)}, u32[]{:S(2)}) collective-permute-start(bf16[16,768]{1,0:T(8,128)(2,1)S(1)} %fusion.37), channel_id=1, source_target_pairs={{0,2},{1,3},{2,0},{3,1},{4,6},{5,7},{6,4},{7,5},{8,10},{9,11},{10,... | collective-permute-start | bytes 73736 | tf_op jit(solution)/shard_map/ppermute | solution.py:69
  (32 other events, 259.6 us)
